TPU v7x, 32 devices: a whole 2x2x4 slice. The times are simulated.
32 devices in a mesh: row: 8 (over y, x, core), col: 4 (over z).
Axes of the slice: x: 2, y: 2, z: 4, core: 2. Of those that a mesh axis runs over, the one named last changes fastest.
Arguments:
- points_here: float32 [4, 3, 32, 64, 128], P(None, None, 'row', 'col'), may hold values from -4 to 4
- points_there: float32 [4, 3, 32, 64, 128], P(None, None, 'row', 'col'), may hold values from -4 to 4
- outlier_mask: int32 [4, 32, 64, 128], P(None, 'row', 'col'), may hold values 0 or 1
- transforms: float32 [3, 4, 32, 64], P(None, None, 'row', 'col'), may hold values from -3 to 3
Outputs:
- aligned: float32 [3, 4, 32, 64], P(None, None, 'row', 'col')
- error_stats: float32 [2, 2], replicated
All inputs are finite; a program needn't handle non-finite values. No bound on the sum of `outlier_mask` on one device may be relied on, other than what follows from the above.
Results may differ from a plain program's by a relative error of at most 0.0003.
Values sent between devices are 32-bit elements; how exact they have to be, the bound alone decides.
No kernel may reach another device: no remote copies, remote signals or barrier semaphores. Data moves between devices by JAX's collectives and lax.ppermute only.
A program may use at most 64 MiB of HBM per device.

v0:
```python
import jax
import jax.numpy as jnp
from jax import lax
from jax.sharding import PartitionSpec as P

ITERS = 2


link_offsets = ((0, 1), (1, 0), (1, 1), (1, -1))
damping_scale = 64.0


def from_behind(array, axis, by):
    peers = lax.axis_size(axis)
    pairs = [(i, i + by) for i in range(peers) if 0 <= i + by < peers]
    return lax.ppermute(array, axis, pairs)


def with_halo(block, sides, width):
    for axis, dim in sides:
        count = lax.axis_size(axis)
        forward = [(i, i + 1) for i in range(count - 1)]
        backward = [(target, source) for source, target in forward]
        low = lax.ppermute(
            lax.slice_in_dim(block, block.shape[dim] - width, None, axis=dim), axis, forward
        )
        high = lax.ppermute(lax.slice_in_dim(block, 0, width, axis=dim), axis, backward)
        block = jnp.concatenate([low, block, high], axis=dim)
    return block


def apply_affine(affine, points):
    mapped = []
    for component in range(3):
        value = affine[component, 3][..., None] + affine[component, 0][..., None] * points[0]
        value = value + affine[component, 1][..., None] * points[1]
        value = value + affine[component, 2][..., None] * points[2]
        mapped.append(value)
    return jnp.stack(mapped)


def link_error(here, there):
    delta = here - there
    return delta[0] * delta[0] + delta[1] * delta[1] + delta[2] * delta[2]


def gram_terms(weight, points):
    weighted = [weight * points[0], weight * points[1], weight * points[2], weight]
    entries = []
    for first in range(4):
        for second in range(4):
            if second == 3:
                entries.append(jnp.sum(weighted[first], axis=-1))
            else:
                entries.append(jnp.sum(weighted[first] * points[second], axis=-1))
    return jnp.stack(entries).reshape((4, 4) + weight.shape[:-1])


def cross_terms(weight, target, points):
    entries = []
    for component in range(3):
        scaled = weight * target[component]
        for second in range(4):
            if second == 3:
                entries.append(jnp.sum(scaled, axis=-1))
            else:
                entries.append(jnp.sum(scaled * points[second], axis=-1))
    return jnp.stack(entries).reshape((3, 4) + weight.shape[:-1])


def solve_small(gram, rhs):
    factor = [[None] * 4 for _ in range(4)]
    for first in range(4):
        for second in range(first + 1):
            value = gram[first, second]
            for inner in range(second):
                value = value - factor[first][inner] * factor[second][inner]
            if first == second:
                factor[first][first] = jnp.sqrt(value)
            else:
                factor[first][second] = value / factor[second][second]
    result = []
    for component in range(3):
        forward = []
        for first in range(4):
            value = rhs[component, first]
            for inner in range(first):
                value = value - factor[first][inner] * forward[inner]
            forward.append(value / factor[first][first])
        backward = [None] * 4
        for first in (3, 2, 1, 0):
            value = forward[first]
            for inner in range(first + 1, 4):
                value = value - factor[inner][first] * backward[inner]
            backward[first] = value / factor[first][first]
        result.append(jnp.stack(backward))
    return jnp.stack(result)


def move_blocks(packages):
    east_pair = jnp.stack([packages[0], packages[2]])
    arrived_east = from_behind(east_pair[:, :, :, -1:], "col", 1)
    east_pair = jnp.concatenate([arrived_east, east_pair[:, :, :, :-1]], axis=3)
    west_one = packages[3]
    arrived_west = from_behind(west_one[:, :, :1], "col", -1)
    west_one = jnp.concatenate([west_one[:, :, 1:], arrived_west], axis=2)
    south_set = jnp.stack([packages[1], east_pair[1], west_one])
    arrived_south = from_behind(south_set[:, :, -1:], "row", 1)
    south_set = jnp.concatenate([arrived_south, south_set[:, :, :-1]], axis=2)
    return [east_pair[0], south_set[0], south_set[1], south_set[2]]


def on_device(points_here, points_there, outlier_mask, transforms):
    rows_local = transforms.shape[2]
    cols_local = transforms.shape[3]
    grid_rows = rows_local * lax.axis_size("row")
    grid_cols = cols_local * lax.axis_size("col")
    row_ids = lax.axis_index("row") * rows_local + jnp.arange(rows_local, dtype=jnp.int32)
    col_ids = lax.axis_index("col") * cols_local + jnp.arange(cols_local, dtype=jnp.int32)
    weight_masks = []
    for direction in range(4):
        row_step, col_step = link_offsets[direction]
        row_valid = row_ids + row_step < grid_rows
        col_valid = (col_ids + col_step >= 0) & (col_ids + col_step < grid_cols)
        valid = (row_valid[:, None] & col_valid[None, :]).astype(jnp.float32)
        weight_masks.append(outlier_mask[direction].astype(jnp.float32) * valid[..., None])
    affine = transforms
    records = []
    for iteration in range(ITERS):
        side_ext = with_halo(affine, (("col", 3),), 1)
        below = from_behind(side_ext[:, :, :1], "row", -1)
        extended = jnp.concatenate([side_ext, below], axis=2)
        mapped_here = []
        mapped_there = []
        errors = []
        largest_local = jnp.zeros((), jnp.float32)
        total_local = jnp.zeros((), jnp.float32)
        count_local = jnp.zeros((), jnp.float32)
        for direction in range(4):
            row_step, col_step = link_offsets[direction]
            target = extended[
                :, :, row_step : row_step + rows_local, 1 + col_step : 1 + col_step + cols_local
            ]
            here = apply_affine(affine, points_here[direction])
            there = apply_affine(target, points_there[direction])
            error = link_error(here, there)
            masked = weight_masks[direction] * error
            largest_local = jnp.maximum(largest_local, jnp.max(masked))
            total_local = total_local + jnp.sum(masked)
            count_local = count_local + jnp.sum(weight_masks[direction])
            mapped_here.append(here)
            mapped_there.append(there)
            errors.append(error)
        largest = lax.pmax(largest_local, ("row", "col"))
        total, count = lax.psum((total_local, count_local), ("row", "col"))
        mean_error = total / jnp.maximum(count, 1.0)
        scale = 0.25 * largest + 1e-06
        damping = damping_scale * mean_error + 1.0
        gram = jnp.zeros((4, 4, rows_local, cols_local), jnp.float32)
        cross = jnp.zeros((3, 4, rows_local, cols_local), jnp.float32)
        packages = []
        for direction in range(4):
            weight = weight_masks[direction] / (1.0 + errors[direction] / scale)
            gram = gram + gram_terms(weight, points_here[direction])
            cross = cross + cross_terms(weight, mapped_there[direction], points_here[direction])
            far_gram = gram_terms(weight, points_there[direction]).reshape(
                (16, rows_local, cols_local)
            )
            far_cross = cross_terms(
                weight, mapped_here[direction], points_there[direction]
            ).reshape((12, rows_local, cols_local))
            packages.append(jnp.concatenate([far_gram, far_cross], axis=0))
        arrived = move_blocks(packages)
        for package in arrived:
            gram = gram + package[:16].reshape((4, 4, rows_local, cols_local))
            cross = cross + package[16:].reshape((3, 4, rows_local, cols_local))
        identity = jnp.eye(4, dtype=jnp.float32)[:, :, None, None]
        affine = solve_small(gram + damping * identity, cross + damping * affine)
        records.append(jnp.stack([largest, mean_error]))
    return (affine, jnp.stack(records, axis=1))


def solution(mesh):
    return jax.shard_map(
        on_device,
        mesh=mesh,
        in_specs=(
            P(None, None, "row", "col", None),
            P(None, None, "row", "col", None),
            P(None, "row", "col", None),
            P(None, None, "row", "col"),
        ),
        out_specs=(P(None, None, "row", "col"), P()),
        check_vma=False,
    )
```

profile of v0, /device:TPU:20, one launch (start us, length us, event | category | flops | bytes accessed | tf_op | source)
XLA Modules:
  0.0 255.7 jit_solution(17610199159023931294)
XLA Ops:
  0.6 0.9 fusion.869
  1.6 2.5 collective-permute-start
  4.0 3.5 %collective-permute-start.1 = (f32[3,4,4,1]{3,2,1,0:T(4,128)S(1)}, f32[3,4,4,1]{3,2,1,0:T(4,128)S(1)}, u32[]{:S(2)}, u32[]{:S(2)}) collective-permute-start(f32[3,4,4,1]{3,2,1,0:T(4,128)S(1)} %get-tuple-element.921), channel_id=1, source_target_pairs={{0,1},{1,2},{2,3},{4,5},{5,6},{6,7},{8,9},{9,10},{10,11},{12,13},{... | collective-permute-start | bytes 584 | tf_op jit(solution)/shard_map/ppermute | solution.py:24
  7.7 2.1 collective-permute-done.1
  9.9 1.9 collective-permute-start.2
  11.9 1.0 fusion.525
  20.1 41.2 %pmax.14 = f32[]{:T(128)} all-reduce(f32[]{:T(128)S(6)} %max.35), channel_id=1, replica_groups=mesh['row'=8,'col'=4] {'row','col'}, use_global_device_ids=true, to_apply=%region_4.0 | all-reduce | flops 1 | bytes 8 | tf_op jit(solution)/shard_map/pmax | solution.py:154
  66.8 2.3 collective-permute-start.3
  75.4 3.5 %collective-permute-start.4 = (f32[28,4,1]{2,1,0:T(4,128)S(1)}, f32[28,4,1]{2,1,0:T(4,128)S(1)}, u32[]{:S(2)}, u32[]{:S(2)}) collective-permute-start(f32[28,4,1]{2,1,0:T(4,128)S(1)} %bitcast.4424), channel_id=1, source_target_pairs={{1,0},{2,1},{3,2},{5,4},{6,5},{7,6},{9,8},{10,9},{11,10},{13,12},{... | collective-permute-start | bytes 1352 | tf_op jit(solution)/shard_map/ppermute | solution.py:16
  78.9 39.2 %all-reduce = (f32[]{:T(128)}, f32[]{:T(128)}) all-reduce(f32[]{:T(128)S(6)} %add.2610, f32[]{:T(128)S(6)} %add.2613), channel_id=1, replica_groups=mesh['row'=8,'col'=4] {'row','col'}, use_global_device_ids=true, to_apply=%region_157.0 | all-reduce | flops 2 | bytes 16 | tf_op jit(solution)/shard_map/psum | solution.py:155
  121.1 1.9 collective-permute-start.5
  123.2 4.1 %collective-permute-done.5 = f32[3,28,1,16]{3,2,1,0:T(1,128)S(1)} collective-permute-done((f32[3,28,1,16]{3,2,1,0:T(1,128)S(1)}, f32[3,28,1,16]{3,2,1,0:T(1,128)S(1)}, u32[]{:S(2)}, u32[]{:S(2)}) %collective-permute-start.5) | collective-permute-done | bytes 5408 | tf_op jit(solution)/shard_map/ppermute | solution.py:16
  127.9 2.6 collective-permute-start.6
  130.4 3.3 %collective-permute-start.7 = (f32[3,4,4,1]{3,2,1,0:T(4,128)S(1)}, f32[3,4,4,1]{3,2,1,0:T(4,128)S(1)}, u32[]{:S(2)}, u32[]{:S(2)}) collective-permute-start(f32[3,4,4,1]{3,2,1,0:T(4,128)S(1)} %get-tuple-element.908), channel_id=1, source_target_pairs={{0,1},{1,2},{2,3},{4,5},{5,6},{6,7},{8,9},{9,10},{10,11},{12,13},{... | collective-permute-start | bytes 584 | tf_op jit(solution)/shard_map/ppermute | solution.py:24
  134.1 2.1 collective-permute-done.7
  136.3 1.9 collective-permute-start.8
  138.4 1.2 collective-permute-done.8
  144.6 41.1 %pmax.15 = f32[]{:T(128)} all-reduce(f32[]{:T(128)S(6)} %max.40), channel_id=1, replica_groups=mesh['row'=8,'col'=4] {'row','col'}, use_global_device_ids=true, to_apply=%region_215.0 | all-reduce | flops 1 | bytes 8 | tf_op jit(solution)/shard_map/pmax | solution.py:154
  191.7 39.6 %psum.26 = f32[]{:T(128)} all-reduce(f32[]{:T(128)S(6)} %add.2842), channel_id=1, replica_groups=mesh['row'=8,'col'=4] {'row','col'}, use_global_device_ids=true, to_apply=%region_368.0 | all-reduce | flops 1 | bytes 8 | tf_op jit(solution)/shard_map/psum | solution.py:155
  235.3 3.3 %collective-permute-start.10 = (f32[28,4,1]{2,1,0:T(4,128)S(1)}, f32[28,4,1]{2,1,0:T(4,128)S(1)}, u32[]{:S(2)}, u32[]{:S(2)}) collective-permute-start(f32[28,4,1]{2,1,0:T(4,128)S(1)} %bitcast.4425), channel_id=1, source_target_pairs={{1,0},{2,1},{3,2},{5,4},{6,5},{7,6},{9,8},{10,9},{11,10},{13,12},{... | collective-permute-start | bytes 1352 | tf_op jit(solution)/shard_map/ppermute | solution.py:16
  241.5 2.5 collective-permute-start.9
  244.1 4.0 %collective-permute-done.9 = f32[2,28,4,1]{3,2,1,0:T(4,128)S(1)} collective-permute-done((f32[2,28,4,1]{3,2,1,0:T(4,128)S(1)}, f32[2,28,4,1]{3,2,1,0:T(4,128)S(1)}, u32[]{:S(2)}, u32[]{:S(2)}) %collective-permute-start.9) | collective-permute-done | bytes 928 | tf_op jit(solution)/shard_map/ppermute | solution.py:16
  248.3 1.9 collective-permute-start.11
  250.4 4.1 %collective-permute-done.11 = f32[3,28,1,16]{3,2,1,0:T(1,128)S(1)} collective-permute-done((f32[3,28,1,16]{3,2,1,0:T(1,128)S(1)}, f32[3,28,1,16]{3,2,1,0:T(1,128)S(1)}, u32[]{:S(2)}, u32[]{:S(2)}) %collective-permute-start.11) | collective-permute-done | bytes 5408 | tf_op jit(solution)/shard_map/ppermute | solution.py:16
  (588 shorter events, 25.1 us)
Async XLA Ops:
  0.6 7.0 %copy-start.3 = (f32[3,4,4,16]{3,2,1,0:T(4,128)S(1)}, f32[3,4,4,16]{3,2,1,0:T(4,128)}, u32[]{:S(2)}) copy-start(f32[3,4,4,16]{3,2,1,0:T(4,128)} %param.7) | copy-start | bytes 9220
  1.6 11.4 %copy-start = (f32[4,3,4,16,128]{4,3,2,1,0:T(8,128)S(1)}, f32[4,3,4,16,128]{4,3,2,1,0:T(8,128)}, u32[]{:S(2)}) copy-start(f32[4,3,4,16,128]{4,3,2,1,0:T(8,128)} %param.4) | copy-start | bytes 1179652
  1.6 6.1 %collective-permute-start = (f32[3,4,4,1]{3,2,1,0:T(4,128)S(1)}, f32[3,4,4,1]{3,2,1,0:T(4,128)S(1)}, u32[]{:S(2)}, u32[]{:S(2)}) collective-permute-start(f32[3,4,4,1]{3,2,1,0:T(4,128)S(1)} %get-tuple-element.922), channel_id=1, source_target_pairs={{1,0},{2,1},{3,2},{5,4},{6,5},{7,6},{9,8},{10,9},{11,10},{13,12},{... | collective-permute-start | bytes 584 | tf_op jit(solution)/shard_map/ppermute | solution.py:27
  4.0 5.7 %collective-permute-start.1 = (f32[3,4,4,1]{3,2,1,0:T(4,128)S(1)}, f32[3,4,4,1]{3,2,1,0:T(4,128)S(1)}, u32[]{:S(2)}, u32[]{:S(2)}) collective-permute-start(f32[3,4,4,1]{3,2,1,0:T(4,128)S(1)} %get-tuple-element.921), channel_id=1, source_target_pairs={{0,1},{1,2},{2,3},{4,5},{5,6},{6,7},{8,9},{9,10},{10,11},{12,13},{... | collective-permute-start | bytes 584 | tf_op jit(solution)/shard_map/ppermute | solution.py:24
  9.9 3.5 %collective-permute-start.2 = (f32[3,4,1,18]{3,2,1,0:T(1,128)S(1)}, f32[3,4,1,18]{3,2,1,0:T(1,128)S(1)}, u32[]{:S(2)}, u32[]{:S(2)}) collective-permute-start(f32[3,4,1,18]{3,2,1,0:T(1,128)S(1)} %pad_maximum_fusion.33), channel_id=1, source_target_pairs={{4,0},{8,4},{12,8},{16,12},{20,16},{24,20},{28,24},{5,1},{9,5},{13... | collective-permute-start | bytes 2600 | tf_op jit(solution)/shard_map/ppermute | solution.py:16
  13.2 1.0 copy-start.1
  15.1 0.9 copy-start.2
  66.8 54.1 %collective-permute-start.3 = (f32[2,28,4,1]{3,2,1,0:T(4,128)S(1)}, f32[2,28,4,1]{3,2,1,0:T(4,128)S(1)}, u32[]{:S(2)}, u32[]{:S(2)}) collective-permute-start(f32[2,28,4,1]{3,2,1,0:T(4,128)S(1)} %slice_maximum_fusion.1), channel_id=1, source_target_pairs={{0,1},{1,2},{2,3},{4,5},{5,6},{6,7},{8,9},{9,10},{10,11},{12,13},{... | collective-permute-start | bytes 2696 | tf_op jit(solution)/shard_map/ppermute | solution.py:16
  75.4 45.3 %collective-permute-start.4 = (f32[28,4,1]{2,1,0:T(4,128)S(1)}, f32[28,4,1]{2,1,0:T(4,128)S(1)}, u32[]{:S(2)}, u32[]{:S(2)}) collective-permute-start(f32[28,4,1]{2,1,0:T(4,128)S(1)} %bitcast.4424), channel_id=1, source_target_pairs={{1,0},{2,1},{3,2},{5,4},{6,5},{7,6},{9,8},{10,9},{11,10},{13,12},{... | collective-permute-start | bytes 1352 | tf_op jit(solution)/shard_map/ppermute | solution.py:16
  121.1 6.2 %collective-permute-start.5 = (f32[3,28,1,16]{3,2,1,0:T(1,128)S(1)}, f32[3,28,1,16]{3,2,1,0:T(1,128)S(1)}, u32[]{:S(2)}, u32[]{:S(2)}) collective-permute-start(f32[3,28,1,16]{3,2,1,0:T(1,128)S(1)} %pad_maximum_fusion.5), channel_id=1, source_target_pairs={{0,4},{4,8},{8,12},{12,16},{16,20},{20,24},{24,28},{1,5},{5,9},{9,... | collective-permute-start | bytes 16136 | tf_op jit(solution)/shard_map/ppermute | solution.py:16
  127.9 6.2 %collective-permute-start.6 = (f32[3,4,4,1]{3,2,1,0:T(4,128)S(1)}, f32[3,4,4,1]{3,2,1,0:T(4,128)S(1)}, u32[]{:S(2)}, u32[]{:S(2)}) collective-permute-start(f32[3,4,4,1]{3,2,1,0:T(4,128)S(1)} %get-tuple-element.909), channel_id=1, source_target_pairs={{1,0},{2,1},{3,2},{5,4},{6,5},{7,6},{9,8},{10,9},{11,10},{13,12},{... | collective-permute-start | bytes 584 | tf_op jit(solution)/shard_map/ppermute | solution.py:27
  130.4 5.7 %collective-permute-start.7 = (f32[3,4,4,1]{3,2,1,0:T(4,128)S(1)}, f32[3,4,4,1]{3,2,1,0:T(4,128)S(1)}, u32[]{:S(2)}, u32[]{:S(2)}) collective-permute-start(f32[3,4,4,1]{3,2,1,0:T(4,128)S(1)} %get-tuple-element.908), channel_id=1, source_target_pairs={{0,1},{1,2},{2,3},{4,5},{5,6},{6,7},{8,9},{9,10},{10,11},{12,13},{... | collective-permute-start | bytes 584 | tf_op jit(solution)/shard_map/ppermute | solution.py:24
  136.3 3.3 %collective-permute-start.8 = (f32[3,4,1,18]{3,2,1,0:T(1,128)S(1)}, f32[3,4,1,18]{3,2,1,0:T(1,128)S(1)}, u32[]{:S(2)}, u32[]{:S(2)}) collective-permute-start(f32[3,4,1,18]{3,2,1,0:T(1,128)S(1)} %pad_maximum_fusion.29), channel_id=1, source_target_pairs={{4,0},{8,4},{12,8},{16,12},{20,16},{24,20},{28,24},{5,1},{9,5},{13... | collective-permute-start | bytes 2600 | tf_op jit(solution)/shard_map/ppermute | solution.py:16
  235.3 8.7 %collective-permute-start.10 = (f32[28,4,1]{2,1,0:T(4,128)S(1)}, f32[28,4,1]{2,1,0:T(4,128)S(1)}, u32[]{:S(2)}, u32[]{:S(2)}) collective-permute-start(f32[28,4,1]{2,1,0:T(4,128)S(1)} %bitcast.4425), channel_id=1, source_target_pairs={{1,0},{2,1},{3,2},{5,4},{6,5},{7,6},{9,8},{10,9},{11,10},{13,12},{... | collective-permute-start | bytes 1352 | tf_op jit(solution)/shard_map/ppermute | solution.py:16
  241.5 6.7 %collective-permute-start.9 = (f32[2,28,4,1]{3,2,1,0:T(4,128)S(1)}, f32[2,28,4,1]{3,2,1,0:T(4,128)S(1)}, u32[]{:S(2)}, u32[]{:S(2)}) collective-permute-start(f32[2,28,4,1]{3,2,1,0:T(4,128)S(1)} %slice_maximum_fusion), channel_id=1, source_target_pairs={{0,1},{1,2},{2,3},{4,5},{5,6},{6,7},{8,9},{9,10},{10,11},{12,13},{... | collective-permute-start | bytes 2696 | tf_op jit(solution)/shard_map/ppermute | solution.py:16
  248.3 6.2 %collective-permute-start.11 = (f32[3,28,1,16]{3,2,1,0:T(1,128)S(1)}, f32[3,28,1,16]{3,2,1,0:T(1,128)S(1)}, u32[]{:S(2)}, u32[]{:S(2)}) collective-permute-start(f32[3,28,1,16]{3,2,1,0:T(1,128)S(1)} %pad_maximum_fusion.4), channel_id=1, source_target_pairs={{0,4},{4,8},{8,12},{12,16},{16,20},{20,24},{24,28},{1,5},{5,9},{9,... | collective-permute-start | bytes 16136 | tf_op jit(solution)/shard_map/ppermute | solution.py:16
where the time goes:
time: 257 us; the launch traced here: 256 us
  blocking collectives  161 us (63%)
  starting transfers between devices  31.2 us (12%)
  other arithmetic  19.6 us (8%)
  between operations  18.7 us (7%)
  waiting for transfers between devices  17.6 us (7%)
  local copies, waits for them, and re-layouts  7.5 us (3%)
    pmax x2, blocking collectives, on_device(): largest = lax.pmax(largest_local, ('row', 'col'))  82.3 us
    psum x2, blocking collectives, on_device(): total, count = lax.psum((total_local, count_local), ('row', 'col'))  78.7 us
    ppermute x8, starting transfers between devices, from_behind(): return lax.ppermute(array, axis, pairs)  19.4 us
    ppermute x8, waiting for transfers between devices, from_behind(): return lax.ppermute(array, axis, pairs)  13.5 us
    ppermute x2, starting transfers between devices, with_halo(): lax.ppermute(lax.slice_in_dim(block, block.shape[dim] - width, None, axis...  6.76 us
    unnamed x425, local copies, waits for them, and re-layouts  5.69 us
  transfers between devices with their start and end apart: 12, of which 6 were waited for; matrix products, arithmetic and copies ran while one was open for 3% of the time, Pallas kernels for 0%

commit v1 on v0

--- a/solution.py
+++ b/solution.py
@@ -14,6 +14,14 @@
     peers = lax.axis_size(axis)
     pairs = [(i, i + by) for i in range(peers) if 0 <= i + by < peers]
     return lax.ppermute(array, axis, pairs)
+
+
+def over_devices(largest, total, count):
+    devices = lax.axis_size("row") * lax.axis_size("col")
+    mine = jnp.stack([largest, total, count])
+    sent = jnp.broadcast_to(jnp.pad(mine, (0, 125))[None], (devices, 128))
+    got = lax.all_to_all(sent, ("row", "col"), 0, 0)
+    return jnp.max(got[:, 0]), jnp.sum(got[:, 1]), jnp.sum(got[:, 2])
 
 
 def with_halo(block, sides, width):
@@ -151,8 +159,7 @@
             mapped_here.append(here)
             mapped_there.append(there)
             errors.append(error)
-        largest = lax.pmax(largest_local, ("row", "col"))
-        total, count = lax.psum((total_local, count_local), ("row", "col"))
+        largest, total, count = over_devices(largest_local, total_local, count_local)
         mean_error = total / jnp.maximum(count, 1.0)
         scale = 0.25 * largest + 1e-06
         damping = damping_scale * mean_error + 1.0

time: 257 us -> 119 us (0.46)
  blocking collectives: 161 us -> 9.97 us
  starting transfers between devices: 31.2 us -> 36.3 us
  waiting for transfers between devices: 17.6 us -> 22.1 us
    pmax x2 -> x0, blocking collectives: 82.3 us -> none  [on_device(): largest = lax.pmax(largest_local, ('row', 'col'))]
    psum x2 -> x0, blocking collectives: 78.7 us -> none  [on_device(): total, count = lax.psum((total_local, count_local), ('row', 'col'))]
    all_to_all x0 -> x1, blocking collectives: none -> 9.97 us  [over_devices(): got = lax.all_to_all(sent, ('row', 'col'), 0, 0)]
    all_to_all x0 -> x1, starting transfers between devices: none -> 5.1 us  [over_devices(): got = lax.all_to_all(sent, ('row', 'col'), 0, 0)]
    all_to_all x0 -> x1, waiting for transfers between devices: none -> 3.46 us  [over_devices(): got = lax.all_to_all(sent, ('row', 'col'), 0, 0)]
  transfers between devices with their start and end apart: 12 -> 13, of which waited for: 6 -> 8; matrix products, arithmetic and copies ran while one was open for 3% -> 7% of each run, Pallas kernels for 0% -> 0%
where the time goes in v1:
time: 119 us; the launch traced here: 117 us
  starting transfers between devices  36.3 us (31%)
  waiting for transfers between devices  22.1 us (19%)
  other arithmetic  21.1 us (18%)
  between operations  19.3 us (16%)
  blocking collectives  9.97 us (8%)
  local copies, waits for them, and re-layouts  8.15 us (7%)
    ppermute x8, starting transfers between devices, from_behind(): return lax.ppermute(array, axis, pairs)  19.4 us
    ppermute x8, waiting for transfers between devices, from_behind(): return lax.ppermute(array, axis, pairs)  13.6 us
    all_to_all x1, blocking collectives, over_devices(): got = lax.all_to_all(sent, ('row', 'col'), 0, 0)  9.97 us
    ppermute x2, starting transfers between devices, with_halo(): lax.ppermute(lax.slice_in_dim(block, block.shape[dim] - width, None, axis...  5.93 us
    ppermute x2, starting transfers between devices, with_halo(): lax.ppermute(lax.slice_in_dim(block, 0, width, axis=dim), axis, backward)  5.87 us
    unnamed x425, local copies, waits for them, and re-layouts  5.69 us
    all_to_all x1, starting transfers between devices, over_devices(): got = lax.all_to_all(sent, ('row', 'col'), 0, 0)  5.1 us
    ppermute x2, waiting for transfers between devices, with_halo(): lax.ppermute(lax.slice_in_dim(block, block.shape[dim] - width, None, axis...  5.01 us
  transfers between devices with their start and end apart: 13, of which 8 were waited for; matrix products, arithmetic and copies ran while one was open for 7% of the time, Pallas kernels for 0%

profile of v1, /device:TPU:20, one launch (start us, length us, event | category | flops | bytes accessed | tf_op | source)
XLA Modules:
  0.0 116.9 jit_solution(9431133484623327857)
XLA Ops:
  0.6 0.9 fusion.869
  1.6 2.5 %collective-permute-start = (f32[3,4,4,1]{3,2,1,0:T(4,128)S(1)}, f32[3,4,4,1]{3,2,1,0:T(4,128)S(1)}, u32[]{:S(2)}, u32[]{:S(2)}) collective-permute-start(f32[3,4,4,1]{3,2,1,0:T(4,128)S(1)} %get-tuple-element.930), channel_id=1, source_target_pairs={{1,0},{2,1},{3,2},{5,4},{6,5},{7,6},{9,8},{10,9},{11,10},{13,12},{... | collective-permute-start | bytes 584 | tf_op jit(solution)/shard_map/ppermute | solution.py:35
  4.0 3.5 %collective-permute-start.1 = (f32[3,4,4,1]{3,2,1,0:T(4,128)S(1)}, f32[3,4,4,1]{3,2,1,0:T(4,128)S(1)}, u32[]{:S(2)}, u32[]{:S(2)}) collective-permute-start(f32[3,4,4,1]{3,2,1,0:T(4,128)S(1)} %get-tuple-element.929), channel_id=1, source_target_pairs={{0,1},{1,2},{2,3},{4,5},{5,6},{6,7},{8,9},{9,10},{10,11},{12,13},{... | collective-permute-start | bytes 584 | tf_op jit(solution)/shard_map/ppermute | solution.py:32
  7.7 2.1 %collective-permute-done.1 = f32[3,4,4,1]{3,2,1,0:T(4,128)S(1)} collective-permute-done((f32[3,4,4,1]{3,2,1,0:T(4,128)S(1)}, f32[3,4,4,1]{3,2,1,0:T(4,128)S(1)}, u32[]{:S(2)}, u32[]{:S(2)}) %collective-permute-start.1) | collective-permute-done | bytes 224 | tf_op jit(solution)/shard_map/ppermute | solution.py:32
  9.9 1.9 %collective-permute-start.2 = (f32[3,4,1,18]{3,2,1,0:T(1,128)S(1)}, f32[3,4,1,18]{3,2,1,0:T(1,128)S(1)}, u32[]{:S(2)}, u32[]{:S(2)}) collective-permute-start(f32[3,4,1,18]{3,2,1,0:T(1,128)S(1)} %pad_maximum_fusion.33), channel_id=1, source_target_pairs={{4,0},{8,4},{12,8},{16,12},{20,16},{24,20},{28,24},{5,1},{9,5},{13... | collective-permute-start | bytes 2600 | tf_op jit(solution)/shard_map/ppermute | solution.py:16
  11.9 1.0 fusion.525
  15.2 0.9 copy-done.2
  25.2 10.0 %all_to_all.18 = f32[32,1,128]{2,1,0:T(1,128)S(1)} all-to-all(f32[32,1,128]{2,1,0:T(1,128)S(1)} %broadcast_in_dim.4), channel_id=1, replica_groups=mesh['row'=8,'col'=4] {'row','col'}, dimensions={0} | all-to-all | bytes 32768 | tf_op jit(solution)/shard_map/all_to_all | solution.py:23
  41.3 2.5 %collective-permute-start.3 = (f32[2,28,4,1]{3,2,1,0:T(4,128)S(1)}, f32[2,28,4,1]{3,2,1,0:T(4,128)S(1)}, u32[]{:S(2)}, u32[]{:S(2)}) collective-permute-start(f32[2,28,4,1]{3,2,1,0:T(4,128)S(1)} %slice_maximum_fusion.1), channel_id=1, source_target_pairs={{0,1},{1,2},{2,3},{4,5},{5,6},{6,7},{8,9},{9,10},{10,11},{12,13},{... | collective-permute-start | bytes 2696 | tf_op jit(solution)/shard_map/ppermute | solution.py:16
  45.1 3.4 %collective-permute-start.4 = (f32[28,4,1]{2,1,0:T(4,128)S(1)}, f32[28,4,1]{2,1,0:T(4,128)S(1)}, u32[]{:S(2)}, u32[]{:S(2)}) collective-permute-start(f32[28,4,1]{2,1,0:T(4,128)S(1)} %bitcast.4433), channel_id=1, source_target_pairs={{1,0},{2,1},{3,2},{5,4},{6,5},{7,6},{9,8},{10,9},{11,10},{13,12},{... | collective-permute-start | bytes 1352 | tf_op jit(solution)/shard_map/ppermute | solution.py:16
  51.5 1.9 %collective-permute-start.5 = (f32[3,28,1,16]{3,2,1,0:T(1,128)S(1)}, f32[3,28,1,16]{3,2,1,0:T(1,128)S(1)}, u32[]{:S(2)}, u32[]{:S(2)}) collective-permute-start(f32[3,28,1,16]{3,2,1,0:T(1,128)S(1)} %pad_maximum_fusion.5), channel_id=1, source_target_pairs={{0,4},{4,8},{8,12},{12,16},{16,20},{20,24},{24,28},{1,5},{5,9},{9,... | collective-permute-start | bytes 16136 | tf_op jit(solution)/shard_map/ppermute | solution.py:16
  53.6 4.1 %collective-permute-done.5 = f32[3,28,1,16]{3,2,1,0:T(1,128)S(1)} collective-permute-done((f32[3,28,1,16]{3,2,1,0:T(1,128)S(1)}, f32[3,28,1,16]{3,2,1,0:T(1,128)S(1)}, u32[]{:S(2)}, u32[]{:S(2)}) %collective-permute-start.5) | collective-permute-done | bytes 5408 | tf_op jit(solution)/shard_map/ppermute | solution.py:16
  58.3 3.4 %collective-permute-start.6 = (f32[3,4,4,1]{3,2,1,0:T(4,128)S(1)}, f32[3,4,4,1]{3,2,1,0:T(4,128)S(1)}, u32[]{:S(2)}, u32[]{:S(2)}) collective-permute-start(f32[3,4,4,1]{3,2,1,0:T(4,128)S(1)} %get-tuple-element.905), channel_id=1, source_target_pairs={{1,0},{2,1},{3,2},{5,4},{6,5},{7,6},{9,8},{10,9},{11,10},{13,12},{... | collective-permute-start | bytes 584 | tf_op jit(solution)/shard_map/ppermute | solution.py:35
  61.7 2.4 %collective-permute-start.7 = (f32[3,4,4,1]{3,2,1,0:T(4,128)S(1)}, f32[3,4,4,1]{3,2,1,0:T(4,128)S(1)}, u32[]{:S(2)}, u32[]{:S(2)}) collective-permute-start(f32[3,4,4,1]{3,2,1,0:T(4,128)S(1)} %get-tuple-element.904), channel_id=1, source_target_pairs={{0,1},{1,2},{2,3},{4,5},{5,6},{6,7},{8,9},{9,10},{10,11},{12,13},{... | collective-permute-start | bytes 584 | tf_op jit(solution)/shard_map/ppermute | solution.py:32
  64.5 2.9 %collective-permute-done.7 = f32[3,4,4,1]{3,2,1,0:T(4,128)S(1)} collective-permute-done((f32[3,4,4,1]{3,2,1,0:T(4,128)S(1)}, f32[3,4,4,1]{3,2,1,0:T(4,128)S(1)}, u32[]{:S(2)}, u32[]{:S(2)}) %collective-permute-start.7) | collective-permute-done | bytes 224 | tf_op jit(solution)/shard_map/ppermute | solution.py:32
  67.5 1.9 %collective-permute-start.8 = (f32[3,4,1,18]{3,2,1,0:T(1,128)S(1)}, f32[3,4,1,18]{3,2,1,0:T(1,128)S(1)}, u32[]{:S(2)}, u32[]{:S(2)}) collective-permute-start(f32[3,4,1,18]{3,2,1,0:T(1,128)S(1)} %pad_maximum_fusion.29), channel_id=1, source_target_pairs={{4,0},{8,4},{12,8},{16,12},{20,16},{24,20},{28,24},{5,1},{9,5},{13... | collective-permute-start | bytes 2600 | tf_op jit(solution)/shard_map/ppermute | solution.py:16
  69.6 1.2 collective-permute-done.8
  78.5 5.1 %all-to-all-start.1 = ((f32[32,1,128]{2,1,0:T(1,128)}), f32[32,1,128]{2,1,0:T(1,128)S(1)}, u32[]{:S(2)}, u32[]{:S(2)}) async-start(f32[32,1,128]{2,1,0:T(1,128)} %broadcast_in_dim.5), calls=%async_computation.1 | async-start | bytes 32768 | tf_op jit(solution)/shard_map/all_to_all | solution.py:23
  84.2 3.5 %all-to-all-done.1 = f32[32,1,128]{2,1,0:T(1,128)S(1)} async-done(((f32[32,1,128]{2,1,0:T(1,128)}), f32[32,1,128]{2,1,0:T(1,128)S(1)}, u32[]{:S(2)}, u32[]{:S(2)}) %all-to-all-start.1) | async-done | bytes 16416 | tf_op jit(solution)/shard_map/all_to_all | solution.py:23
  95.7 3.3 %collective-permute-start.10 = (f32[28,4,1]{2,1,0:T(4,128)S(1)}, f32[28,4,1]{2,1,0:T(4,128)S(1)}, u32[]{:S(2)}, u32[]{:S(2)}) collective-permute-start(f32[28,4,1]{2,1,0:T(4,128)S(1)} %bitcast.4434), channel_id=1, source_target_pairs={{1,0},{2,1},{3,2},{5,4},{6,5},{7,6},{9,8},{10,9},{11,10},{13,12},{... | collective-permute-start | bytes 1352 | tf_op jit(solution)/shard_map/ppermute | solution.py:16
  102.7 2.5 %collective-permute-start.9 = (f32[2,28,4,1]{3,2,1,0:T(4,128)S(1)}, f32[2,28,4,1]{3,2,1,0:T(4,128)S(1)}, u32[]{:S(2)}, u32[]{:S(2)}) collective-permute-start(f32[2,28,4,1]{3,2,1,0:T(4,128)S(1)} %slice_maximum_fusion), channel_id=1, source_target_pairs={{0,1},{1,2},{2,3},{4,5},{5,6},{6,7},{8,9},{9,10},{10,11},{12,13},{... | collective-permute-start | bytes 2696 | tf_op jit(solution)/shard_map/ppermute | solution.py:16
  105.3 4.0 %collective-permute-done.9 = f32[2,28,4,1]{3,2,1,0:T(4,128)S(1)} collective-permute-done((f32[2,28,4,1]{3,2,1,0:T(4,128)S(1)}, f32[2,28,4,1]{3,2,1,0:T(4,128)S(1)}, u32[]{:S(2)}, u32[]{:S(2)}) %collective-permute-start.9) | collective-permute-done | bytes 928 | tf_op jit(solution)/shard_map/ppermute | solution.py:16
  109.5 1.9 %collective-permute-start.11 = (f32[3,28,1,16]{3,2,1,0:T(1,128)S(1)}, f32[3,28,1,16]{3,2,1,0:T(1,128)S(1)}, u32[]{:S(2)}, u32[]{:S(2)}) collective-permute-start(f32[3,28,1,16]{3,2,1,0:T(1,128)S(1)} %pad_maximum_fusion.4), channel_id=1, source_target_pairs={{0,4},{4,8},{8,12},{12,16},{16,20},{20,24},{24,28},{1,5},{5,9},{9,... | collective-permute-start | bytes 16136 | tf_op jit(solution)/shard_map/ppermute | solution.py:16
  111.6 4.1 %collective-permute-done.11 = f32[3,28,1,16]{3,2,1,0:T(1,128)S(1)} collective-permute-done((f32[3,28,1,16]{3,2,1,0:T(1,128)S(1)}, f32[3,28,1,16]{3,2,1,0:T(1,128)S(1)}, u32[]{:S(2)}, u32[]{:S(2)}) %collective-permute-start.11) | collective-permute-done | bytes 5408 | tf_op jit(solution)/shard_map/ppermute | solution.py:16
  (595 shorter events, 26.6 us)
Async XLA Ops:
  0.6 7.0 %copy-start.3 = (f32[3,4,4,16]{3,2,1,0:T(4,128)S(1)}, f32[3,4,4,16]{3,2,1,0:T(4,128)}, u32[]{:S(2)}) copy-start(f32[3,4,4,16]{3,2,1,0:T(4,128)} %param.7) | copy-start | bytes 9220
  1.6 11.4 %copy-start = (f32[4,3,4,16,128]{4,3,2,1,0:T(8,128)S(1)}, f32[4,3,4,16,128]{4,3,2,1,0:T(8,128)}, u32[]{:S(2)}) copy-start(f32[4,3,4,16,128]{4,3,2,1,0:T(8,128)} %param.4) | copy-start | bytes 1179652
  1.6 6.1 %collective-permute-start = (f32[3,4,4,1]{3,2,1,0:T(4,128)S(1)}, f32[3,4,4,1]{3,2,1,0:T(4,128)S(1)}, u32[]{:S(2)}, u32[]{:S(2)}) collective-permute-start(f32[3,4,4,1]{3,2,1,0:T(4,128)S(1)} %get-tuple-element.930), channel_id=1, source_target_pairs={{1,0},{2,1},{3,2},{5,4},{6,5},{7,6},{9,8},{10,9},{11,10},{13,12},{... | collective-permute-start | bytes 584 | tf_op jit(solution)/shard_map/ppermute | solution.py:35
  4.0 5.7 %collective-permute-start.1 = (f32[3,4,4,1]{3,2,1,0:T(4,128)S(1)}, f32[3,4,4,1]{3,2,1,0:T(4,128)S(1)}, u32[]{:S(2)}, u32[]{:S(2)}) collective-permute-start(f32[3,4,4,1]{3,2,1,0:T(4,128)S(1)} %get-tuple-element.929), channel_id=1, source_target_pairs={{0,1},{1,2},{2,3},{4,5},{5,6},{6,7},{8,9},{9,10},{10,11},{12,13},{... | collective-permute-start | bytes 584 | tf_op jit(solution)/shard_map/ppermute | solution.py:32
  9.9 3.5 %collective-permute-start.2 = (f32[3,4,1,18]{3,2,1,0:T(1,128)S(1)}, f32[3,4,1,18]{3,2,1,0:T(1,128)S(1)}, u32[]{:S(2)}, u32[]{:S(2)}) collective-permute-start(f32[3,4,1,18]{3,2,1,0:T(1,128)S(1)} %pad_maximum_fusion.33), channel_id=1, source_target_pairs={{4,0},{8,4},{12,8},{16,12},{20,16},{24,20},{28,24},{5,1},{9,5},{13... | collective-permute-start | bytes 2600 | tf_op jit(solution)/shard_map/ppermute | solution.py:16
  13.2 1.0 copy-start.1
  15.1 0.9 copy-start.2
  41.3 10.0 %collective-permute-start.3 = (f32[2,28,4,1]{3,2,1,0:T(4,128)S(1)}, f32[2,28,4,1]{3,2,1,0:T(4,128)S(1)}, u32[]{:S(2)}, u32[]{:S(2)}) collective-permute-start(f32[2,28,4,1]{3,2,1,0:T(4,128)S(1)} %slice_maximum_fusion.1), channel_id=1, source_target_pairs={{0,1},{1,2},{2,3},{4,5},{5,6},{6,7},{8,9},{9,10},{10,11},{12,13},{... | collective-permute-start | bytes 2696 | tf_op jit(solution)/shard_map/ppermute | solution.py:16
  45.1 6.1 %collective-permute-start.4 = (f32[28,4,1]{2,1,0:T(4,128)S(1)}, f32[28,4,1]{2,1,0:T(4,128)S(1)}, u32[]{:S(2)}, u32[]{:S(2)}) collective-permute-start(f32[28,4,1]{2,1,0:T(4,128)S(1)} %bitcast.4433), channel_id=1, source_target_pairs={{1,0},{2,1},{3,2},{5,4},{6,5},{7,6},{9,8},{10,9},{11,10},{13,12},{... | collective-permute-start | bytes 1352 | tf_op jit(solution)/shard_map/ppermute | solution.py:16
  51.5 6.2 %collective-permute-start.5 = (f32[3,28,1,16]{3,2,1,0:T(1,128)S(1)}, f32[3,28,1,16]{3,2,1,0:T(1,128)S(1)}, u32[]{:S(2)}, u32[]{:S(2)}) collective-permute-start(f32[3,28,1,16]{3,2,1,0:T(1,128)S(1)} %pad_maximum_fusion.5), channel_id=1, source_target_pairs={{0,4},{4,8},{8,12},{12,16},{16,20},{20,24},{24,28},{1,5},{5,9},{9,... | collective-permute-start | bytes 16136 | tf_op jit(solution)/shard_map/ppermute | solution.py:16
  58.3 6.2 %collective-permute-start.6 = (f32[3,4,4,1]{3,2,1,0:T(4,128)S(1)}, f32[3,4,4,1]{3,2,1,0:T(4,128)S(1)}, u32[]{:S(2)}, u32[]{:S(2)}) collective-permute-start(f32[3,4,4,1]{3,2,1,0:T(4,128)S(1)} %get-tuple-element.905), channel_id=1, source_target_pairs={{1,0},{2,1},{3,2},{5,4},{6,5},{7,6},{9,8},{10,9},{11,10},{13,12},{... | collective-permute-start | bytes 584 | tf_op jit(solution)/shard_map/ppermute | solution.py:35
  61.7 5.7 %collective-permute-start.7 = (f32[3,4,4,1]{3,2,1,0:T(4,128)S(1)}, f32[3,4,4,1]{3,2,1,0:T(4,128)S(1)}, u32[]{:S(2)}, u32[]{:S(2)}) collective-permute-start(f32[3,4,4,1]{3,2,1,0:T(4,128)S(1)} %get-tuple-element.904), channel_id=1, source_target_pairs={{0,1},{1,2},{2,3},{4,5},{5,6},{6,7},{8,9},{9,10},{10,11},{12,13},{... | collective-permute-start | bytes 584 | tf_op jit(solution)/shard_map/ppermute | solution.py:32
  67.5 3.3 %collective-permute-start.8 = (f32[3,4,1,18]{3,2,1,0:T(1,128)S(1)}, f32[3,4,1,18]{3,2,1,0:T(1,128)S(1)}, u32[]{:S(2)}, u32[]{:S(2)}) collective-permute-start(f32[3,4,1,18]{3,2,1,0:T(1,128)S(1)} %pad_maximum_fusion.29), channel_id=1, source_target_pairs={{4,0},{8,4},{12,8},{16,12},{20,16},{24,20},{28,24},{5,1},{9,5},{13... | collective-permute-start | bytes 2600 | tf_op jit(solution)/shard_map/ppermute | solution.py:16
  78.5 9.2 %all-to-all-start.1 = ((f32[32,1,128]{2,1,0:T(1,128)}), f32[32,1,128]{2,1,0:T(1,128)S(1)}, u32[]{:S(2)}, u32[]{:S(2)}) async-start(f32[32,1,128]{2,1,0:T(1,128)} %broadcast_in_dim.5), calls=%async_computation.1 | async-start | bytes 32768 | tf_op jit(solution)/shard_map/all_to_all | solution.py:23
  95.7 9.4 %collective-permute-start.10 = (f32[28,4,1]{2,1,0:T(4,128)S(1)}, f32[28,4,1]{2,1,0:T(4,128)S(1)}, u32[]{:S(2)}, u32[]{:S(2)}) collective-permute-start(f32[28,4,1]{2,1,0:T(4,128)S(1)} %bitcast.4434), channel_id=1, source_target_pairs={{1,0},{2,1},{3,2},{5,4},{6,5},{7,6},{9,8},{10,9},{11,10},{13,12},{... | collective-permute-start | bytes 1352 | tf_op jit(solution)/shard_map/ppermute | solution.py:16
  102.7 6.7 %collective-permute-start.9 = (f32[2,28,4,1]{3,2,1,0:T(4,128)S(1)}, f32[2,28,4,1]{3,2,1,0:T(4,128)S(1)}, u32[]{:S(2)}, u32[]{:S(2)}) collective-permute-start(f32[2,28,4,1]{3,2,1,0:T(4,128)S(1)} %slice_maximum_fusion), channel_id=1, source_target_pairs={{0,1},{1,2},{2,3},{4,5},{5,6},{6,7},{8,9},{9,10},{10,11},{12,13},{... | collective-permute-start | bytes 2696 | tf_op jit(solution)/shard_map/ppermute | solution.py:16
  109.5 6.2 %collective-permute-start.11 = (f32[3,28,1,16]{3,2,1,0:T(1,128)S(1)}, f32[3,28,1,16]{3,2,1,0:T(1,128)S(1)}, u32[]{:S(2)}, u32[]{:S(2)}) collective-permute-start(f32[3,28,1,16]{3,2,1,0:T(1,128)S(1)} %pad_maximum_fusion.4), channel_id=1, source_target_pairs={{0,4},{4,8},{8,12},{12,16},{16,20},{20,24},{24,28},{1,5},{5,9},{9,... | collective-permute-start | bytes 16136 | tf_op jit(solution)/shard_map/ppermute | solution.py:16

commit v2 on v0

v2 whole, which is shorter than its diff:
```python
import jax
import jax.numpy as jnp
from jax import lax
from jax.experimental import pallas as pl
from jax.experimental.pallas import tpu as pltpu
from jax.sharding import PartitionSpec as P

ITERS = 2
LANES = 128
SUB = 8
COMPS = 7

link_offsets = ((0, 1), (1, 0), (1, 1), (1, -1))
damping_scale = 64.0
GRAM = [(a, b) for a in range(4) for b in range(a + 1)]


def whole(count):
    return [pl.BlockSpec(memory_space=pltpu.VMEM) for _ in range(count)]


def call(body, out_shapes, scratch=(), **params):
    shapes = [jax.ShapeDtypeStruct(s, jnp.float32) for s in out_shapes]

    def run(*args):
        return pl.pallas_call(
            body,
            out_shape=shapes,
            in_specs=whole(len(args)),
            out_specs=whole(len(shapes)),
            scratch_shapes=[pltpu.VMEM(s, jnp.float32) for s in scratch],
            **params,
        )(*args)

    return run


def iota(shape, axis):
    return lax.broadcasted_iota(jnp.int32, shape, axis)


def component(refs, d, c):
    here, there, mask = refs
    if c < 3:
        return here.at[d, c]
    if c < 6:
        return there.at[d, c - 3]
    return mask.at[d]


def pack_cols(rows, cols):
    def body(here, there, outlier, transforms, mask, to_east, to_west):
        grid_rows = rows * lax.axis_size("row")
        grid_cols = cols * lax.axis_size("col")
        row0 = lax.axis_index("row") * rows
        col_ids = lax.axis_index("col") * cols + iota((cols, LANES), 0)
        for d, (dr, dc) in enumerate(link_offsets):
            col_valid = jnp.where((col_ids + dc >= 0) & (col_ids + dc < grid_cols), 1.0, 0.0)
            for r in range(rows):
                row_valid = jnp.where(row0 + r + dr < grid_rows, 1.0, 0.0)
                mask[d, r] = outlier[d, r].astype(jnp.float32) * (col_valid * row_valid)
        refs = (here, there, mask)
        for d in range(4):
            for c in range(COMPS):
                src = component(refs, d, c)
                for r in range(rows):
                    at = ((d * COMPS + c) * rows + r) * 2
                    to_east[at : at + 2] = src[r, cols - 2 : cols]
                    to_west[at : at + 2] = src[r, 0:2]
        at = 4 * COMPS * rows * 2
        for out in (to_east, to_west):
            out[at:] = jnp.zeros((12 * rows, LANES), jnp.float32)
            out[at:, 0:cols] = transforms[...]

    count = 4 * COMPS * rows * 2 + 12 * rows
    return call(body, [(4, rows, cols, LANES), (count, LANES), (count, LANES)])


def pack_rows(rows, cols):
    span = cols + 4

    def body(here, there, mask, transforms, west, east, text, up_t, down, up):
        at = 4 * COMPS * rows * 2
        lane = iota((12 * rows, LANES), 1)
        text[...] = jnp.zeros((12 * rows, LANES), jnp.float32)
        text[:, 0:cols] = transforms[...]
        wide = pltpu.roll(text[...], 2, 1)
        left = pltpu.roll(west[at:], LANES - (cols - 2), 1)
        right = pltpu.roll(east[at:], cols + 2, 1)
        value = jnp.where(lane < 2, left, jnp.where(lane < cols + 2, wide, right))
        text[...] = jnp.where(lane < span, value, 0.0)
        refs = (here, there, mask)
        for d in range(4):
            for c in range(COMPS):
                src = component(refs, d, c)
                n = d * COMPS + c
                for out, k, r in ((down, 0, rows - 2), (down, 1, rows - 1), (up, 0, 0)):
                    per = 2 if out is down else 1
                    to = (n * per + k) * span
                    side = (n * rows + r) * 2
                    out[to : to + 2] = west[side : side + 2]
                    out[to + 2 : to + 2 + cols] = src[r]
                    out[to + 2 + cols : to + span] = east[side : side + 2]
        at = 4 * COMPS * 2 * span
        for k in range(12):
            up_t[2 * k : 2 * k + 2] = text[k * rows : k * rows + 2]
            down[at + 2 * k : at + 2 * k + 2] = text[(k + 1) * rows - 2 : (k + 1) * rows]

    n = 4 * COMPS
    return call(
        body,
        [(12 * rows, LANES), (24, LANES), (n * 2 * span + 24, LANES), (n * span, LANES)],
    )


def spread(row, out, k, at, span):
    full = -(-span // SUB) * SUB
    wide = jnp.broadcast_to(row, (full, LANES))
    picked = jnp.where(iota((full, LANES), 0) == iota((full, LANES), 1), wide, 0.0)
    value = jnp.broadcast_to(jnp.sum(picked, axis=1, keepdims=True), (full, LANES))
    out[k, at : at + span] = value[:span]


def apply_rows(affine, points):
    mapped = []
    for c in range(3):
        value = affine(4 * c + 3) + affine(4 * c) * points[0]
        value = value + affine(4 * c + 1) * points[1]
        mapped.append(value + affine(4 * c + 2) * points[2])
    return mapped


def squared(here, there):
    delta = [a - b for a, b in zip(here, there)]
    return delta[0] * delta[0] + delta[1] * delta[1] + delta[2] * delta[2]


def send_stats(out, largest, total, count):
    lane = iota(out.shape, len(out.shape) - 1)
    out[...] = jnp.where(lane == 0, largest, jnp.where(lane == 1, total, jnp.where(lane == 2, count, 0.0)))


def read_stats(got):
    values = got[...]
    lane = iota(values.shape, 2)
    largest = jnp.max(jnp.where(lane == 0, values, 0.0))
    total = jnp.sum(jnp.where(lane == 1, values, 0.0))
    count = jnp.sum(jnp.where(lane == 2, values, 0.0))
    return largest, total / jnp.maximum(count, 1.0)


def first_stats(rows, cols, devices):
    span = cols + 4

    def body(here, there, mask, text, up_t, out, rep):
        for k in range(12):
            for r in range(rows):
                spread(text[k * rows + r : k * rows + r + 1], rep, k, r * span, span)
            spread(up_t[2 * k : 2 * k + 1], rep, k, rows * span, span)
        top = jnp.zeros((cols, LANES), jnp.float32)
        total = jnp.zeros((cols, LANES), jnp.float32)
        count = jnp.zeros((cols, LANES), jnp.float32)
        for d, (dr, dc) in enumerate(link_offsets):
            for r in range(rows):
                near = r * span + 2
                far = (r + dr) * span + 2 + dc
                a = apply_rows(lambda k: rep[k, near : near + cols], [here[d, c, r] for c in range(3)])
                b = apply_rows(lambda k: rep[k, far : far + cols], [there[d, c, r] for c in range(3)])
                weight = mask[d, r]
                masked = weight * squared(a, b)
                top = jnp.maximum(top, masked)
                total = total + masked
                count = count + weight
        send_stats(out, jnp.max(top), jnp.sum(total), jnp.sum(count))

    pad = -(-((rows + 1) * span) // SUB) * SUB + SUB
    return call(body, [(devices, 1, LANES)], [(12, pad, LANES)])


class Flat:

    def __init__(self, rows, cols):
        self.rows, self.cols = rows, cols
        self.span = cols + 4
        self.tiles = -(-((rows + 4) * self.span + self.span + 1) // SUB) * SUB + 2 * SUB
        self.shift = [dr * self.span + dc for dr, dc in link_offsets]

    def at(self, r, c):
        return SUB + (r + 2) * self.span + c + 2

    def blocks(self, r0, c0, r1, c1):
        return range(self.at(r0, c0) // SUB * SUB, self.at(r1, c1) + 1, SUB)

    def owned(self, f):
        index = iota((SUB, LANES), 0) + f
        keep = None
        for r in range(self.rows):
            low, high = self.at(r, 0), self.at(r, self.cols - 1)
            if low <= f and f + SUB - 1 <= high:
                return True
            if low < f + SUB and high >= f:
                one = (index >= low) & (index <= high)
                keep = one if keep is None else keep | one
        return keep


def link_values(flat, f, d, points, rep, errors, here_out, there_out):
    near = slice(f, f + SUB)
    far = slice(f + flat.shift[d], f + flat.shift[d] + SUB)
    a = apply_rows(lambda k: rep[k, near], [points[d * COMPS + c, near] for c in range(3)])
    b = apply_rows(lambda k: rep[k, far], [points[d * COMPS + 3 + c, near] for c in range(3)])
    error = squared(a, b)
    errors[d, near] = error
    for c in range(3):
        here_out[3 * d + c, near] = a[c]
        there_out[3 * d + c, near] = b[c]
    return error


def assemble(rows, cols):
    flat = Flat(rows, cols)
    span = flat.span

    def body(here, there, mask, text, west, east, north, south, up_t, points, rep, errors, mapped, target):
        refs = (here, there, mask)
        for d in range(4):
            for c in range(COMPS):
                n = d * COMPS + c
                src = component(refs, d, c)
                at = flat.at(-2, -2)
                points[n, at : at + 2 * span] = north[n * 2 * span : (n + 1) * 2 * span]
                for r in range(rows):
                    at = flat.at(r, -2)
                    side = (n * rows + r) * 2
                    points[n, at : at + 2] = west[side : side + 2]
                    points[n, at + 2 : at + 2 + cols] = src[r]
                    points[n, at + 2 + cols : at + span] = east[side : side + 2]
                at = flat.at(rows, -2)
                points[n, at : at + span] = south[n * span : (n + 1) * span]
        north_t = 4 * COMPS * 2 * span
        for k in range(12):
            for j in range(2):
                row = north_t + 2 * k + j
                spread(north[row : row + 1], rep, k, flat.at(j - 2, -2), span)
                spread(up_t[2 * k + j : 2 * k + j + 1], rep, k, flat.at(rows + j, -2), span)
            for r in range(rows):
                spread(text[k * rows + r : k * rows + r + 1], rep, k, flat.at(r, -2), span)
        for f in flat.blocks(-2, -2, rows, cols + 1):
            for d in range(4):
                link_values(flat, f, d, points, rep, errors, mapped, target)

    t = flat.tiles
    return call(
        body,
        [(4 * COMPS, t, LANES), (12, t, LANES), (4, t, LANES), (12, t, LANES), (12, t, LANES)],
    )


def weigh(flat, blocks, points, errors, weights, scale):
    for f in blocks:
        for d in range(4):
            weights[d, f : f + SUB] = points[d * COMPS + 6, f : f + SUB] * scale / (scale + errors[d, f : f + SUB])


def tile_sums(flat, f, points, mapped, target, weights):
    gram = {}
    cross = {}

    def put(store, key, value):
        store[key] = value if key not in store else store[key] + value

    for d in range(4):
        for end in range(2):
            at = f if end == 0 else f - flat.shift[d]
            rows = slice(at, at + SUB)
            base = d * COMPS + 3 * end
            x = [points[base + c, rows] for c in range(3)]
            other = target if end == 0 else mapped
            weight = weights[d, rows]
            weighted = [weight * v for v in x] + [weight]
            for a, b in GRAM:
                if a == 3:
                    put(gram, (a, b), weighted[b])
                else:
                    put(gram, (a, b), weighted[a] * x[b])
            for c in range(3):
                scaled = weight * other[3 * d + c, rows]
                put(cross, (c, 3), scaled)
                for b in range(3):
                    put(cross, (c, b), scaled * x[b])

    def lanes(v):
        return jnp.broadcast_to(jnp.sum(v, axis=1, keepdims=True), v.shape)

    return {k: lanes(v) for k, v in gram.items()}, {k: lanes(v) for k, v in cross.items()}


def solve_small(gram, cross):
    factor = {}
    inverse = {}
    for a in range(4):
        for b in range(a + 1):
            value = gram[a, b]
            for i in range(b):
                value = value - factor[a, i] * factor[b, i]
            if a == b:
                inverse[a] = 1.0 / jnp.sqrt(value)
            else:
                factor[a, b] = value * inverse[b]
    result = []
    for c in range(3):
        forward = []
        for a in range(4):
            value = cross[c, a]
            for i in range(a):
                value = value - factor[a, i] * forward[i]
            forward.append(value * inverse[a])
        backward = [None] * 4
        for a in (3, 2, 1, 0):
            value = forward[a]
            for i in range(a + 1, 4):
                value = value - factor[i, a] * backward[i]
            backward[a] = value * inverse[a]
        result.extend(backward)
    return result


def update(flat, blocks, points, rep, mapped, target, weights, damping, out):
    for f in blocks:
        gram, cross = tile_sums(flat, f, points, mapped, target, weights)
        for a in range(4):
            gram[a, a] = gram[a, a] + damping
        for c in range(3):
            for b in range(4):
                cross[c, b] = cross[c, b] + damping * rep[4 * c + b, f : f + SUB]
        for k, value in enumerate(solve_small(gram, cross)):
            out[k, f : f + SUB] = value


def first_update(rows, cols, devices):
    flat = Flat(rows, cols)

    def body(got, points, rep, errors, mapped, target, new_rep, new_errors, new_mapped, new_target, out, weights):
        largest, mean_error = read_stats(got)
        scale = 0.25 * largest + 1e-06
        damping = damping_scale * mean_error + 1.0
        weigh(flat, flat.blocks(-2, -2, rows, cols + 1), points, errors, weights, scale)
        update(flat, flat.blocks(-1, -1, rows, cols), points, rep, mapped, target, weights, damping, new_rep)
        zero = jnp.zeros((SUB, LANES), jnp.float32)
        top, total, count = zero, zero, zero
        for f in flat.blocks(-1, -1, rows - 1, cols):
            keep = flat.owned(f)
            for d in range(4):
                error = link_values(flat, f, d, points, new_rep, new_errors, new_mapped, new_target)
                if keep is None:
                    continue
                weight = points[d * COMPS + 6, f : f + SUB]
                masked = weight * error
                if keep is not True:
                    masked = jnp.where(keep, masked, 0.0)
                    weight = jnp.where(keep, weight, 0.0)
                top = jnp.maximum(top, masked)
                total = total + masked
                count = count + weight
        send_stats(out, jnp.max(top), jnp.sum(total), jnp.sum(count))

    t = flat.tiles
    return call(
        body,
        [(12, t, LANES), (4, t, LANES), (12, t, LANES), (12, t, LANES), (devices, 1, LANES)],
        [(4, t, LANES)],
    )


def last_update(rows, cols):
    flat = Flat(rows, cols)

    def body(got0, got1, points, rep, errors, mapped, target, aligned, stats, weights, new_rep):
        first, mean0 = read_stats(got0)
        largest, mean_error = read_stats(got1)
        scale = 0.25 * largest + 1e-06
        damping = damping_scale * mean_error + 1.0
        weigh(flat, flat.blocks(-1, -1, rows - 1, cols), points, errors, weights, scale)
        update(flat, flat.blocks(0, 0, rows - 1, cols - 1), points, rep, mapped, target, weights, damping, new_rep)
        diagonal = iota((cols, LANES), 0) == iota((cols, LANES), 1)
        for k in range(12):
            for r in range(rows):
                at = flat.at(r, 0)
                value = jnp.where(diagonal, new_rep[k, at : at + cols], 0.0)
                aligned[k, r : r + 1] = jnp.sum(value, axis=0, keepdims=True)[:, 0:cols]
        row = iota((2, 2), 0)
        col = iota((2, 2), 1)
        stats[...] = jnp.where(row == 0, jnp.where(col == 0, first, largest), jnp.where(col == 0, mean0, mean_error))

    t = flat.tiles
    return call(body, [(12, rows, cols), (2, 2)], [(4, t, LANES), (12, t, LANES)])


def onward(array, axis, by):
    peers = lax.axis_size(axis)
    return lax.ppermute(array, axis, [(i, i + by) for i in range(peers) if 0 <= i + by < peers])


def everyone(array):
    return lax.all_to_all(array, ("row", "col"), 0, 0)


def on_device(points_here, points_there, outlier_mask, transforms):
    rows, cols = transforms.shape[2:]
    devices = lax.axis_size("row") * lax.axis_size("col")
    flat_transforms = transforms.reshape(12 * rows, cols)
    mask, to_east, to_west = pack_cols(rows, cols)(points_here, points_there, outlier_mask, flat_transforms)
    west = onward(to_east, "col", 1)
    east = onward(to_west, "col", -1)
    text, to_up_t, to_down, to_up = pack_rows(rows, cols)(
        points_here, points_there, mask, flat_transforms, west, east
    )
    up_t = onward(to_up_t, "row", -1)
    north = onward(to_down, "row", 1)
    south = onward(to_up, "row", -1)
    (sent,) = first_stats(rows, cols, devices)(points_here, points_there, mask, text, up_t)
    got0 = everyone(sent)
    points, rep, errors, mapped, target = assemble(rows, cols)(
        points_here, points_there, mask, text, west, east, north, south, up_t
    )
    rep, errors, mapped, target, sent = first_update(rows, cols, devices)(
        got0, points, rep, errors, mapped, target
    )
    got1 = everyone(sent)
    aligned, stats = last_update(rows, cols)(got0, got1, points, rep, errors, mapped, target)
    return aligned.reshape(3, 4, rows, cols), stats


def solution(mesh):
    return jax.shard_map(
        on_device,
        mesh=mesh,
        in_specs=(
            P(None, None, "row", "col", None),
            P(None, None, "row", "col", None),
            P(None, "row", "col", None),
            P(None, None, "row", "col"),
        ),
        out_specs=(P(None, None, "row", "col"), P()),
        check_vma=False,
    )
```

time: 257 us -> 71.8 us (0.28)
  the two profiles are of different devices: /device:TPU:20 before, /device:TPU:0 now
where the time goes in v2:
time: 71.8 us; the launch traced here: 71.5 us
  Pallas kernels  23.4 us (33%)
  starting transfers between devices  20.7 us (29%)
  blocking collectives  12.7 us (18%)
  waiting for transfers between devices  10.6 us (15%)
  local copies, waits for them, and re-layouts  3.35 us (5%)
    pallas_call x6, Pallas kernels, run(): pl.pallas_call(body, out_shape=shapes, in_specs=whole(len(args)), out_spe...  23.4 us
    all_to_all x1, blocking collectives, everyone(): return lax.all_to_all(array, ('row', 'col'), 0, 0)  12.7 us
    all_to_all x1, starting transfers between devices, everyone(): return lax.all_to_all(array, ('row', 'col'), 0, 0)  10.6 us
    ppermute x5, waiting for transfers between devices, onward(): lax.ppermute(array, axis, [(i, i + by) for i in range(peers) if 0 <= i +...  10.2 us
    ppermute x5, starting transfers between devices, onward(): lax.ppermute(array, axis, [(i, i + by) for i in range(peers) if 0 <= i +...  10.1 us
    unnamed x12, local copies, waits for them, and re-layouts  3.35 us
  transfers between devices with their start and end apart: 6, of which 4 were waited for; matrix products, arithmetic and copies ran while one was open for 0% of the time, Pallas kernels for 11%

profile of v2, /device:TPU:0, one launch (start us, length us, event | category | flops | bytes accessed | tf_op | source)
XLA Modules:
  0.0 71.5 jit_solution(12068612018482183223)
XLA Ops:
  0.6 2.0 %shard_map.59 = (f32[4,4,16,128]{3,2,1,0:T(8,128)}, f32[272,128]{1,0:T(8,128)}, f32[272,128]{1,0:T(8,128)}) custom-call(f32[4,3,4,16,128]{4,3,2,1,0:T(8,128)} %here.7, f32[4,3,4,16,128]{4,3,2,1,0:T(8,128)} %there.7, s32[4,4,16,128]{3,2,1,0:T(8,128)} %outlier.1, f32[48,16]{1,0:T(8,128)} %bitcast.2), custom_call_target="tpu_custom_call" | custom-call | tf_op jit(solution)/shard_map/pallas_call | solution.py:26
  2.6 5.0 %collective-permute-start = (f32[272,128]{1,0:T(8,128)}, f32[272,128]{1,0:T(8,128)S(1)}, u32[]{:S(2)}, u32[]{:S(2)}) collective-permute-start(f32[272,128]{1,0:T(8,128)} %get-tuple-element.22), channel_id=1, source_target_pairs={{0,1},{1,2},{2,3},{4,5},{5,6},{6,7},{8,9},{9,10},{10,11},{12,13},{... | collective-permute-start | bytes 417800 | tf_op jit(solution)/shard_map/ppermute | solution.py:401
  7.6 1.3 %collective-permute-start.1 = (f32[272,128]{1,0:T(8,128)}, f32[272,128]{1,0:T(8,128)S(1)}, u32[]{:S(2)}, u32[]{:S(2)}) collective-permute-start(f32[272,128]{1,0:T(8,128)} %get-tuple-element.23), channel_id=1, source_target_pairs={{1,0},{2,1},{3,2},{5,4},{6,5},{7,6},{9,8},{10,9},{11,10},{13,12},{... | collective-permute-start | bytes 417800 | tf_op jit(solution)/shard_map/ppermute | solution.py:401
  8.9 1.9 %collective-permute-done.west = f32[272,128]{1,0:T(8,128)S(1)} collective-permute-done((f32[272,128]{1,0:T(8,128)}, f32[272,128]{1,0:T(8,128)S(1)}, u32[]{:S(2)}, u32[]{:S(2)}) %collective-permute-start) | collective-permute-done | bytes 139296 | tf_op jit(solution)/shard_map/ppermute | solution.py:401
  10.8 4.0 %collective-permute-done.1.east = f32[272,128]{1,0:T(8,128)S(1)} collective-permute-done((f32[272,128]{1,0:T(8,128)}, f32[272,128]{1,0:T(8,128)S(1)}, u32[]{:S(2)}, u32[]{:S(2)}) %collective-permute-start.1) | collective-permute-done | bytes 139296 | tf_op jit(solution)/shard_map/ppermute | solution.py:401
  14.8 0.6 copy-done.2
  15.5 2.3 %shard_map.60 = (f32[48,128]{1,0:T(8,128)}, f32[24,128]{1,0:T(8,128)}, f32[1144,128]{1,0:T(8,128)}, f32[560,128]{1,0:T(8,128)}) custom-call(f32[4,3,4,16,128]{4,3,2,1,0:T(8,128)} %here.7, f32[4,3,4,16,128]{4,3,2,1,0:T(8,128)} %there.7, f32[4,4,16,128]{3,2,1,0:T(8,128)} %get-tuple-element.21.mask, f32[48,16]{1,0:T(8,128)} %bitcast.3, f32[272,128]{1,0:T(8,128)} %copy-done.1, ...), custom_call_target="tpu_custom_call" | custom-call | tf_op jit(solution)/shard_map/pallas_call | solution.py:26
  17.7 1.3 %collective-permute-start.3 = (f32[1144,128]{1,0:T(8,128)}, f32[1144,128]{1,0:T(8,128)S(1)}, u32[]{:S(2)}, u32[]{:S(2)}) collective-permute-start(f32[1144,128]{1,0:T(8,128)} %get-tuple-element.26), channel_id=1, source_target_pairs={{0,4},{4,8},{8,12},{12,16},{16,20},{20,24},{24,28},{1,5},{5,9},{9,... | collective-permute-start | bytes 1757192 | tf_op jit(solution)/shard_map/ppermute | solution.py:401
  19.1 1.3 %collective-permute-start.4 = (f32[560,128]{1,0:T(8,128)}, f32[560,128]{1,0:T(8,128)S(1)}, u32[]{:S(2)}, u32[]{:S(2)}) collective-permute-start(f32[560,128]{1,0:T(8,128)} %get-tuple-element.27), channel_id=1, source_target_pairs={{4,0},{8,4},{12,8},{16,12},{20,16},{24,20},{28,24},{5,1},{9,5},{13... | collective-permute-start | bytes 860168 | tf_op jit(solution)/shard_map/ppermute | solution.py:401
  20.4 1.3 %collective-permute-start.2 = (f32[24,128]{1,0:T(8,128)}, f32[24,128]{1,0:T(8,128)S(1)}, u32[]{:S(2)}, u32[]{:S(2)}) collective-permute-start(f32[24,128]{1,0:T(8,128)} %get-tuple-element.25), channel_id=1, source_target_pairs={{4,0},{8,4},{12,8},{16,12},{20,16},{24,20},{28,24},{5,1},{9,5},{13... | collective-permute-start | bytes 36872 | tf_op jit(solution)/shard_map/ppermute | solution.py:401
  21.7 4.3 %collective-permute-done.2.up_t = f32[24,128]{1,0:T(8,128)S(1)} collective-permute-done((f32[24,128]{1,0:T(8,128)}, f32[24,128]{1,0:T(8,128)S(1)}, u32[]{:S(2)}, u32[]{:S(2)}) %collective-permute-start.2) | collective-permute-done | bytes 12320 | tf_op jit(solution)/shard_map/ppermute | solution.py:401
  26.0 0.6 copy-done.5
  26.6 2.3 %shard_map.61 = f32[32,1,128]{2,1,0:T(1,128)} custom-call(f32[4,3,4,16,128]{4,3,2,1,0:T(8,128)} %here.7, f32[4,3,4,16,128]{4,3,2,1,0:T(8,128)} %there.7, f32[4,4,16,128]{3,2,1,0:T(8,128)} %get-tuple-element.21.mask, f32[48,128]{1,0:T(8,128)} %get-tuple-element.24.text, f32[24,128]{1,0:T(8,128)} %copy-done.5), custom_call_target="tpu_custom_call" | custom-call | tf_op jit(solution)/shard_map/pallas_call | solution.py:26
  28.9 10.6 %all-to-all-start = ((f32[32,1,128]{2,1,0:T(1,128)}), f32[32,1,128]{2,1,0:T(1,128)S(1)}, u32[]{:S(2)}, u32[]{:S(2)}) async-start(f32[32,1,128]{2,1,0:T(1,128)} %shard_map.61), calls=%async_computation | async-start | bytes 32768 | tf_op jit(solution)/shard_map/all_to_all | solution.py:405
  39.5 0.0 collective-permute-done.4.south
  39.5 0.0 collective-permute-done.3.north
  39.5 0.7 copy-done.3
  40.2 0.8 %copy-done = f32[1144,128]{1,0:T(8,128)} copy-done((f32[1144,128]{1,0:T(8,128)}, f32[1144,128]{1,0:T(8,128)S(1)}, u32[]{:S(2)}) %copy-start) | copy-done | bytes 585752
  41.0 5.3 %shard_map.62 = (f32[28,200,128]{2,1,0:T(8,128)}, f32[12,200,128]{2,1,0:T(8,128)}, f32[4,200,128]{2,1,0:T(8,128)}, f32[12,200,128]{2,1,0:T(8,128)}, f32[12,200,128]{2,1,0:T(8,128)}) custom-call(f32[4,3,4,16,128]{4,3,2,1,0:T(8,128)} %here.7, f32[4,3,4,16,128]{4,3,2,1,0:T(8,128)} %there.7, f32[4,4,16,128]{3,2,1,0:T(8,128)} %get-tuple-element.21.mask, ...), custom_call_target="tpu_custom_call" | custom-call | tf_op jit(solution)/shard_map/pallas_call | solution.py:26
  46.3 0.3 all-to-all-done.got.got0
  46.7 0.6 copy-done.4
  47.3 6.7 %shard_map.63 = (f32[12,200,128]{2,1,0:T(8,128)}, f32[4,200,128]{2,1,0:T(8,128)}, f32[12,200,128]{2,1,0:T(8,128)}, f32[12,200,128]{2,1,0:T(8,128)}, f32[32,1,128]{2,1,0:T(1,128)}) custom-call(f32[32,1,128]{2,1,0:T(1,128)} %copy-done.4, f32[28,200,128]{2,1,0:T(8,128)} %get-tuple-element.28.points, f32[12,200,128]{2,1,0:T(8,128)} %get-tuple-element.29.rep, ...), custom_call_target="tpu_custom_call" | custom-call | tf_op jit(solution)/shard_map/pallas_call | solution.py:26
  53.9 12.7 %all_to_all.10.got1 = f32[32,1,128]{2,1,0:T(1,128)} all-to-all(f32[32,1,128]{2,1,0:T(1,128)} %get-tuple-element.33), channel_id=1, replica_groups=mesh['row'=8,'col'=4] {'row','col'}, dimensions={0} | all-to-all | bytes 32768 | tf_op jit(solution)/shard_map/all_to_all | solution.py:405
  66.7 4.8 %shard_map.64 = (f32[12,4,16]{2,1,0:T(4,128)}, f32[2,2]{1,0:T(2,128)}) custom-call(f32[32,1,128]{2,1,0:T(1,128)} %copy-done.4, f32[32,1,128]{2,1,0:T(1,128)} %all_to_all.10.got1, f32[28,200,128]{2,1,0:T(8,128)} %get-tuple-element.28.points, f32[12,200,128]{2,1,0:T(8,128)} %get-tuple-element.34.rep, f32[4,200,128]{2,1,0:T(8,128)} %get-tuple-element.35.errors, ...), custom_call_target="tpu_custom_call" | custom-call | tf_op jit(solution)/shard_map/pallas_call | solution.py:26
  (7 shorter events, 0.0 us)
Async XLA Ops:
  2.6 8.2 %collective-permute-start = (f32[272,128]{1,0:T(8,128)}, f32[272,128]{1,0:T(8,128)S(1)}, u32[]{:S(2)}, u32[]{:S(2)}) collective-permute-start(f32[272,128]{1,0:T(8,128)} %get-tuple-element.22), channel_id=1, source_target_pairs={{0,1},{1,2},{2,3},{4,5},{5,6},{6,7},{8,9},{9,10},{10,11},{12,13},{... | collective-permute-start | bytes 417800 | tf_op jit(solution)/shard_map/ppermute | solution.py:401
  7.6 7.2 %collective-permute-start.1 = (f32[272,128]{1,0:T(8,128)}, f32[272,128]{1,0:T(8,128)S(1)}, u32[]{:S(2)}, u32[]{:S(2)}) collective-permute-start(f32[272,128]{1,0:T(8,128)} %get-tuple-element.23), channel_id=1, source_target_pairs={{1,0},{2,1},{3,2},{5,4},{6,5},{7,6},{9,8},{10,9},{11,10},{13,12},{... | collective-permute-start | bytes 417800 | tf_op jit(solution)/shard_map/ppermute | solution.py:401
  10.8 4.0 %copy-start.1 = (f32[272,128]{1,0:T(8,128)}, f32[272,128]{1,0:T(8,128)S(1)}, u32[]{:S(2)}) copy-start(f32[272,128]{1,0:T(8,128)S(1)} %collective-permute-done.west) | copy-start | bytes 417796
  14.8 0.6 copy-start.2
  17.7 21.8 %collective-permute-start.3 = (f32[1144,128]{1,0:T(8,128)}, f32[1144,128]{1,0:T(8,128)S(1)}, u32[]{:S(2)}, u32[]{:S(2)}) collective-permute-start(f32[1144,128]{1,0:T(8,128)} %get-tuple-element.26), channel_id=1, source_target_pairs={{0,4},{4,8},{8,12},{12,16},{16,20},{20,24},{24,28},{1,5},{5,9},{9,... | collective-permute-start | bytes 1757192 | tf_op jit(solution)/shard_map/ppermute | solution.py:401
  19.1 20.4 %collective-permute-start.4 = (f32[560,128]{1,0:T(8,128)}, f32[560,128]{1,0:T(8,128)S(1)}, u32[]{:S(2)}, u32[]{:S(2)}) collective-permute-start(f32[560,128]{1,0:T(8,128)} %get-tuple-element.27), channel_id=1, source_target_pairs={{4,0},{8,4},{12,8},{16,12},{20,16},{24,20},{28,24},{5,1},{9,5},{13... | collective-permute-start | bytes 860168 | tf_op jit(solution)/shard_map/ppermute | solution.py:401
  20.4 5.6 %collective-permute-start.2 = (f32[24,128]{1,0:T(8,128)}, f32[24,128]{1,0:T(8,128)S(1)}, u32[]{:S(2)}, u32[]{:S(2)}) collective-permute-start(f32[24,128]{1,0:T(8,128)} %get-tuple-element.25), channel_id=1, source_target_pairs={{4,0},{8,4},{12,8},{16,12},{20,16},{24,20},{28,24},{5,1},{9,5},{13... | collective-permute-start | bytes 36872 | tf_op jit(solution)/shard_map/ppermute | solution.py:401
  26.0 0.6 copy-start.5
  28.9 17.8 %all-to-all-start = ((f32[32,1,128]{2,1,0:T(1,128)}), f32[32,1,128]{2,1,0:T(1,128)S(1)}, u32[]{:S(2)}, u32[]{:S(2)}) async-start(f32[32,1,128]{2,1,0:T(1,128)} %shard_map.61), calls=%async_computation | async-start | bytes 32768 | tf_op jit(solution)/shard_map/all_to_all | solution.py:405
  39.5 0.7 copy-start.3
  40.2 0.8 %copy-start = (f32[1144,128]{1,0:T(8,128)}, f32[1144,128]{1,0:T(8,128)S(1)}, u32[]{:S(2)}) copy-start(f32[1144,128]{1,0:T(8,128)S(1)} %collective-permute-done.3.north) | copy-start | bytes 1757188
  46.7 0.6 copy-start.4

commit v3 on v2

v3 whole, which is shorter than its diff:
```python
import jax
import jax.numpy as jnp
from jax import lax
from jax.experimental import pallas as pl
from jax.experimental.pallas import tpu as pltpu
from jax.sharding import PartitionSpec as P

LANES = 128
SUB = 8
COMPS = 7

link_offsets = ((0, 1), (1, 0), (1, 1), (1, -1))
damping_scale = 64.0
GRAM = [(a, b) for a in range(4) for b in range(a + 1)]


def call(body, out_shapes, scratch=(), in_vmem=(), in_hbm=(), aliases=None, results=pltpu.VMEM):
    shapes = [(results or jax.ShapeDtypeStruct)(s, jnp.float32) for s in out_shapes]
    vmem = pl.BlockSpec(memory_space=pltpu.VMEM)
    hbm = pl.BlockSpec(memory_space=pltpu.HBM)

    def run(*args):
        spaces = {**dict.fromkeys(in_vmem, pltpu.VMEM), **dict.fromkeys(in_hbm, pltpu.HBM)}
        args = [pltpu.with_memory_space_constraint(v, spaces[i]) if i in spaces else v for i, v in enumerate(args)]
        return pl.pallas_call(
            body,
            out_shape=shapes,
            in_specs=[hbm if i in in_hbm else vmem for i in range(len(args))],
            out_specs=[vmem] * len(shapes),
            scratch_shapes=[pltpu.VMEM(s, jnp.float32) if isinstance(s, tuple) else s for s in scratch],
            input_output_aliases=aliases or {},
            compiler_params=pltpu.CompilerParams(vmem_limit_bytes=16 * 1024 * 1024),
        )(*args)

    return run


def iota(shape, axis):
    return lax.broadcasted_iota(jnp.int32, shape, axis)


WEST_LINKS = [(0, d) for d in (0, 2)] + [(1, d) for d in range(4)]
EAST_LINKS = [(0, d) for d in range(4)] + [(1, 3)]


def side_rows(links, rows):
    return [(d, j, c, (n * COMPS + c) * rows) for n, (j, d) in enumerate(links) for c in range(COMPS)]


def pack_cols(flat):
    rows, cols = flat.rows, flat.cols
    groups = 12 * rows // SUB

    def body(here_in, there_in, outlier_in, transforms_in, points, padded, to_east, to_west, *scratch):
        here, there, outlier, transforms, sems = scratch
        copies = []
        for n, (source, goal) in enumerate(((here_in, here), (there_in, there), (outlier_in, outlier))):
            copies.append([pltpu.make_async_copy(source.at[d], goal.at[d], sems.at[n, d]) for d in range(4)])
        copies.append([pltpu.make_async_copy(transforms_in, transforms, sems.at[3, 0])])
        for d in range(4):
            for n in range(3):
                copies[n][d].start()
        copies[3][0].start()
        grid_rows = rows * lax.axis_size("row")
        grid_cols = cols * lax.axis_size("col")
        row0 = lax.axis_index("row") * rows
        col_ids = lax.axis_index("col") * cols + iota((cols, LANES), 0)
        for d, (dr, dc) in enumerate(link_offsets):
            col_valid = jnp.where((col_ids + dc >= 0) & (col_ids + dc < grid_cols), 1.0, 0.0)
            for n in range(3):
                copies[n][d].wait()
            for r in range(rows):
                own = slice(flat.at(r, 0), flat.at(r, cols))
                row_valid = jnp.where(row0 + r + dr < grid_rows, 1.0, 0.0)
                points[d * COMPS + 6, own] = outlier[d, r].astype(jnp.float32) * (col_valid * row_valid)
                for c in range(3):
                    points[d * COMPS + c, own] = here[d, c, r]
                    points[d * COMPS + 3 + c, own] = there[d, c, r]
        for out, links, first in ((to_east, WEST_LINKS, cols - 2), (to_west, EAST_LINKS, 0)):
            for d, j, c, at in side_rows(links, rows):
                for r in range(rows):
                    tile = flat.at(r, first + j)
                    out[at + r : at + r + 1] = points[d * COMPS + c, tile : tile + 1]
        padded[...] = jnp.zeros((12 * rows, LANES), jnp.float32)
        copies[3][0].wait()
        padded[:, 0:cols] = transforms[...]
        lane = iota((SUB, LANES), 1)
        for out, links, first in ((to_east, WEST_LINKS, cols - 2), (to_west, EAST_LINKS, 0)):
            packed = jnp.zeros((SUB, LANES), jnp.float32)
            for g in range(groups):
                moved = pltpu.roll(padded[g * SUB : (g + 1) * SUB], (2 * g - first) % LANES, 1)
                packed = jnp.where((lane == 2 * g) | (lane == 2 * g + 1), moved, packed)
            out[len(links) * COMPS * rows :] = packed

    count = [len(links) * COMPS * rows + SUB for links in (WEST_LINKS, EAST_LINKS)]
    return call(
        body,
        [(4 * COMPS, flat.tiles, LANES), (12 * rows, LANES), (count[0], LANES), (count[1], LANES)],
        [
            pltpu.VMEM((4, 3, rows, cols, LANES), jnp.float32),
            pltpu.VMEM((4, 3, rows, cols, LANES), jnp.float32),
            pltpu.VMEM((4, rows, cols, LANES), jnp.int32),
            pltpu.VMEM((12 * rows, cols), jnp.float32),
            pltpu.SemaphoreType.DMA((4, 4)),
        ],
        in_hbm=range(4),
    )


def pack_corner_rows(flat):
    rows, cols = flat.rows, flat.cols

    def body(padded, west, east, text, up_t):
        lane = iota((SUB, LANES), 1)
        from_west = west[len(WEST_LINKS) * COMPS * rows :]
        from_east = east[len(EAST_LINKS) * COMPS * rows :]
        for g in range(12 * rows // SUB):
            part = slice(g * SUB, (g + 1) * SUB)
            left = pltpu.roll(from_west, -2 * g % LANES, 1)
            right = pltpu.roll(from_east, (cols + 2 - 2 * g) % LANES, 1)
            own = pltpu.roll(padded[part], 2, 1)
            value = jnp.where(lane < 2, left, jnp.where(lane < cols + 2, own, right))
            text[part] = jnp.where(lane < flat.span, value, 0.0)
        for k in range(12):
            up_t[2 * k : 2 * k + 2] = text[k * rows : k * rows + 2]

    return call(body, [(12 * rows, LANES), (24, LANES)], in_vmem=(0, 1, 2))


def north_slices(flat):
    span, at, found = flat.span, 0, []
    for d in range(4):
        for c in range(COMPS):
            count = 1 if d == 0 else 2
            found.append((d * COMPS + c, 2 - count, count * span, at))
            at += count * span
    return found, at


def pack_rows(flat):
    rows, cols, span = flat.rows, flat.cols, flat.span
    slices, north_t = north_slices(flat)

    def body(points_in, west, east, text, points, down, up):
        for side, links, first in ((west, WEST_LINKS, -2), (east, EAST_LINKS, cols)):
            for d, j, c, at in side_rows(links, rows):
                for r in range(rows):
                    tile = flat.at(r, first + j)
                    points[d * COMPS + c, tile : tile + 1] = side[at + r : at + r + 1]
        for n, skip, count, to in slices:
            at = flat.at(rows - 2 + skip, -2)
            down[to : to + count] = points[n, at : at + count]
        for n in range(4 * COMPS):
            up[n * span : (n + 1) * span] = points[n, flat.at(0, -2) : flat.at(0, -2) + span]
        for k in range(12):
            down[north_t + 2 * k : north_t + 2 * k + 2] = text[(k + 1) * rows - 2 : (k + 1) * rows]

    return call(
        body,
        [(4 * COMPS, flat.tiles, LANES), (north_t + 24, LANES), (4 * COMPS * span, LANES)],
        in_vmem=(0, 1, 2, 3),
        aliases={0: 0},
    )


def spread(row, out, k, at, span):
    full = -(-span // SUB) * SUB
    wide = jnp.broadcast_to(row, (full, LANES))
    picked = jnp.where(iota((full, LANES), 0) == iota((full, LANES), 1), wide, 0.0)
    value = jnp.broadcast_to(jnp.sum(picked, axis=1, keepdims=True), (full, LANES))
    out[k, at : at + span] = value[:span]


def apply_rows(affine, points):
    mapped = []
    for c in range(3):
        value = affine(4 * c + 3) + affine(4 * c) * points[0]
        value = value + affine(4 * c + 1) * points[1]
        mapped.append(value + affine(4 * c + 2) * points[2])
    return mapped


def squared(here, there):
    delta = [a - b for a, b in zip(here, there)]
    return delta[0] * delta[0] + delta[1] * delta[1] + delta[2] * delta[2]


def send_stats(out, largest, total, count):
    lane = iota(out.shape, len(out.shape) - 1)
    out[...] = jnp.where(lane == 0, largest, jnp.where(lane == 1, total, jnp.where(lane == 2, count, 0.0)))


def read_stats(got):
    values = got[...]
    lane = iota(values.shape, 2)
    largest = jnp.max(jnp.where(lane == 0, values, 0.0))
    total = jnp.sum(jnp.where(lane == 1, values, 0.0))
    count = jnp.sum(jnp.where(lane == 2, values, 0.0))
    return largest, total / jnp.maximum(count, 1.0)


class Flat:

    def __init__(self, rows, cols):
        self.rows, self.cols = rows, cols
        self.span = cols + 4
        self.tiles = -(-((rows + 4) * self.span + self.span + 1) // SUB) * SUB + 2 * SUB
        self.shift = [dr * self.span + dc for dr, dc in link_offsets]

    def at(self, r, c):
        return SUB + (r + 2) * self.span + c + 2

    def blocks(self, r0, c0, r1, c1):
        return range(self.at(r0, c0) // SUB * SUB, self.at(r1, c1) + 1, SUB)

    def own_blocks(self):
        return self.blocks(0, 0, self.rows - 1, self.cols - 1)

    def owned(self, f):
        index = iota((SUB, LANES), 0) + f
        keep = None
        for r in range(self.rows):
            low, high = self.at(r, 0), self.at(r, self.cols - 1)
            if low <= f and f + SUB - 1 <= high:
                return True
            if low < f + SUB and high >= f:
                one = (index >= low) & (index <= high)
                keep = one if keep is None else keep | one
        return keep


def link_values(flat, f, d, points, rep, errors, here_out, there_out):
    near = slice(f, f + SUB)
    far = slice(f + flat.shift[d], f + flat.shift[d] + SUB)
    a = apply_rows(lambda k: rep[k, near], [points[d * COMPS + c, near] for c in range(3)])
    b = apply_rows(lambda k: rep[k, far], [points[d * COMPS + 3 + c, near] for c in range(3)])
    error = squared(a, b)
    errors[d, near] = error
    for c in range(3):
        here_out[3 * d + c, near] = a[c]
        there_out[3 * d + c, near] = b[c]
    return error


def own_stats(flat, points, rep, errors, mapped, target, blocks, out):
    zero = jnp.zeros((SUB, LANES), jnp.float32)
    top, total, count = zero, zero, zero
    for f in blocks:
        keep = flat.owned(f)
        for d in range(4):
            error = link_values(flat, f, d, points, rep, errors, mapped, target)
            if keep is None:
                continue
            weight = points[d * COMPS + 6, f : f + SUB]
            masked = weight * error
            if keep is not True:
                masked = jnp.where(keep, masked, 0.0)
                weight = jnp.where(keep, weight, 0.0)
            top = jnp.maximum(top, masked)
            total = total + masked
            count = count + weight
    send_stats(out, jnp.max(top), jnp.sum(total), jnp.sum(count))


def first_stats(flat, devices):
    rows = flat.rows

    def body(points, text, up_t, rep, errors, mapped, target, out):
        for k in range(12):
            for r in range(rows):
                spread(text[k * rows + r : k * rows + r + 1], rep, k, flat.at(r, -2), flat.span)
            spread(up_t[2 * k : 2 * k + 1], rep, k, flat.at(rows, -2), flat.span)
        own_stats(flat, points, rep, errors, mapped, target, flat.own_blocks(), out)

    t = flat.tiles
    return call(
        body,
        [(12, t, LANES), (4, t, LANES), (12, t, LANES), (12, t, LANES), (devices, 1, LANES)],
        in_vmem=(0, 1, 2),
    )


def outer_values(flat, points, rep, errors, mapped, target, north, south, up_t):
    rows, span = flat.rows, flat.span
    slices, north_t = north_slices(flat)
    for n, skip, count, src in slices:
        at = flat.at(skip - 2, -2)
        points[n, at : at + count] = north[src : src + count]
    for n in range(4 * COMPS):
        at = flat.at(rows, -2)
        points[n, at : at + span] = south[n * span : (n + 1) * span]
    for k in range(12):
        for j in range(2):
            row = north_t + 2 * k + j
            spread(north[row : row + 1], rep, k, flat.at(j - 2, -2), span)
        spread(up_t[2 * k + 1 : 2 * k + 2], rep, k, flat.at(rows + 1, -2), span)
    inner = set(flat.own_blocks())
    for f in flat.blocks(-2, -2, rows, flat.cols + 1):
        if f not in inner:
            for d in range(4):
                link_values(flat, f, d, points, rep, errors, mapped, target)


def weigh(blocks, points, errors, weights, scale):
    for f in blocks:
        for d in range(4):
            weights[d, f : f + SUB] = points[d * COMPS + 6, f : f + SUB] * scale / (scale + errors[d, f : f + SUB])


def tile_sums(flat, f, points, mapped, target, weights):
    gram = {}
    cross = {}

    def put(store, key, value):
        store[key] = value if key not in store else store[key] + value

    for d in range(4):
        for end in range(2):
            at = f if end == 0 else f - flat.shift[d]
            rows = slice(at, at + SUB)
            base = d * COMPS + 3 * end
            x = [points[base + c, rows] for c in range(3)]
            other = target if end == 0 else mapped
            weight = weights[d, rows]
            weighted = [weight * v for v in x] + [weight]
            for a, b in GRAM:
                if a == 3:
                    put(gram, (a, b), weighted[b])
                else:
                    put(gram, (a, b), weighted[a] * x[b])
            for c in range(3):
                scaled = weight * other[3 * d + c, rows]
                put(cross, (c, 3), scaled)
                for b in range(3):
                    put(cross, (c, b), scaled * x[b])

    def lanes(v):
        return jnp.broadcast_to(jnp.sum(v, axis=1, keepdims=True), v.shape)

    return {k: lanes(v) for k, v in gram.items()}, {k: lanes(v) for k, v in cross.items()}


def solve_small(gram, cross):
    factor = {}
    inverse = {}
    for a in range(4):
        for b in range(a + 1):
            value = gram[a, b]
            for i in range(b):
                value = value - factor[a, i] * factor[b, i]
            if a == b:
                inverse[a] = 1.0 / jnp.sqrt(value)
            else:
                factor[a, b] = value * inverse[b]
    result = []
    for c in range(3):
        forward = []
        for a in range(4):
            value = cross[c, a]
            for i in range(a):
                value = value - factor[a, i] * forward[i]
            forward.append(value * inverse[a])
        backward = [None] * 4
        for a in (3, 2, 1, 0):
            value = forward[a]
            for i in range(a + 1, 4):
                value = value - factor[i, a] * backward[i]
            backward[a] = value * inverse[a]
        result.extend(backward)
    return result


def update(flat, blocks, points, rep, mapped, target, weights, damping, out):
    for f in blocks:
        gram, cross = tile_sums(flat, f, points, mapped, target, weights)
        for a in range(4):
            gram[a, a] = gram[a, a] + damping
        for c in range(3):
            for b in range(4):
                cross[c, b] = cross[c, b] + damping * rep[4 * c + b, f : f + SUB]
        for k, value in enumerate(solve_small(gram, cross)):
            out[k, f : f + SUB] = value


def first_update(flat, devices):
    rows, cols = flat.rows, flat.cols

    def body(*refs):
        got, north, south, up_t = refs[5:9]
        points, rep, errors, mapped, target, new_rep, out, weights = refs[9:]
        state = (points, rep, errors, mapped, target)
        outer_values(flat, *state, north, south, up_t)
        largest, mean_error = read_stats(got)
        scale = 0.25 * largest + 1e-06
        damping = damping_scale * mean_error + 1.0
        weigh(flat.blocks(-2, -2, rows, cols + 1), points, errors, weights, scale)
        update(flat, flat.blocks(-1, -1, rows, cols), points, rep, mapped, target, weights, damping, new_rep)
        blocks = flat.blocks(-1, -1, rows - 1, cols)
        own_stats(flat, points, new_rep, errors, mapped, target, blocks, out)

    t = flat.tiles
    return call(
        body,
        [(4 * COMPS, t, LANES)] + [(n, t, LANES) for n in (12, 4, 12, 12, 12)] + [(devices, 1, LANES)],
        [(4, t, LANES)],
        in_vmem=range(9),
        aliases={i: i for i in range(5)},
    )


def last_update(flat):
    rows, cols = flat.rows, flat.cols

    def body(got0, got1, points, rep, errors, mapped, target, aligned, stats, weights, new_rep):
        first, mean0 = read_stats(got0)
        largest, mean_error = read_stats(got1)
        scale = 0.25 * largest + 1e-06
        damping = damping_scale * mean_error + 1.0
        weigh(flat.blocks(-1, -1, rows - 1, cols), points, errors, weights, scale)
        update(flat, flat.blocks(0, 0, rows - 1, cols - 1), points, rep, mapped, target, weights, damping, new_rep)
        diagonal = iota((cols, LANES), 0) == iota((cols, LANES), 1)
        for k in range(12):
            for r in range(rows):
                at = flat.at(r, 0)
                value = jnp.where(diagonal, new_rep[k, at : at + cols], 0.0)
                aligned[k, r : r + 1] = jnp.sum(value, axis=0, keepdims=True)[:, 0:cols]
        row = iota((2, 2), 0)
        col = iota((2, 2), 1)
        stats[...] = jnp.where(row == 0, jnp.where(col == 0, first, largest), jnp.where(col == 0, mean0, mean_error))

    t = flat.tiles
    return call(body, [(12, rows, cols), (2, 2)], [(4, t, LANES), (12, t, LANES)], in_vmem=range(7), results=None)


def onward(array, axis, by):
    peers = lax.axis_size(axis)
    return lax.ppermute(array, axis, [(i, i + by) for i in range(peers) if 0 <= i + by < peers])


def everyone(array):
    return lax.all_to_all(array, ("row", "col"), 0, 0)


def on_device(points_here, points_there, outlier_mask, transforms):
    rows, cols = transforms.shape[2:]
    devices = lax.axis_size("row") * lax.axis_size("col")
    flat = Flat(rows, cols)
    points, padded, to_east, to_west = pack_cols(flat)(
        points_here, points_there, outlier_mask, transforms.reshape(12 * rows, cols)
    )
    west = onward(to_east, "col", 1)
    east = onward(to_west, "col", -1)
    text, to_up_t = pack_corner_rows(flat)(padded, west, east)
    up_t = onward(to_up_t, "row", -1)
    points, to_down, to_up = pack_rows(flat)(points, west, east, text)
    north = onward(to_down, "row", 1)
    south = onward(to_up, "row", -1)
    rep, errors, mapped, target, sent = first_stats(flat, devices)(points, text, up_t)
    got0 = everyone(sent)
    points, _, errors, mapped, target, rep, sent = first_update(flat, devices)(
        points, rep, errors, mapped, target, got0, north, south, up_t
    )
    got1 = everyone(sent)
    aligned, stats = last_update(flat)(got0, got1, points, rep, errors, mapped, target)
    return aligned.reshape(3, 4, rows, cols), stats


def solution(mesh):
    return jax.shard_map(
        on_device,
        mesh=mesh,
        in_specs=(
            P(None, None, "row", "col", None),
            P(None, None, "row", "col", None),
            P(None, "row", "col", None),
            P(None, None, "row", "col"),
        ),
        out_specs=(P(None, None, "row", "col"), P()),
        check_vma=False,
    )
```

time: 71.8 us -> 53 us (0.74)
  Pallas kernels: 23.4 us -> 6.99 us
  blocking collectives: 12.7 us -> 25.8 us
  starting transfers between devices: 20.7 us -> 10.2 us
  local copies, waits for them, and re-layouts: 3.35 us -> 0 us
  waiting for transfers between devices: 10.6 us -> 9.09 us
    pallas_call x6, Pallas kernels: 23.4 us -> 6.99 us  [run(): pl.pallas_call(body, out_shape=shapes, in_specs=[hbm if i in in_hbm else...]
    all_to_all x1 -> x2, blocking collectives: 12.7 us -> 25.8 us  [everyone(): return lax.all_to_all(array, ('row', 'col'), 0, 0)]
    all_to_all x1 -> x0, starting transfers between devices: 10.6 us -> none  [everyone(): return lax.all_to_all(array, ('row', 'col'), 0, 0)]
    unnamed x12 -> x0, local copies, waits for them, and re-layouts: 3.35 us -> none
    ppermute x5, waiting for transfers between devices: 10.2 us -> 9.09 us  [onward(): lax.ppermute(array, axis, [(i, i + by) for i in range(peers) if 0 <= i +...]
  transfers between devices with their start and end apart: 6 -> 5, of which waited for: 4 -> 2; matrix products, arithmetic and copies ran while one was open for 0% -> 0% of each run, Pallas kernels for 11% -> 1%
where the time goes in v3:
time: 53 us; the launch traced here: 52.7 us
  blocking collectives  25.8 us (49%)
  starting transfers between devices  10.2 us (19%)
  waiting for transfers between devices  9.09 us (17%)
  Pallas kernels  6.99 us (13%)
  between operations  0.71 us (1%)
    all_to_all x2, blocking collectives, everyone(): return lax.all_to_all(array, ('row', 'col'), 0, 0)  25.8 us
    ppermute x5, starting transfers between devices, onward(): lax.ppermute(array, axis, [(i, i + by) for i in range(peers) if 0 <= i +...  10.2 us
    ppermute x5, waiting for transfers between devices, onward(): lax.ppermute(array, axis, [(i, i + by) for i in range(peers) if 0 <= i +...  9.09 us
    pallas_call x6, Pallas kernels, run(): pl.pallas_call(body, out_shape=shapes, in_specs=[hbm if i in in_hbm else...  6.99 us
  transfers between devices with their start and end apart: 5, of which 2 were waited for; matrix products, arithmetic and copies ran while one was open for 0% of the time, Pallas kernels for 1%

profile of v3, /device:TPU:0, one launch (start us, length us, event | category | flops | bytes accessed | tf_op | source)
XLA Modules:
  0.0 52.7 jit_solution(6721663309231155582)
XLA Ops:
  0.6 1.6 %shard_map.59 = (f32[28,200,128]{2,1,0:T(8,128)S(1)}, f32[48,128]{1,0:T(8,128)S(1)}, f32[176,128]{1,0:T(8,128)S(1)}, f32[148,128]{1,0:T(8,128)S(1)}) custom-call(f32[4,3,4,16,128]{4,3,2,1,0:T(8,128)} %here_in.1, f32[4,3,4,16,128]{4,3,2,1,0:T(8,128)} %there_in.1, s32[4,4,16,128]{3,2,1,0:T(8,128)} %outlier_in.1, f32[48,16]{1,0:T(8,128)} %bitcast.2), custom_call_target="tpu_custom_call" | custom-call | tf_op jit(solution)/shard_map/pallas_call | solution.py:25
  2.2 5.0 %collective-permute-start = (f32[176,128]{1,0:T(8,128)S(1)}, f32[176,128]{1,0:T(8,128)S(1)}, u32[]{:S(2)}, u32[]{:S(2)}) collective-permute-start(f32[176,128]{1,0:T(8,128)S(1)} %get-tuple-element.25), channel_id=1, source_target_pairs={{0,1},{1,2},{2,3},{4,5},{5,6},{6,7},{8,9},{9,10},{10,11},{12,13},{... | collective-permute-start | bytes 270344 | tf_op jit(solution)/shard_map/ppermute | solution.py:437
  7.2 1.3 %collective-permute-start.1 = (f32[148,128]{1,0:T(8,128)S(1)}, f32[148,128]{1,0:T(8,128)S(1)}, u32[]{:S(2)}, u32[]{:S(2)}) collective-permute-start(f32[148,128]{1,0:T(8,128)S(1)} %get-tuple-element.26), channel_id=1, source_target_pairs={{1,0},{2,1},{3,2},{5,4},{6,5},{7,6},{9,8},{10,9},{11,10},{13,12},{... | collective-permute-start | bytes 227336 | tf_op jit(solution)/shard_map/ppermute | solution.py:437
  8.5 5.0 %collective-permute-done.1.east = f32[148,128]{1,0:T(8,128)S(1)} collective-permute-done((f32[148,128]{1,0:T(8,128)S(1)}, f32[148,128]{1,0:T(8,128)S(1)}, u32[]{:S(2)}, u32[]{:S(2)}) %collective-permute-start.1) | collective-permute-done | bytes 75808 | tf_op jit(solution)/shard_map/ppermute | solution.py:437
  13.5 0.0 collective-permute-done.west
  13.5 0.1 shard_map.60
  13.6 0.2 shard_map.61
  13.8 1.3 %collective-permute-start.3 = (f32[1004,128]{1,0:T(8,128)S(1)}, f32[1004,128]{1,0:T(8,128)S(1)}, u32[]{:S(2)}, u32[]{:S(2)}) collective-permute-start(f32[1004,128]{1,0:T(8,128)S(1)} %get-tuple-element.36), channel_id=1, source_target_pairs={{0,4},{4,8},{8,12},{12,16},{16,20},{20,24},{24,28},{1,5},{5,9},{9,... | collective-permute-start | bytes 1542152 | tf_op jit(solution)/shard_map/ppermute | solution.py:437
  15.1 1.3 %collective-permute-start.4 = (f32[560,128]{1,0:T(8,128)S(1)}, f32[560,128]{1,0:T(8,128)S(1)}, u32[]{:S(2)}, u32[]{:S(2)}) collective-permute-start(f32[560,128]{1,0:T(8,128)S(1)} %get-tuple-element.37), channel_id=1, source_target_pairs={{4,0},{8,4},{12,8},{16,12},{20,16},{24,20},{28,24},{5,1},{9,5},{13... | collective-permute-start | bytes 860168 | tf_op jit(solution)/shard_map/ppermute | solution.py:437
  16.4 1.3 %collective-permute-start.2 = (f32[24,128]{1,0:T(8,128)S(1)}, f32[24,128]{1,0:T(8,128)S(1)}, u32[]{:S(2)}, u32[]{:S(2)}) collective-permute-start(f32[24,128]{1,0:T(8,128)S(1)} %get-tuple-element.30), channel_id=1, source_target_pairs={{4,0},{8,4},{12,8},{16,12},{20,16},{24,20},{28,24},{5,1},{9,5},{13... | collective-permute-start | bytes 36872 | tf_op jit(solution)/shard_map/ppermute | solution.py:437
  17.7 4.1 %collective-permute-done.2.up_t.refs_8_ = f32[24,128]{1,0:T(8,128)S(1)} collective-permute-done((f32[24,128]{1,0:T(8,128)S(1)}, f32[24,128]{1,0:T(8,128)S(1)}, u32[]{:S(2)}, u32[]{:S(2)}) %collective-permute-start.2) | collective-permute-done | bytes 12320 | tf_op jit(solution)/shard_map/ppermute | solution.py:437
  21.8 0.7 %shard_map.62 = (f32[12,200,128]{2,1,0:T(8,128)S(1)}, f32[4,200,128]{2,1,0:T(8,128)S(1)}, f32[12,200,128]{2,1,0:T(8,128)S(1)}, f32[12,200,128]{2,1,0:T(8,128)S(1)}, f32[32,1,128]{2,1,0:T(1,128)S(1)}) custom-call(f32[28,200,128]{2,1,0:T(8,128)S(1)} %get-tuple-element.29.points.refs_0_, f32[48,128]{1,0:T(8,128)S(1)} %get-tuple-element.28.text, ...), custom_call_target="tpu_custom_call" | custom-call | tf_op jit(solution)/shard_map/pallas_call | solution.py:25
  22.5 16.9 %all_to_all.10.refs_5_.got0 = f32[32,1,128]{2,1,0:T(1,128)S(1)} all-to-all(f32[32,1,128]{2,1,0:T(1,128)S(1)} %get-tuple-element.31), channel_id=1, replica_groups=mesh['row'=8,'col'=4] {'row','col'}, dimensions={0} | all-to-all | bytes 32768 | tf_op jit(solution)/shard_map/all_to_all | solution.py:441
  39.4 0.0 collective-permute-done.4.refs_7_
  39.4 0.0 collective-permute-done.3.refs_6_
  39.4 2.6 %shard_map.63 = (f32[28,200,128]{2,1,0:T(8,128)S(1)}, f32[12,200,128]{2,1,0:T(8,128)S(1)}, f32[4,200,128]{2,1,0:T(8,128)S(1)}, f32[12,200,128]{2,1,0:T(8,128)S(1...) custom-call(f32[28,200,128]{2,1,0:T(8,128)S(1)} %get-tuple-element.2, ...), custom_call_target="tpu_custom_call", output_to_operand_aliasing={{0}: (0, {}), {1}: (1, {}), {2}: (2, {}), {3}: (3, {}), {4}... | custom-call | tf_op jit(solution)/shard_map/pallas_call | solution.py:25
  41.9 8.9 %all_to_all.11.got1 = f32[32,1,128]{2,1,0:T(1,128)S(1)} all-to-all(f32[32,1,128]{2,1,0:T(1,128)S(1)} %get-tuple-element.38), channel_id=1, replica_groups=mesh['row'=8,'col'=4] {'row','col'}, dimensions={0} | all-to-all | bytes 32768 | tf_op jit(solution)/shard_map/all_to_all | solution.py:441
  50.8 1.9 %shard_map.64 = (f32[12,4,16]{2,1,0:T(4,128)}, f32[2,2]{1,0:T(2,128)}) custom-call(f32[32,1,128]{2,1,0:T(1,128)S(1)} %all_to_all.10.refs_5_.got0, f32[32,1,128]{2,1,0:T(1,128)S(1)} %all_to_all.11.got1, f32[28,200,128]{2,1,0:T(8,128)S(1)} %get-tuple-element.39.points, f32[12,200,128]{2,1,0:T(8,128)S(1)} %get-tuple-element.40.rep, ...), custom_call_target="tpu_custom_call" | custom-call | tf_op jit(solution)/shard_map/pallas_call | solution.py:25
Async XLA Ops:
  2.2 11.3 %collective-permute-start = (f32[176,128]{1,0:T(8,128)S(1)}, f32[176,128]{1,0:T(8,128)S(1)}, u32[]{:S(2)}, u32[]{:S(2)}) collective-permute-start(f32[176,128]{1,0:T(8,128)S(1)} %get-tuple-element.25), channel_id=1, source_target_pairs={{0,1},{1,2},{2,3},{4,5},{5,6},{6,7},{8,9},{9,10},{10,11},{12,13},{... | collective-permute-start | bytes 270344 | tf_op jit(solution)/shard_map/ppermute | solution.py:437
  7.2 6.3 %collective-permute-start.1 = (f32[148,128]{1,0:T(8,128)S(1)}, f32[148,128]{1,0:T(8,128)S(1)}, u32[]{:S(2)}, u32[]{:S(2)}) collective-permute-start(f32[148,128]{1,0:T(8,128)S(1)} %get-tuple-element.26), channel_id=1, source_target_pairs={{1,0},{2,1},{3,2},{5,4},{6,5},{7,6},{9,8},{10,9},{11,10},{13,12},{... | collective-permute-start | bytes 227336 | tf_op jit(solution)/shard_map/ppermute | solution.py:437
  13.8 25.6 %collective-permute-start.3 = (f32[1004,128]{1,0:T(8,128)S(1)}, f32[1004,128]{1,0:T(8,128)S(1)}, u32[]{:S(2)}, u32[]{:S(2)}) collective-permute-start(f32[1004,128]{1,0:T(8,128)S(1)} %get-tuple-element.36), channel_id=1, source_target_pairs={{0,4},{4,8},{8,12},{12,16},{16,20},{20,24},{24,28},{1,5},{5,9},{9,... | collective-permute-start | bytes 1542152 | tf_op jit(solution)/shard_map/ppermute | solution.py:437
  15.1 24.3 %collective-permute-start.4 = (f32[560,128]{1,0:T(8,128)S(1)}, f32[560,128]{1,0:T(8,128)S(1)}, u32[]{:S(2)}, u32[]{:S(2)}) collective-permute-start(f32[560,128]{1,0:T(8,128)S(1)} %get-tuple-element.37), channel_id=1, source_target_pairs={{4,0},{8,4},{12,8},{16,12},{20,16},{24,20},{28,24},{5,1},{9,5},{13... | collective-permute-start | bytes 860168 | tf_op jit(solution)/shard_map/ppermute | solution.py:437
  16.4 5.4 %collective-permute-start.2 = (f32[24,128]{1,0:T(8,128)S(1)}, f32[24,128]{1,0:T(8,128)S(1)}, u32[]{:S(2)}, u32[]{:S(2)}) collective-permute-start(f32[24,128]{1,0:T(8,128)S(1)} %get-tuple-element.30), channel_id=1, source_target_pairs={{4,0},{8,4},{12,8},{16,12},{20,16},{24,20},{28,24},{5,1},{9,5},{13... | collective-permute-start | bytes 36872 | tf_op jit(solution)/shard_map/ppermute | solution.py:437

commit v4 on v3

--- a/solution.py
+++ b/solution.py
@@ -47,11 +47,33 @@
     return [(d, j, c, (n * COMPS + c) * rows) for n, (j, d) in enumerate(links) for c in range(COMPS)]
 
 
+def side_count(rows):
+    return max(len(WEST_LINKS), len(EAST_LINKS)) * COMPS * rows + SUB
+
+
+def by_parity(axis, body, first, second):
+    odd = lax.rem(lax.axis_index(axis), 2)
+
+    @pl.when(odd == 0)
+    def _():
+        body(first, second)
+
+    @pl.when(odd == 1)
+    def _():
+        body(second, first)
+
+
+def swap(array, axis, first):
+    peers = lax.axis_size(axis)
+    lower = range(first, peers - 1, 2)
+    return lax.ppermute(array, axis, [pair for i in lower for pair in ((i, i + 1), (i + 1, i))])
+
+
 def pack_cols(flat):
     rows, cols = flat.rows, flat.cols
     groups = 12 * rows // SUB
 
-    def body(here_in, there_in, outlier_in, transforms_in, points, padded, to_east, to_west, *scratch):
+    def body(here_in, there_in, outlier_in, transforms_in, points, padded, first_swap, second_swap, *scratch):
         here, there, outlier, transforms, sems = scratch
         copies = []
         for n, (source, goal) in enumerate(((here_in, here), (there_in, there), (outlier_in, outlier))):
@@ -76,26 +98,37 @@
                 for c in range(3):
                     points[d * COMPS + c, own] = here[d, c, r]
                     points[d * COMPS + 3 + c, own] = there[d, c, r]
-        for out, links, first in ((to_east, WEST_LINKS, cols - 2), (to_west, EAST_LINKS, 0)):
-            for d, j, c, at in side_rows(links, rows):
-                for r in range(rows):
-                    tile = flat.at(r, first + j)
-                    out[at + r : at + r + 1] = points[d * COMPS + c, tile : tile + 1]
+
+        def pack_points(to_east, to_west):
+            for out, links, first in ((to_east, WEST_LINKS, cols - 2), (to_west, EAST_LINKS, 0)):
+                for d, j, c, at in side_rows(links, rows):
+                    for r in range(rows):
+                        tile = flat.at(r, first + j)
+                        out[at + r : at + r + 1] = points[d * COMPS + c, tile : tile + 1]
+
+        by_parity("col", pack_points, first_swap, second_swap)
         padded[...] = jnp.zeros((12 * rows, LANES), jnp.float32)
         copies[3][0].wait()
         padded[:, 0:cols] = transforms[...]
         lane = iota((SUB, LANES), 1)
-        for out, links, first in ((to_east, WEST_LINKS, cols - 2), (to_west, EAST_LINKS, 0)):
-            packed = jnp.zeros((SUB, LANES), jnp.float32)
+        packed = []
+        for first in (cols - 2, 0):
+            value = jnp.zeros((SUB, LANES), jnp.float32)
             for g in range(groups):
                 moved = pltpu.roll(padded[g * SUB : (g + 1) * SUB], (2 * g - first) % LANES, 1)
-                packed = jnp.where((lane == 2 * g) | (lane == 2 * g + 1), moved, packed)
-            out[len(links) * COMPS * rows :] = packed
-
-    count = [len(links) * COMPS * rows + SUB for links in (WEST_LINKS, EAST_LINKS)]
+                value = jnp.where((lane == 2 * g) | (lane == 2 * g + 1), moved, value)
+            packed.append(value)
+
+        def pack_transforms(to_east, to_west):
+            to_east[side_count(rows) - SUB :] = packed[0]
+            to_west[side_count(rows) - SUB :] = packed[1]
+
+        by_parity("col", pack_transforms, first_swap, second_swap)
+
+    count = side_count(rows)
     return call(
         body,
-        [(4 * COMPS, flat.tiles, LANES), (12 * rows, LANES), (count[0], LANES), (count[1], LANES)],
+        [(4 * COMPS, flat.tiles, LANES), (12 * rows, LANES), (count, LANES), (count, LANES)],
         [
             pltpu.VMEM((4, 3, rows, cols, LANES), jnp.float32),
             pltpu.VMEM((4, 3, rows, cols, LANES), jnp.float32),
@@ -107,26 +140,6 @@
     )
 
 
-def pack_corner_rows(flat):
-    rows, cols = flat.rows, flat.cols
-
-    def body(padded, west, east, text, up_t):
-        lane = iota((SUB, LANES), 1)
-        from_west = west[len(WEST_LINKS) * COMPS * rows :]
-        from_east = east[len(EAST_LINKS) * COMPS * rows :]
-        for g in range(12 * rows // SUB):
-            part = slice(g * SUB, (g + 1) * SUB)
-            left = pltpu.roll(from_west, -2 * g % LANES, 1)
-            right = pltpu.roll(from_east, (cols + 2 - 2 * g) % LANES, 1)
-            own = pltpu.roll(padded[part], 2, 1)
-            value = jnp.where(lane < 2, left, jnp.where(lane < cols + 2, own, right))
-            text[part] = jnp.where(lane < flat.span, value, 0.0)
-        for k in range(12):
-            up_t[2 * k : 2 * k + 2] = text[k * rows : k * rows + 2]
-
-    return call(body, [(12 * rows, LANES), (24, LANES)], in_vmem=(0, 1, 2))
-
-
 def north_slices(flat):
     span, at, found = flat.span, 0, []
     for d in range(4):
@@ -140,24 +153,40 @@
 def pack_rows(flat):
     rows, cols, span = flat.rows, flat.cols, flat.span
     slices, north_t = north_slices(flat)
-
-    def body(points_in, west, east, text, points, down, up):
-        for side, links, first in ((west, WEST_LINKS, -2), (east, EAST_LINKS, cols)):
-            for d, j, c, at in side_rows(links, rows):
-                for r in range(rows):
-                    tile = flat.at(r, first + j)
-                    points[d * COMPS + c, tile : tile + 1] = side[at + r : at + r + 1]
+    south_t = 4 * COMPS * span
+
+    def body(points_in, padded, first_swap, second_swap, points, text, down, up):
+        def unpack(east, west):
+            for side, links, first in ((west, WEST_LINKS, -2), (east, EAST_LINKS, cols)):
+                for d, j, c, at in side_rows(links, rows):
+                    for r in range(rows):
+                        tile = flat.at(r, first + j)
+                        points[d * COMPS + c, tile : tile + 1] = side[at + r : at + r + 1]
+            lane = iota((SUB, LANES), 1)
+            from_west = west[side_count(rows) - SUB :]
+            from_east = east[side_count(rows) - SUB :]
+            for g in range(12 * rows // SUB):
+                part = slice(g * SUB, (g + 1) * SUB)
+                left = pltpu.roll(from_west, -2 * g % LANES, 1)
+                right = pltpu.roll(from_east, (cols + 2 - 2 * g) % LANES, 1)
+                own = pltpu.roll(padded[part], 2, 1)
+                value = jnp.where(lane < 2, left, jnp.where(lane < cols + 2, own, right))
+                text[part] = jnp.where(lane < span, value, 0.0)
+
+        by_parity("col", unpack, first_swap, second_swap)
+        for n in range(4 * COMPS):
+            up[n * span : (n + 1) * span] = points[n, flat.at(0, -2) : flat.at(0, -2) + span]
+        for k in range(12):
+            up[south_t + 2 * k : south_t + 2 * k + 2] = text[k * rows : k * rows + 2]
         for n, skip, count, to in slices:
             at = flat.at(rows - 2 + skip, -2)
             down[to : to + count] = points[n, at : at + count]
-        for n in range(4 * COMPS):
-            up[n * span : (n + 1) * span] = points[n, flat.at(0, -2) : flat.at(0, -2) + span]
         for k in range(12):
             down[north_t + 2 * k : north_t + 2 * k + 2] = text[(k + 1) * rows - 2 : (k + 1) * rows]
 
     return call(
         body,
-        [(4 * COMPS, flat.tiles, LANES), (north_t + 24, LANES), (4 * COMPS * span, LANES)],
+        [(4 * COMPS, flat.tiles, LANES), (12 * rows, LANES), (north_t + 24, LANES), (south_t + 24, LANES)],
         in_vmem=(0, 1, 2, 3),
         aliases={0: 0},
     )
@@ -265,11 +294,14 @@
 def first_stats(flat, devices):
     rows = flat.rows
 
-    def body(points, text, up_t, rep, errors, mapped, target, out):
+    south_t = 4 * COMPS * flat.span
+
+    def body(points, text, south, rep, errors, mapped, target, out):
         for k in range(12):
             for r in range(rows):
                 spread(text[k * rows + r : k * rows + r + 1], rep, k, flat.at(r, -2), flat.span)
-            spread(up_t[2 * k : 2 * k + 1], rep, k, flat.at(rows, -2), flat.span)
+            row = south_t + 2 * k
+            spread(south[row : row + 1], rep, k, flat.at(rows, -2), flat.span)
         own_stats(flat, points, rep, errors, mapped, target, flat.own_blocks(), out)
 
     t = flat.tiles
@@ -280,7 +312,7 @@
     )
 
 
-def outer_values(flat, points, rep, errors, mapped, target, north, south, up_t):
+def outer_values(flat, points, rep, errors, mapped, target, north, south):
     rows, span = flat.rows, flat.span
     slices, north_t = north_slices(flat)
     for n, skip, count, src in slices:
@@ -293,7 +325,8 @@
         for j in range(2):
             row = north_t + 2 * k + j
             spread(north[row : row + 1], rep, k, flat.at(j - 2, -2), span)
-        spread(up_t[2 * k + 1 : 2 * k + 2], rep, k, flat.at(rows + 1, -2), span)
+        row = 4 * COMPS * span + 2 * k + 1
+        spread(south[row : row + 1], rep, k, flat.at(rows + 1, -2), span)
     inner = set(flat.own_blocks())
     for f in flat.blocks(-2, -2, rows, flat.cols + 1):
         if f not in inner:
@@ -333,11 +366,7 @@
                 put(cross, (c, 3), scaled)
                 for b in range(3):
                     put(cross, (c, b), scaled * x[b])
-
-    def lanes(v):
-        return jnp.broadcast_to(jnp.sum(v, axis=1, keepdims=True), v.shape)
-
-    return {k: lanes(v) for k, v in gram.items()}, {k: lanes(v) for k, v in cross.items()}
+    return gram, cross
 
 
 def solve_small(gram, cross):
@@ -370,31 +399,53 @@
     return result
 
 
-def update(flat, blocks, points, rep, mapped, target, weights, damping, out):
-    for f in blocks:
-        gram, cross = tile_sums(flat, f, points, mapped, target, weights)
+def update(flat, blocks, points, rep, mapped, target, weights, damping):
+    group = iota((SUB, LANES), 1) // SUB
+    results = []
+    for start in range(0, len(blocks), LANES // SUB):
+        part = blocks[start : start + LANES // SUB]
+        gram, cross, old = {}, {}, {}
+        for b, f in enumerate(part):
+            keep = group == b
+
+            def place(store, key, value):
+                store[key] = value if b == 0 else jnp.where(keep, value, store[key])
+
+            sums = tile_sums(flat, f, points, mapped, target, weights)
+            for store, found in zip((gram, cross), sums):
+                for key, value in found.items():
+                    place(store, key, jnp.broadcast_to(jnp.sum(value, axis=1, keepdims=True), value.shape))
+            for k in range(12):
+                place(old, (k // 4, k % 4), rep[k, f : f + SUB])
         for a in range(4):
             gram[a, a] = gram[a, a] + damping
-        for c in range(3):
-            for b in range(4):
-                cross[c, b] = cross[c, b] + damping * rep[4 * c + b, f : f + SUB]
-        for k, value in enumerate(solve_small(gram, cross)):
-            out[k, f : f + SUB] = value
+        for key, value in old.items():
+            cross[key] = cross[key] + damping * value
+        results.append((part, solve_small(gram, cross)))
+    return results
+
+
+def replicate(results, out):
+    for part, solved in results:
+        for k, value in enumerate(solved):
+            for b, f in enumerate(part):
+                out[k, f : f + SUB] = jnp.broadcast_to(value[:, b * SUB : b * SUB + 1], (SUB, LANES))
 
 
 def first_update(flat, devices):
     rows, cols = flat.rows, flat.cols
 
     def body(*refs):
-        got, north, south, up_t = refs[5:9]
-        points, rep, errors, mapped, target, new_rep, out, weights = refs[9:]
+        got, north, south = refs[5:8]
+        points, rep, errors, mapped, target, new_rep, out, weights = refs[8:]
         state = (points, rep, errors, mapped, target)
-        outer_values(flat, *state, north, south, up_t)
+        outer_values(flat, *state, north, south)
         largest, mean_error = read_stats(got)
         scale = 0.25 * largest + 1e-06
         damping = damping_scale * mean_error + 1.0
         weigh(flat.blocks(-2, -2, rows, cols + 1), points, errors, weights, scale)
-        update(flat, flat.blocks(-1, -1, rows, cols), points, rep, mapped, target, weights, damping, new_rep)
+        blocks = flat.blocks(-1, -1, rows, cols)
+        replicate(update(flat, blocks, points, rep, mapped, target, weights, damping), new_rep)
         blocks = flat.blocks(-1, -1, rows - 1, cols)
         own_stats(flat, points, new_rep, errors, mapped, target, blocks, out)
 
@@ -403,33 +454,45 @@
         body,
         [(4 * COMPS, t, LANES)] + [(n, t, LANES) for n in (12, 4, 12, 12, 12)] + [(devices, 1, LANES)],
         [(4, t, LANES)],
-        in_vmem=range(9),
+        in_vmem=range(8),
         aliases={i: i for i in range(5)},
     )
+
+
+def take_lanes(lines, at, count):
+    pieces = []
+    while count:
+        n, lane = divmod(at, LANES)
+        size = min(count, LANES - lane)
+        pieces.append(lines[n][:, lane : lane + size])
+        at, count = at + size, count - size
+    return pieces[0] if len(pieces) == 1 else jnp.concatenate(pieces, axis=1)
 
 
 def last_update(flat):
     rows, cols = flat.rows, flat.cols
 
-    def body(got0, got1, points, rep, errors, mapped, target, aligned, stats, weights, new_rep):
+    def body(got0, got1, points, rep, errors, mapped, target, aligned, stats, weights):
         first, mean0 = read_stats(got0)
         largest, mean_error = read_stats(got1)
         scale = 0.25 * largest + 1e-06
         damping = damping_scale * mean_error + 1.0
         weigh(flat.blocks(-1, -1, rows - 1, cols), points, errors, weights, scale)
-        update(flat, flat.blocks(0, 0, rows - 1, cols - 1), points, rep, mapped, target, weights, damping, new_rep)
-        diagonal = iota((cols, LANES), 0) == iota((cols, LANES), 1)
+        results = update(flat, flat.own_blocks(), points, rep, mapped, target, weights, damping)
+        diagonal = iota((SUB, LANES), 0) == lax.rem(iota((SUB, LANES), 1), SUB)
         for k in range(12):
+            lines = []
+            for part, solved in results:
+                lines.append(jnp.sum(jnp.where(diagonal, solved[k], 0.0), axis=0, keepdims=True))
             for r in range(rows):
-                at = flat.at(r, 0)
-                value = jnp.where(diagonal, new_rep[k, at : at + cols], 0.0)
-                aligned[k, r : r + 1] = jnp.sum(value, axis=0, keepdims=True)[:, 0:cols]
+                at = flat.at(r, 0) - results[0][0][0]
+                aligned[k, r : r + 1] = take_lanes(lines, at, cols)
         row = iota((2, 2), 0)
         col = iota((2, 2), 1)
         stats[...] = jnp.where(row == 0, jnp.where(col == 0, first, largest), jnp.where(col == 0, mean0, mean_error))
 
     t = flat.tiles
-    return call(body, [(12, rows, cols), (2, 2)], [(4, t, LANES), (12, t, LANES)], in_vmem=range(7), results=None)
+    return call(body, [(12, rows, cols), (2, 2)], [(4, t, LANES)], in_vmem=range(7), results=None)
 
 
 def onward(array, axis, by):
@@ -445,20 +508,18 @@
     rows, cols = transforms.shape[2:]
     devices = lax.axis_size("row") * lax.axis_size("col")
     flat = Flat(rows, cols)
-    points, padded, to_east, to_west = pack_cols(flat)(
+    points, padded, to_first, to_second = pack_cols(flat)(
         points_here, points_there, outlier_mask, transforms.reshape(12 * rows, cols)
     )
-    west = onward(to_east, "col", 1)
-    east = onward(to_west, "col", -1)
-    text, to_up_t = pack_corner_rows(flat)(padded, west, east)
-    up_t = onward(to_up_t, "row", -1)
-    points, to_down, to_up = pack_rows(flat)(points, west, east, text)
+    first_swap = swap(to_first, "col", 0)
+    second_swap = swap(to_second, "col", 1)
+    points, text, to_down, to_up = pack_rows(flat)(points, padded, first_swap, second_swap)
+    south = onward(to_up, "row", -1)
     north = onward(to_down, "row", 1)
-    south = onward(to_up, "row", -1)
-    rep, errors, mapped, target, sent = first_stats(flat, devices)(points, text, up_t)
+    rep, errors, mapped, target, sent = first_stats(flat, devices)(points, text, south)
     got0 = everyone(sent)
     points, _, errors, mapped, target, rep, sent = first_update(flat, devices)(
-        points, rep, errors, mapped, target, got0, north, south, up_t
+        points, rep, errors, mapped, target, got0, north, south
     )
     got1 = everyone(sent)
     aligned, stats = last_update(flat)(got0, got1, points, rep, errors, mapped, target)

time: 53 us -> 50.7 us (0.957)
  blocking collectives: 25.8 us -> 30.7 us
  starting transfers between devices: 10.2 us -> 6.39 us
  waiting for transfers between devices: 9.09 us -> 6.17 us
  Pallas kernels: 6.99 us -> 6.45 us
    ppermute x5 -> x2, starting transfers between devices: 10.2 us -> 2.61 us  [onward(): lax.ppermute(array, axis, [(i, i + by) for i in range(peers) if 0 <= i +...]
    all_to_all x2, blocking collectives: 25.8 us -> 30.7 us  [everyone(): return lax.all_to_all(array, ('row', 'col'), 0, 0)]
    ppermute x5 -> x2, waiting for transfers between devices: 9.09 us -> 4.21 us  [onward(): lax.ppermute(array, axis, [(i, i + by) for i in range(peers) if 0 <= i +...]
    ppermute x0 -> x2, starting transfers between devices: none -> 3.77 us  [swap(): lax.ppermute(array, axis, [pair for i in lower for pair in ((i, i + 1), (...]
    ppermute x0 -> x2, waiting for transfers between devices: none -> 1.96 us  [swap(): lax.ppermute(array, axis, [pair for i in lower for pair in ((i, i + 1), (...]
    pallas_call x6 -> x5, Pallas kernels: 6.99 us -> 6.45 us  [run(): pl.pallas_call(body, out_shape=shapes, in_specs=[hbm if i in in_hbm else...]
  transfers between devices with their start and end apart: 5 -> 4, of which waited for: 2 -> 2; matrix products, arithmetic and copies ran while one was open for 0% -> 0% of each run, Pallas kernels for 1% -> 1%
where the time goes in v4:
time: 50.7 us; the launch traced here: 50.4 us
  blocking collectives  30.7 us (61%)
  Pallas kernels  6.45 us (13%)
  starting transfers between devices  6.39 us (13%)
  waiting for transfers between devices  6.17 us (12%)
  between operations  0.69 us (1%)
    all_to_all x2, blocking collectives, everyone(): return lax.all_to_all(array, ('row', 'col'), 0, 0)  30.7 us
    pallas_call x5, Pallas kernels, run(): pl.pallas_call(body, out_shape=shapes, in_specs=[hbm if i in in_hbm else...  6.45 us
    ppermute x2, waiting for transfers between devices, onward(): lax.ppermute(array, axis, [(i, i + by) for i in range(peers) if 0 <= i +...  4.21 us
    ppermute x2, starting transfers between devices, swap(): lax.ppermute(array, axis, [pair for i in lower for pair in ((i, i + 1), (...  3.77 us
    ppermute x2, starting transfers between devices, onward(): lax.ppermute(array, axis, [(i, i + by) for i in range(peers) if 0 <= i +...  2.61 us
    ppermute x2, waiting for transfers between devices, swap(): lax.ppermute(array, axis, [pair for i in lower for pair in ((i, i + 1), (...  1.96 us
  transfers between devices with their start and end apart: 4, of which 2 were waited for; matrix products, arithmetic and copies ran while one was open for 0% of the time, Pallas kernels for 1%

profile of v4, /device:TPU:0, one launch (start us, length us, event | category | flops | bytes accessed | tf_op | source)
XLA Modules:
  0.0 50.4 jit_solution(5390592765360160948)
XLA Ops:
  0.6 1.6 %shard_map.59 = (f32[28,200,128]{2,1,0:T(8,128)S(1)}, f32[48,128]{1,0:T(8,128)S(1)}, f32[176,128]{1,0:T(8,128)S(1)}, f32[176,128]{1,0:T(8,128)S(1)}) custom-call(f32[4,3,4,16,128]{4,3,2,1,0:T(8,128)} %here_in.1, f32[4,3,4,16,128]{4,3,2,1,0:T(8,128)} %there_in.1, s32[4,4,16,128]{3,2,1,0:T(8,128)} %outlier_in.1, f32[48,16]{1,0:T(8,128)} %bitcast.2), custom_call_target="tpu_custom_call" | custom-call | tf_op jit(solution)/shard_map/pallas_call | solution.py:25
  2.2 3.1 %collective-permute-start = (f32[176,128]{1,0:T(8,128)S(1)}, f32[176,128]{1,0:T(8,128)S(1)}, u32[]{:S(2)}, u32[]{:S(2)}) collective-permute-start(f32[176,128]{1,0:T(8,128)S(1)} %get-tuple-element.25), channel_id=1, source_target_pairs={{0,1},{1,0},{2,3},{3,2},{4,5},{5,4},{6,7},{7,6},{8,9},{9,8},{10,11... | collective-permute-start | bytes 270344 | tf_op jit(solution)/shard_map/ppermute | solution.py:69
  5.4 0.7 %collective-permute-start.1 = (f32[176,128]{1,0:T(8,128)S(1)}, f32[176,128]{1,0:T(8,128)S(1)}, u32[]{:S(2)}, u32[]{:S(2)}) collective-permute-start(f32[176,128]{1,0:T(8,128)S(1)} %get-tuple-element.26), channel_id=1, source_target_pairs={{1,2},{2,1},{5,6},{6,5},{9,10},{10,9},{13,14},{14,13},{17,18},{18,... | collective-permute-start | bytes 270344 | tf_op jit(solution)/shard_map/ppermute | solution.py:69
  6.0 2.0 %collective-permute-done.first_swap = f32[176,128]{1,0:T(8,128)S(1)} collective-permute-done((f32[176,128]{1,0:T(8,128)S(1)}, f32[176,128]{1,0:T(8,128)S(1)}, u32[]{:S(2)}, u32[]{:S(2)}) %collective-permute-start) | collective-permute-done | bytes 90144 | tf_op jit(solution)/shard_map/ppermute | solution.py:69
  8.0 0.0 collective-permute-done.1.second_swap
  8.0 0.2 shard_map.60
  8.2 1.3 %collective-permute-start.3 = (f32[1004,128]{1,0:T(8,128)S(1)}, f32[1004,128]{1,0:T(8,128)S(1)}, u32[]{:S(2)}, u32[]{:S(2)}) collective-permute-start(f32[1004,128]{1,0:T(8,128)S(1)} %get-tuple-element.35), channel_id=1, source_target_pairs={{0,4},{4,8},{8,12},{12,16},{16,20},{20,24},{24,28},{1,5},{5,9},{9,... | collective-permute-start | bytes 1542152 | tf_op jit(solution)/shard_map/ppermute | solution.py:500
  9.5 1.3 %collective-permute-start.2 = (f32[584,128]{1,0:T(8,128)S(1)}, f32[584,128]{1,0:T(8,128)S(1)}, u32[]{:S(2)}, u32[]{:S(2)}) collective-permute-start(f32[584,128]{1,0:T(8,128)S(1)} %get-tuple-element.29), channel_id=1, source_target_pairs={{4,0},{8,4},{12,8},{16,12},{20,16},{24,20},{28,24},{5,1},{9,5},{13... | collective-permute-start | bytes 897032 | tf_op jit(solution)/shard_map/ppermute | solution.py:500
  10.8 4.2 %collective-permute-done.2.south.refs_7_ = f32[584,128]{1,0:T(8,128)S(1)} collective-permute-done((f32[584,128]{1,0:T(8,128)S(1)}, f32[584,128]{1,0:T(8,128)S(1)}, u32[]{:S(2)}, u32[]{:S(2)}) %collective-permute-start.2) | collective-permute-done | bytes 299040 | tf_op jit(solution)/shard_map/ppermute | solution.py:500
  15.0 0.6 %shard_map.61 = (f32[12,200,128]{2,1,0:T(8,128)S(1)}, f32[4,200,128]{2,1,0:T(8,128)S(1)}, f32[12,200,128]{2,1,0:T(8,128)S(1)}, f32[12,200,128]{2,1,0:T(8,128)S(1)}, f32[32,1,128]{2,1,0:T(1,128)S(1)}) custom-call(f32[28,200,128]{2,1,0:T(8,128)S(1)} %get-tuple-element.27.points.refs_0_, f32[48,128]{1,0:T(8,128)S(1)} %get-tuple-element.28.text, ...), custom_call_target="tpu_custom_call" | custom-call | tf_op jit(solution)/shard_map/pallas_call | solution.py:25
  15.6 21.8 %all_to_all.10.refs_5_.got0 = f32[32,1,128]{2,1,0:T(1,128)S(1)} all-to-all(f32[32,1,128]{2,1,0:T(1,128)S(1)} %get-tuple-element.30), channel_id=1, replica_groups=mesh['row'=8,'col'=4] {'row','col'}, dimensions={0} | all-to-all | bytes 32768 | tf_op jit(solution)/shard_map/all_to_all | solution.py:504
  37.5 0.0 collective-permute-done.3.refs_6_
  37.5 2.3 %shard_map.62 = (f32[28,200,128]{2,1,0:T(8,128)S(1)}, f32[12,200,128]{2,1,0:T(8,128)S(1)}, f32[4,200,128]{2,1,0:T(8,128)S(1)}, f32[12,200,128]{2,1,0:T(8,128)S(1...) custom-call(f32[28,200,128]{2,1,0:T(8,128)S(1)} %get-tuple-element.2, ...), custom_call_target="tpu_custom_call", output_to_operand_aliasing={{0}: (0, {}), {1}: (1, {}), {2}: (2, {}), {3}: (3, {}), {4}... | custom-call | tf_op jit(solution)/shard_map/pallas_call | solution.py:25
  39.8 8.9 %all_to_all.11.got1 = f32[32,1,128]{2,1,0:T(1,128)S(1)} all-to-all(f32[32,1,128]{2,1,0:T(1,128)S(1)} %get-tuple-element.36), channel_id=1, replica_groups=mesh['row'=8,'col'=4] {'row','col'}, dimensions={0} | all-to-all | bytes 32768 | tf_op jit(solution)/shard_map/all_to_all | solution.py:504
  48.7 1.7 %shard_map.63 = (f32[12,4,16]{2,1,0:T(4,128)}, f32[2,2]{1,0:T(2,128)}) custom-call(f32[32,1,128]{2,1,0:T(1,128)S(1)} %all_to_all.10.refs_5_.got0, f32[32,1,128]{2,1,0:T(1,128)S(1)} %all_to_all.11.got1, f32[28,200,128]{2,1,0:T(8,128)S(1)} %get-tuple-element.37.points, f32[12,200,128]{2,1,0:T(8,128)S(1)} %get-tuple-element.38.rep, ...), custom_call_target="tpu_custom_call" | custom-call | tf_op jit(solution)/shard_map/pallas_call | solution.py:25
Async XLA Ops:
  2.2 5.7 %collective-permute-start = (f32[176,128]{1,0:T(8,128)S(1)}, f32[176,128]{1,0:T(8,128)S(1)}, u32[]{:S(2)}, u32[]{:S(2)}) collective-permute-start(f32[176,128]{1,0:T(8,128)S(1)} %get-tuple-element.25), channel_id=1, source_target_pairs={{0,1},{1,0},{2,3},{3,2},{4,5},{5,4},{6,7},{7,6},{8,9},{9,8},{10,11... | collective-permute-start | bytes 270344 | tf_op jit(solution)/shard_map/ppermute | solution.py:69
  5.4 2.6 %collective-permute-start.1 = (f32[176,128]{1,0:T(8,128)S(1)}, f32[176,128]{1,0:T(8,128)S(1)}, u32[]{:S(2)}, u32[]{:S(2)}) collective-permute-start(f32[176,128]{1,0:T(8,128)S(1)} %get-tuple-element.26), channel_id=1, source_target_pairs={{1,2},{2,1},{5,6},{6,5},{9,10},{10,9},{13,14},{14,13},{17,18},{18,... | collective-permute-start | bytes 270344 | tf_op jit(solution)/shard_map/ppermute | solution.py:69
  8.2 29.3 %collective-permute-start.3 = (f32[1004,128]{1,0:T(8,128)S(1)}, f32[1004,128]{1,0:T(8,128)S(1)}, u32[]{:S(2)}, u32[]{:S(2)}) collective-permute-start(f32[1004,128]{1,0:T(8,128)S(1)} %get-tuple-element.35), channel_id=1, source_target_pairs={{0,4},{4,8},{8,12},{12,16},{16,20},{20,24},{24,28},{1,5},{5,9},{9,... | collective-permute-start | bytes 1542152 | tf_op jit(solution)/shard_map/ppermute | solution.py:500
  9.5 5.5 %collective-permute-start.2 = (f32[584,128]{1,0:T(8,128)S(1)}, f32[584,128]{1,0:T(8,128)S(1)}, u32[]{:S(2)}, u32[]{:S(2)}) collective-permute-start(f32[584,128]{1,0:T(8,128)S(1)} %get-tuple-element.29), channel_id=1, source_target_pairs={{4,0},{8,4},{12,8},{16,12},{20,16},{24,20},{28,24},{5,1},{9,5},{13... | collective-permute-start | bytes 897032 | tf_op jit(solution)/shard_map/ppermute | solution.py:500

commit v5 on v4

--- a/solution.py
+++ b/solution.py
@@ -109,13 +109,13 @@
         by_parity("col", pack_points, first_swap, second_swap)
         padded[...] = jnp.zeros((12 * rows, LANES), jnp.float32)
         copies[3][0].wait()
-        padded[:, 0:cols] = transforms[...]
+        padded[:, 2 : cols + 2] = transforms[...]
         lane = iota((SUB, LANES), 1)
         packed = []
         for first in (cols - 2, 0):
             value = jnp.zeros((SUB, LANES), jnp.float32)
             for g in range(groups):
-                moved = pltpu.roll(padded[g * SUB : (g + 1) * SUB], (2 * g - first) % LANES, 1)
+                moved = pltpu.roll(padded[g * SUB : (g + 1) * SUB], (2 * g - first - 2) % LANES, 1)
                 value = jnp.where((lane == 2 * g) | (lane == 2 * g + 1), moved, value)
             packed.append(value)
 
@@ -169,8 +169,7 @@
                 part = slice(g * SUB, (g + 1) * SUB)
                 left = pltpu.roll(from_west, -2 * g % LANES, 1)
                 right = pltpu.roll(from_east, (cols + 2 - 2 * g) % LANES, 1)
-                own = pltpu.roll(padded[part], 2, 1)
-                value = jnp.where(lane < 2, left, jnp.where(lane < cols + 2, own, right))
+                value = jnp.where(lane < 2, left, jnp.where(lane < cols + 2, padded[part], right))
                 text[part] = jnp.where(lane < span, value, 0.0)
 
         by_parity("col", unpack, first_swap, second_swap)
@@ -243,13 +242,14 @@
         return range(self.at(r0, c0) // SUB * SUB, self.at(r1, c1) + 1, SUB)
 
     def own_blocks(self):
-        return self.blocks(0, 0, self.rows - 1, self.cols - 1)
-
-    def owned(self, f):
+        return self.blocks(0, 0, self.rows - 1, self.cols)
+
+    def counted(self, f, d):
         index = iota((SUB, LANES), 0) + f
         keep = None
         for r in range(self.rows):
-            low, high = self.at(r, 0), self.at(r, self.cols - 1)
+            dc = link_offsets[d][1] if d >= 2 and r == self.rows - 1 else 0
+            low, high = self.at(r, 0 - dc), self.at(r, self.cols - 1 - dc)
             if low <= f and f + SUB - 1 <= high:
                 return True
             if low < f + SUB and high >= f:
@@ -275,8 +275,8 @@
     zero = jnp.zeros((SUB, LANES), jnp.float32)
     top, total, count = zero, zero, zero
     for f in blocks:
-        keep = flat.owned(f)
         for d in range(4):
+            keep = flat.counted(f, d)
             error = link_values(flat, f, d, points, rep, errors, mapped, target)
             if keep is None:
                 continue
@@ -294,14 +294,12 @@
 def first_stats(flat, devices):
     rows = flat.rows
 
-    south_t = 4 * COMPS * flat.span
 
     def body(points, text, south, rep, errors, mapped, target, out):
         for k in range(12):
             for r in range(rows):
                 spread(text[k * rows + r : k * rows + r + 1], rep, k, flat.at(r, -2), flat.span)
-            row = south_t + 2 * k
-            spread(south[row : row + 1], rep, k, flat.at(rows, -2), flat.span)
+            spread(south[k * rows : k * rows + 1], rep, k, flat.at(rows, -2), flat.span)
         own_stats(flat, points, rep, errors, mapped, target, flat.own_blocks(), out)
 
     t = flat.tiles
@@ -325,9 +323,9 @@
         for j in range(2):
             row = north_t + 2 * k + j
             spread(north[row : row + 1], rep, k, flat.at(j - 2, -2), span)
-        row = 4 * COMPS * span + 2 * k + 1
-        spread(south[row : row + 1], rep, k, flat.at(rows + 1, -2), span)
-    inner = set(flat.own_blocks())
+            row = 4 * COMPS * span + 2 * k + j
+            spread(south[row : row + 1], rep, k, flat.at(rows + j, -2), span)
+    inner = set(f for f in flat.own_blocks() if f + SUB <= flat.at(rows - 1, -2))
     for f in flat.blocks(-2, -2, rows, flat.cols + 1):
         if f not in inner:
             for d in range(4):
@@ -513,10 +511,11 @@
     )
     first_swap = swap(to_first, "col", 0)
     second_swap = swap(to_second, "col", 1)
+    below = onward(padded, "row", -1)
     points, text, to_down, to_up = pack_rows(flat)(points, padded, first_swap, second_swap)
     south = onward(to_up, "row", -1)
     north = onward(to_down, "row", 1)
-    rep, errors, mapped, target, sent = first_stats(flat, devices)(points, text, south)
+    rep, errors, mapped, target, sent = first_stats(flat, devices)(points, text, below)
     got0 = everyone(sent)
     points, _, errors, mapped, target, rep, sent = first_update(flat, devices)(
         points, rep, errors, mapped, target, got0, north, south

time: 50.7 us -> 51.2 us (level)
  starting transfers between devices: 6.39 us -> 7.68 us
  blocking collectives: 30.7 us -> 29.5 us
    ppermute x2 -> x3, starting transfers between devices: 2.61 us -> 3.91 us  [onward(): lax.ppermute(array, axis, [(i, i + by) for i in range(peers) if 0 <= i +...]
    all_to_all x2, blocking collectives: 30.7 us -> 29.5 us  [everyone(): return lax.all_to_all(array, ('row', 'col'), 0, 0)]
    ppermute x2 -> x3, waiting for transfers between devices: 4.21 us -> 4.45 us  [onward(): lax.ppermute(array, axis, [(i, i + by) for i in range(peers) if 0 <= i +...]
  transfers between devices with their start and end apart: 4 -> 5, of which waited for: 2 -> 2; matrix products, arithmetic and copies ran while one was open for 0% -> 0% of each run, Pallas kernels for 1% -> 1%
where the time goes in v5:
time: 51.2 us; the launch traced here: 51 us
  blocking collectives  29.5 us (58%)
  starting transfers between devices  7.68 us (15%)
  Pallas kernels  6.71 us (13%)
  waiting for transfers between devices  6.41 us (13%)
  between operations  0.7 us (1%)
    all_to_all x2, blocking collectives, everyone(): return lax.all_to_all(array, ('row', 'col'), 0, 0)  29.5 us
    pallas_call x5, Pallas kernels, run(): pl.pallas_call(body, out_shape=shapes, in_specs=[hbm if i in in_hbm else...  6.71 us
    ppermute x3, waiting for transfers between devices, onward(): lax.ppermute(array, axis, [(i, i + by) for i in range(peers) if 0 <= i +...  4.45 us
    ppermute x3, starting transfers between devices, onward(): lax.ppermute(array, axis, [(i, i + by) for i in range(peers) if 0 <= i +...  3.91 us
    ppermute x2, starting transfers between devices, swap(): lax.ppermute(array, axis, [pair for i in lower for pair in ((i, i + 1), (...  3.77 us
    ppermute x2, waiting for transfers between devices, swap(): lax.ppermute(array, axis, [pair for i in lower for pair in ((i, i + 1), (...  1.96 us
  transfers between devices with their start and end apart: 5, of which 2 were waited for; matrix products, arithmetic and copies ran while one was open for 0% of the time, Pallas kernels for 1%

profile of v5, /device:TPU:0, one launch (start us, length us, event | category | flops | bytes accessed | tf_op | source)
XLA Modules:
  0.0 51.0 jit_solution(8726275292988564890)
XLA Ops:
  0.6 1.7 %shard_map.59 = (f32[28,200,128]{2,1,0:T(8,128)S(1)}, f32[48,128]{1,0:T(8,128)S(1)}, f32[176,128]{1,0:T(8,128)S(1)}, f32[176,128]{1,0:T(8,128)S(1)}) custom-call(f32[4,3,4,16,128]{4,3,2,1,0:T(8,128)} %here_in.1, f32[4,3,4,16,128]{4,3,2,1,0:T(8,128)} %there_in.1, s32[4,4,16,128]{3,2,1,0:T(8,128)} %outlier_in.1, f32[48,16]{1,0:T(8,128)} %bitcast.2), custom_call_target="tpu_custom_call" | custom-call | tf_op jit(solution)/shard_map/pallas_call | solution.py:25
  2.3 3.1 %collective-permute-start = (f32[176,128]{1,0:T(8,128)S(1)}, f32[176,128]{1,0:T(8,128)S(1)}, u32[]{:S(2)}, u32[]{:S(2)}) collective-permute-start(f32[176,128]{1,0:T(8,128)S(1)} %get-tuple-element.25), channel_id=1, source_target_pairs={{0,1},{1,0},{2,3},{3,2},{4,5},{5,4},{6,7},{7,6},{8,9},{9,8},{10,11... | collective-permute-start | bytes 270344 | tf_op jit(solution)/shard_map/ppermute | solution.py:69
  5.4 0.7 %collective-permute-start.1 = (f32[176,128]{1,0:T(8,128)S(1)}, f32[176,128]{1,0:T(8,128)S(1)}, u32[]{:S(2)}, u32[]{:S(2)}) collective-permute-start(f32[176,128]{1,0:T(8,128)S(1)} %get-tuple-element.26), channel_id=1, source_target_pairs={{1,2},{2,1},{5,6},{6,5},{9,10},{10,9},{13,14},{14,13},{17,18},{18,... | collective-permute-start | bytes 270344 | tf_op jit(solution)/shard_map/ppermute | solution.py:69
  6.1 2.0 %collective-permute-done.first_swap = f32[176,128]{1,0:T(8,128)S(1)} collective-permute-done((f32[176,128]{1,0:T(8,128)S(1)}, f32[176,128]{1,0:T(8,128)S(1)}, u32[]{:S(2)}, u32[]{:S(2)}) %collective-permute-start) | collective-permute-done | bytes 90144 | tf_op jit(solution)/shard_map/ppermute | solution.py:69
  8.0 0.0 collective-permute-done.1.second_swap
  8.0 0.2 shard_map.60
  8.2 1.3 %collective-permute-start.3 = (f32[1004,128]{1,0:T(8,128)S(1)}, f32[1004,128]{1,0:T(8,128)S(1)}, u32[]{:S(2)}, u32[]{:S(2)}) collective-permute-start(f32[1004,128]{1,0:T(8,128)S(1)} %get-tuple-element.34), channel_id=1, source_target_pairs={{0,4},{4,8},{8,12},{12,16},{16,20},{20,24},{24,28},{1,5},{5,9},{9,... | collective-permute-start | bytes 1542152 | tf_op jit(solution)/shard_map/ppermute | solution.py:498
  9.6 1.3 %collective-permute-start.4 = (f32[584,128]{1,0:T(8,128)S(1)}, f32[584,128]{1,0:T(8,128)S(1)}, u32[]{:S(2)}, u32[]{:S(2)}) collective-permute-start(f32[584,128]{1,0:T(8,128)S(1)} %get-tuple-element.35), channel_id=1, source_target_pairs={{4,0},{8,4},{12,8},{16,12},{20,16},{24,20},{28,24},{5,1},{9,5},{13... | collective-permute-start | bytes 897032 | tf_op jit(solution)/shard_map/ppermute | solution.py:498
  10.9 1.3 %collective-permute-start.2 = (f32[48,128]{1,0:T(8,128)S(1)}, f32[48,128]{1,0:T(8,128)S(1)}, u32[]{:S(2)}, u32[]{:S(2)}) collective-permute-start(f32[48,128]{1,0:T(8,128)S(1)} %get-tuple-element.24.padded), channel_id=1, source_target_pairs={{4,0},{8,4},{12,8},{16,12},{20,16},{24,20},{28,24},{5,1},{9,5},{13... | collective-permute-start | bytes 73736 | tf_op jit(solution)/shard_map/ppermute | solution.py:498
  12.2 4.4 %collective-permute-done.2.south = f32[48,128]{1,0:T(8,128)S(1)} collective-permute-done((f32[48,128]{1,0:T(8,128)S(1)}, f32[48,128]{1,0:T(8,128)S(1)}, u32[]{:S(2)}, u32[]{:S(2)}) %collective-permute-start.2) | collective-permute-done | bytes 24608 | tf_op jit(solution)/shard_map/ppermute | solution.py:498
  16.6 0.6 %shard_map.61 = (f32[12,200,128]{2,1,0:T(8,128)S(1)}, f32[4,200,128]{2,1,0:T(8,128)S(1)}, f32[12,200,128]{2,1,0:T(8,128)S(1)}, f32[12,200,128]{2,1,0:T(8,128)S(1)}, f32[32,1,128]{2,1,0:T(1,128)S(1)}) custom-call(f32[28,200,128]{2,1,0:T(8,128)S(1)} %get-tuple-element.27.points.refs_0_, f32[48,128]{1,0:T(8,128)S(1)} %get-tuple-element.28.text, ...), custom_call_target="tpu_custom_call" | custom-call | tf_op jit(solution)/shard_map/pallas_call | solution.py:25
  17.3 20.6 %all_to_all.10.refs_5_.got0 = f32[32,1,128]{2,1,0:T(1,128)S(1)} all-to-all(f32[32,1,128]{2,1,0:T(1,128)S(1)} %get-tuple-element.29), channel_id=1, replica_groups=mesh['row'=8,'col'=4] {'row','col'}, dimensions={0} | all-to-all | bytes 32768 | tf_op jit(solution)/shard_map/all_to_all | solution.py:502
  37.8 0.0 collective-permute-done.4.refs_7_
  37.8 0.0 collective-permute-done.3.refs_6_
  37.8 2.5 %shard_map.62 = (f32[28,200,128]{2,1,0:T(8,128)S(1)}, f32[12,200,128]{2,1,0:T(8,128)S(1)}, f32[4,200,128]{2,1,0:T(8,128)S(1)}, f32[12,200,128]{2,1,0:T(8,128)S(1...) custom-call(f32[28,200,128]{2,1,0:T(8,128)S(1)} %get-tuple-element.2, ...), custom_call_target="tpu_custom_call", output_to_operand_aliasing={{0}: (0, {}), {1}: (1, {}), {2}: (2, {}), {3}: (3, {}), {4}... | custom-call | tf_op jit(solution)/shard_map/pallas_call | solution.py:25
  40.3 8.9 %all_to_all.11.got1 = f32[32,1,128]{2,1,0:T(1,128)S(1)} all-to-all(f32[32,1,128]{2,1,0:T(1,128)S(1)} %get-tuple-element.36), channel_id=1, replica_groups=mesh['row'=8,'col'=4] {'row','col'}, dimensions={0} | all-to-all | bytes 32768 | tf_op jit(solution)/shard_map/all_to_all | solution.py:502
  49.2 1.7 %shard_map.63 = (f32[12,4,16]{2,1,0:T(4,128)}, f32[2,2]{1,0:T(2,128)}) custom-call(f32[32,1,128]{2,1,0:T(1,128)S(1)} %all_to_all.10.refs_5_.got0, f32[32,1,128]{2,1,0:T(1,128)S(1)} %all_to_all.11.got1, f32[28,200,128]{2,1,0:T(8,128)S(1)} %get-tuple-element.37.points, f32[12,200,128]{2,1,0:T(8,128)S(1)} %get-tuple-element.38.rep, ...), custom_call_target="tpu_custom_call" | custom-call | tf_op jit(solution)/shard_map/pallas_call | solution.py:25
Async XLA Ops:
  2.3 5.7 %collective-permute-start = (f32[176,128]{1,0:T(8,128)S(1)}, f32[176,128]{1,0:T(8,128)S(1)}, u32[]{:S(2)}, u32[]{:S(2)}) collective-permute-start(f32[176,128]{1,0:T(8,128)S(1)} %get-tuple-element.25), channel_id=1, source_target_pairs={{0,1},{1,0},{2,3},{3,2},{4,5},{5,4},{6,7},{7,6},{8,9},{9,8},{10,11... | collective-permute-start | bytes 270344 | tf_op jit(solution)/shard_map/ppermute | solution.py:69
  5.4 2.6 %collective-permute-start.1 = (f32[176,128]{1,0:T(8,128)S(1)}, f32[176,128]{1,0:T(8,128)S(1)}, u32[]{:S(2)}, u32[]{:S(2)}) collective-permute-start(f32[176,128]{1,0:T(8,128)S(1)} %get-tuple-element.26), channel_id=1, source_target_pairs={{1,2},{2,1},{5,6},{6,5},{9,10},{10,9},{13,14},{14,13},{17,18},{18,... | collective-permute-start | bytes 270344 | tf_op jit(solution)/shard_map/ppermute | solution.py:69
  8.2 29.6 %collective-permute-start.3 = (f32[1004,128]{1,0:T(8,128)S(1)}, f32[1004,128]{1,0:T(8,128)S(1)}, u32[]{:S(2)}, u32[]{:S(2)}) collective-permute-start(f32[1004,128]{1,0:T(8,128)S(1)} %get-tuple-element.34), channel_id=1, source_target_pairs={{0,4},{4,8},{8,12},{12,16},{16,20},{20,24},{24,28},{1,5},{5,9},{9,... | collective-permute-start | bytes 1542152 | tf_op jit(solution)/shard_map/ppermute | solution.py:498
  9.6 28.3 %collective-permute-start.4 = (f32[584,128]{1,0:T(8,128)S(1)}, f32[584,128]{1,0:T(8,128)S(1)}, u32[]{:S(2)}, u32[]{:S(2)}) collective-permute-start(f32[584,128]{1,0:T(8,128)S(1)} %get-tuple-element.35), channel_id=1, source_target_pairs={{4,0},{8,4},{12,8},{16,12},{20,16},{24,20},{28,24},{5,1},{9,5},{13... | collective-permute-start | bytes 897032 | tf_op jit(solution)/shard_map/ppermute | solution.py:498
  10.9 5.7 %collective-permute-start.2 = (f32[48,128]{1,0:T(8,128)S(1)}, f32[48,128]{1,0:T(8,128)S(1)}, u32[]{:S(2)}, u32[]{:S(2)}) collective-permute-start(f32[48,128]{1,0:T(8,128)S(1)} %get-tuple-element.24.padded), channel_id=1, source_target_pairs={{4,0},{8,4},{12,8},{16,12},{20,16},{24,20},{28,24},{5,1},{9,5},{13... | collective-permute-start | bytes 73736 | tf_op jit(solution)/shard_map/ppermute | solution.py:498

commit v6 on v5

--- a/solution.py
+++ b/solution.py
@@ -73,16 +73,33 @@
     rows, cols = flat.rows, flat.cols
     groups = 12 * rows // SUB
 
-    def body(here_in, there_in, outlier_in, transforms_in, points, padded, first_swap, second_swap, *scratch):
+    def body(here_in, there_in, outlier_in, transforms_in, points, padded, first_swap, second_swap, far, *scratch):
         here, there, outlier, transforms, sems = scratch
         copies = []
         for n, (source, goal) in enumerate(((here_in, here), (there_in, there), (outlier_in, outlier))):
             copies.append([pltpu.make_async_copy(source.at[d], goal.at[d], sems.at[n, d]) for d in range(4)])
-        copies.append([pltpu.make_async_copy(transforms_in, transforms, sems.at[3, 0])])
+        maps = pltpu.make_async_copy(transforms_in, transforms, sems.at[3, 0])
+        maps.start()
         for d in range(4):
             for n in range(3):
                 copies[n][d].start()
-        copies[3][0].start()
+        padded[...] = jnp.zeros((12 * rows, LANES), jnp.float32)
+        maps.wait()
+        padded[:, 2 : cols + 2] = transforms[...]
+        lane = iota((SUB, LANES), 1)
+        packed = []
+        for first in (cols - 2, 0):
+            value = jnp.zeros((SUB, LANES), jnp.float32)
+            for g in range(groups):
+                moved = pltpu.roll(padded[g * SUB : (g + 1) * SUB], (2 * g - first - 2) % LANES, 1)
+                value = jnp.where((lane == 2 * g) | (lane == 2 * g + 1), moved, value)
+            packed.append(value)
+
+        def pack_transforms(to_east, to_west):
+            to_east[side_count(rows) - SUB :] = packed[0]
+            to_west[side_count(rows) - SUB :] = packed[1]
+
+        by_parity("col", pack_transforms, first_swap, second_swap)
         grid_rows = rows * lax.axis_size("row")
         grid_cols = cols * lax.axis_size("col")
         row0 = lax.axis_index("row") * rows
@@ -99,36 +116,28 @@
                     points[d * COMPS + c, own] = here[d, c, r]
                     points[d * COMPS + 3 + c, own] = there[d, c, r]
 
-        def pack_points(to_east, to_west):
-            for out, links, first in ((to_east, WEST_LINKS, cols - 2), (to_west, EAST_LINKS, 0)):
-                for d, j, c, at in side_rows(links, rows):
-                    for r in range(rows):
-                        tile = flat.at(r, first + j)
-                        out[at + r : at + r + 1] = points[d * COMPS + c, tile : tile + 1]
-
-        by_parity("col", pack_points, first_swap, second_swap)
-        padded[...] = jnp.zeros((12 * rows, LANES), jnp.float32)
-        copies[3][0].wait()
-        padded[:, 2 : cols + 2] = transforms[...]
-        lane = iota((SUB, LANES), 1)
-        packed = []
-        for first in (cols - 2, 0):
-            value = jnp.zeros((SUB, LANES), jnp.float32)
-            for g in range(groups):
-                moved = pltpu.roll(padded[g * SUB : (g + 1) * SUB], (2 * g - first - 2) % LANES, 1)
-                value = jnp.where((lane == 2 * g) | (lane == 2 * g + 1), moved, value)
-            packed.append(value)
-
-        def pack_transforms(to_east, to_west):
-            to_east[side_count(rows) - SUB :] = packed[0]
-            to_west[side_count(rows) - SUB :] = packed[1]
-
-        by_parity("col", pack_transforms, first_swap, second_swap)
+            def pack_points(to_east, to_west):
+                for out, links, first in ((to_east, WEST_LINKS, cols - 2), (to_west, EAST_LINKS, 0)):
+                    for link, j, c, at in side_rows(links, rows):
+                        for r in range(rows if link == d else 0):
+                            tile = flat.at(r, first + j)
+                            out[at + r : at + r + 1] = points[d * COMPS + c, tile : tile + 1]
+
+            by_parity("col", pack_points, first_swap, second_swap)
+            for c in range(COMPS if d else 0):
+                n = (d - 1) * COMPS + c
+                far[n * cols : (n + 1) * cols] = points[d * COMPS + c, run_of(flat, rows - 2, 0, cols - 1)]
 
     count = side_count(rows)
     return call(
         body,
-        [(4 * COMPS, flat.tiles, LANES), (12 * rows, LANES), (count, LANES), (count, LANES)],
+        [
+            (4 * COMPS, flat.tiles, LANES),
+            (12 * rows, LANES),
+            (count, LANES),
+            (count, LANES),
+            (3 * COMPS * cols, LANES),
+        ],
         [
             pltpu.VMEM((4, 3, rows, cols, LANES), jnp.float32),
             pltpu.VMEM((4, 3, rows, cols, LANES), jnp.float32),
@@ -140,22 +149,33 @@
     )
 
 
-def north_slices(flat):
-    span, at, found = flat.span, 0, []
-    for d in range(4):
-        for c in range(COMPS):
-            count = 1 if d == 0 else 2
-            found.append((d * COMPS + c, 2 - count, count * span, at))
-            at += count * span
-    return found, at
+def row_message(flat):
+    last = flat.cols
+    near = {0: (-2, last), 1: (-1, last), 2: (-2, last), 3: (-1, last + 1)}
+    down = [(d, -1) + near[d] for d in range(4)]
+    down += [(1, -2, -1, -1), (1, -2, last, last), (2, -2, -2, -1), (3, -2, last, last + 1)]
+    up = [(d, flat.rows, -2 if d == 0 else -1, last) for d in range(4)]
+    lists, most = [], 0
+    for runs in (down, up):
+        found, at = [], 0
+        for d, r, c0, c1 in runs:
+            for c in range(COMPS):
+                found.append((d * COMPS + c, r, c0, c1, at))
+                at += c1 - c0 + 1
+        lists.append(found)
+        most = max(most, at)
+    return lists[0], lists[1], -(-most // SUB) * SUB
+
+
+def run_of(flat, r, c0, c1):
+    return slice(flat.at(r, c0), flat.at(r, c1) + 1)
 
 
 def pack_rows(flat):
     rows, cols, span = flat.rows, flat.cols, flat.span
-    slices, north_t = north_slices(flat)
-    south_t = 4 * COMPS * span
-
-    def body(points_in, padded, first_swap, second_swap, points, text, down, up):
+    down, up, maps = row_message(flat)
+
+    def body(points_in, padded, first_swap, second_swap, points, text, first_row, second_row):
         def unpack(east, west):
             for side, links, first in ((west, WEST_LINKS, -2), (east, EAST_LINKS, cols)):
                 for d, j, c, at in side_rows(links, rows):
@@ -173,19 +193,20 @@
                 text[part] = jnp.where(lane < span, value, 0.0)
 
         by_parity("col", unpack, first_swap, second_swap)
-        for n in range(4 * COMPS):
-            up[n * span : (n + 1) * span] = points[n, flat.at(0, -2) : flat.at(0, -2) + span]
-        for k in range(12):
-            up[south_t + 2 * k : south_t + 2 * k + 2] = text[k * rows : k * rows + 2]
-        for n, skip, count, to in slices:
-            at = flat.at(rows - 2 + skip, -2)
-            down[to : to + count] = points[n, at : at + count]
-        for k in range(12):
-            down[north_t + 2 * k : north_t + 2 * k + 2] = text[(k + 1) * rows - 2 : (k + 1) * rows]
+
+        def pack(to_south, to_north):
+            for out, runs, move, source in ((to_south, down, rows, rows - 2), (to_north, up, -rows, 0)):
+                for n, r, c0, c1, at in runs:
+                    out[at : at + c1 - c0 + 1] = points[n, run_of(flat, r + move, c0, c1)]
+                for k in range(12):
+                    row = k * rows + source
+                    out[maps + 2 * k : maps + 2 * k + 2] = text[row : row + 2]
+
+        by_parity("row", pack, first_row, second_row)
 
     return call(
         body,
-        [(4 * COMPS, flat.tiles, LANES), (12 * rows, LANES), (north_t + 24, LANES), (south_t + 24, LANES)],
+        [(4 * COMPS, flat.tiles, LANES), (12 * rows, LANES), (maps + 24, LANES), (maps + 24, LANES)],
         in_vmem=(0, 1, 2, 3),
         aliases={0: 0},
     )
@@ -310,21 +331,22 @@
     )
 
 
-def outer_values(flat, points, rep, errors, mapped, target, north, south):
-    rows, span = flat.rows, flat.span
-    slices, north_t = north_slices(flat)
-    for n, skip, count, src in slices:
-        at = flat.at(skip - 2, -2)
-        points[n, at : at + count] = north[src : src + count]
-    for n in range(4 * COMPS):
-        at = flat.at(rows, -2)
-        points[n, at : at + span] = south[n * span : (n + 1) * span]
-    for k in range(12):
-        for j in range(2):
-            row = north_t + 2 * k + j
-            spread(north[row : row + 1], rep, k, flat.at(j - 2, -2), span)
-            row = 4 * COMPS * span + 2 * k + j
-            spread(south[row : row + 1], rep, k, flat.at(rows + j, -2), span)
+def outer_values(flat, points, rep, errors, mapped, target, far, first_row, second_row):
+    rows, cols, span = flat.rows, flat.cols, flat.span
+    down, up, maps = row_message(flat)
+    for n in range(3 * COMPS):
+        points[COMPS + n, run_of(flat, -2, 0, cols - 1)] = far[n * cols : (n + 1) * cols]
+
+    def unpack(south, north):
+        for source, runs, first in ((north, down, -2), (south, up, rows)):
+            for n, r, c0, c1, at in runs:
+                points[n, run_of(flat, r, c0, c1)] = source[at : at + c1 - c0 + 1]
+            for k in range(12):
+                for j in range(2):
+                    row = maps + 2 * k + j
+                    spread(source[row : row + 1], rep, k, flat.at(first + j, -2), span)
+
+    by_parity("row", unpack, first_row, second_row)
     inner = set(f for f in flat.own_blocks() if f + SUB <= flat.at(rows - 1, -2))
     for f in flat.blocks(-2, -2, rows, flat.cols + 1):
         if f not in inner:
@@ -434,10 +456,10 @@
     rows, cols = flat.rows, flat.cols
 
     def body(*refs):
-        got, north, south = refs[5:8]
-        points, rep, errors, mapped, target, new_rep, out, weights = refs[8:]
+        got, far, first_row, second_row = refs[5:9]
+        points, rep, errors, mapped, target, new_rep, out, weights = refs[9:]
         state = (points, rep, errors, mapped, target)
-        outer_values(flat, *state, north, south)
+        outer_values(flat, *state, far, first_row, second_row)
         largest, mean_error = read_stats(got)
         scale = 0.25 * largest + 1e-06
         damping = damping_scale * mean_error + 1.0
@@ -452,7 +474,7 @@
         body,
         [(4 * COMPS, t, LANES)] + [(n, t, LANES) for n in (12, 4, 12, 12, 12)] + [(devices, 1, LANES)],
         [(4, t, LANES)],
-        in_vmem=range(8),
+        in_vmem=range(9),
         aliases={i: i for i in range(5)},
     )
 
@@ -506,19 +528,20 @@
     rows, cols = transforms.shape[2:]
     devices = lax.axis_size("row") * lax.axis_size("col")
     flat = Flat(rows, cols)
-    points, padded, to_first, to_second = pack_cols(flat)(
+    points, padded, to_first, to_second, to_far = pack_cols(flat)(
         points_here, points_there, outlier_mask, transforms.reshape(12 * rows, cols)
     )
     first_swap = swap(to_first, "col", 0)
     second_swap = swap(to_second, "col", 1)
     below = onward(padded, "row", -1)
-    points, text, to_down, to_up = pack_rows(flat)(points, padded, first_swap, second_swap)
-    south = onward(to_up, "row", -1)
-    north = onward(to_down, "row", 1)
+    far = onward(to_far, "row", 1)
+    points, text, to_first, to_second = pack_rows(flat)(points, padded, first_swap, second_swap)
+    first_row = swap(to_first, "row", 0)
+    second_row = swap(to_second, "row", 1)
     rep, errors, mapped, target, sent = first_stats(flat, devices)(points, text, below)
     got0 = everyone(sent)
     points, _, errors, mapped, target, rep, sent = first_update(flat, devices)(
-        points, rep, errors, mapped, target, got0, north, south
+        points, rep, errors, mapped, target, got0, far, first_row, second_row
     )
     got1 = everyone(sent)
     aligned, stats = last_update(flat)(got0, got1, points, rep, errors, mapped, target)

time: 51.2 us -> 49.8 us (0.973)
  starting transfers between devices: 7.68 us -> 10.9 us
  waiting for transfers between devices: 6.41 us -> 3.76 us
  blocking collectives: 29.5 us -> 27.6 us
    ppermute x3 -> x2, waiting for transfers between devices: 4.45 us -> 1.79 us  [onward(): lax.ppermute(array, axis, [(i, i + by) for i in range(peers) if 0 <= i +...]
    ppermute x3 -> x2, starting transfers between devices: 3.91 us -> 6.37 us  [onward(): lax.ppermute(array, axis, [(i, i + by) for i in range(peers) if 0 <= i +...]
    all_to_all x2, blocking collectives: 29.5 us -> 27.6 us  [everyone(): return lax.all_to_all(array, ('row', 'col'), 0, 0)]
    ppermute x2 -> x4, starting transfers between devices: 3.77 us -> 4.52 us  [swap(): lax.ppermute(array, axis, [pair for i in lower for pair in ((i, i + 1), (...]
    ppermute x2 -> x4, waiting for transfers between devices: 1.96 us -> 1.96 us  [swap(): lax.ppermute(array, axis, [pair for i in lower for pair in ((i, i + 1), (...]
  transfers between devices with their start and end apart: 5 -> 6, of which waited for: 2 -> 2; matrix products, arithmetic and copies ran while one was open for 0% -> 0% of each run, Pallas kernels for 1% -> 1%
where the time goes in v6:
time: 49.8 us; the launch traced here: 49.5 us
  blocking collectives  27.6 us (55%)
  starting transfers between devices  10.9 us (22%)
  Pallas kernels  6.55 us (13%)
  waiting for transfers between devices  3.76 us (8%)
  between operations  0.71 us (1%)
    all_to_all x2, blocking collectives, everyone(): return lax.all_to_all(array, ('row', 'col'), 0, 0)  27.6 us
    pallas_call x5, Pallas kernels, run(): pl.pallas_call(body, out_shape=shapes, in_specs=[hbm if i in in_hbm else...  6.55 us
    ppermute x2, starting transfers between devices, onward(): lax.ppermute(array, axis, [(i, i + by) for i in range(peers) if 0 <= i +...  6.37 us
    ppermute x4, starting transfers between devices, swap(): lax.ppermute(array, axis, [pair for i in lower for pair in ((i, i + 1), (...  4.52 us
    ppermute x4, waiting for transfers between devices, swap(): lax.ppermute(array, axis, [pair for i in lower for pair in ((i, i + 1), (...  1.96 us
    ppermute x2, waiting for transfers between devices, onward(): lax.ppermute(array, axis, [(i, i + by) for i in range(peers) if 0 <= i +...  1.79 us
  transfers between devices with their start and end apart: 6, of which 2 were waited for; matrix products, arithmetic and copies ran while one was open for 0% of the time, Pallas kernels for 1%

profile of v6, /device:TPU:0, one launch (start us, length us, event | category | flops | bytes accessed | tf_op | source)
XLA Modules:
  0.0 49.5 jit_solution(195819389609769602)
XLA Ops:
  0.6 1.4 %shard_map.59 = (f32[28,200,128]{2,1,0:T(8,128)S(1)}, f32[48,128]{1,0:T(8,128)S(1)}, f32[176,128]{1,0:T(8,128)S(1)}, f32[176,128]{1,0:T(8,128)S(1)}, f32[336,128]{1,0:T(8,128)S(1)}) custom-call(f32[4,3,4,16,128]{4,3,2,1,0:T(8,128)} %here_in.1, f32[4,3,4,16,128]{4,3,2,1,0:T(8,128)} %there_in.1, s32[4,4,16,128]{3,2,1,0:T(8,128)} %outlier_in.1, f32[48,16]{1,0:T(8,128)} %bitcast.2), custom_call_target="tpu_custom_call" | custom-call | tf_op jit(solution)/shard_map/pallas_call | solution.py:25
  2.1 3.1 %collective-permute-start = (f32[176,128]{1,0:T(8,128)S(1)}, f32[176,128]{1,0:T(8,128)S(1)}, u32[]{:S(2)}, u32[]{:S(2)}) collective-permute-start(f32[176,128]{1,0:T(8,128)S(1)} %get-tuple-element.26), channel_id=1, source_target_pairs={{0,1},{1,0},{2,3},{3,2},{4,5},{5,4},{6,7},{7,6},{8,9},{9,8},{10,11... | collective-permute-start | bytes 270344 | tf_op jit(solution)/shard_map/ppermute | solution.py:69
  5.2 0.7 %collective-permute-start.1 = (f32[176,128]{1,0:T(8,128)S(1)}, f32[176,128]{1,0:T(8,128)S(1)}, u32[]{:S(2)}, u32[]{:S(2)}) collective-permute-start(f32[176,128]{1,0:T(8,128)S(1)} %get-tuple-element.27), channel_id=1, source_target_pairs={{1,2},{2,1},{5,6},{6,5},{9,10},{10,9},{13,14},{14,13},{17,18},{18,... | collective-permute-start | bytes 270344 | tf_op jit(solution)/shard_map/ppermute | solution.py:69
  5.9 2.0 %collective-permute-done.first_swap = f32[176,128]{1,0:T(8,128)S(1)} collective-permute-done((f32[176,128]{1,0:T(8,128)S(1)}, f32[176,128]{1,0:T(8,128)S(1)}, u32[]{:S(2)}, u32[]{:S(2)}) %collective-permute-start) | collective-permute-done | bytes 90144 | tf_op jit(solution)/shard_map/ppermute | solution.py:69
  7.8 0.0 collective-permute-done.1.second_swap
  7.8 0.2 shard_map.60
  8.0 0.1 collective-permute-start.4
  8.1 0.7 %collective-permute-start.5 = (f32[592,128]{1,0:T(8,128)S(1)}, f32[592,128]{1,0:T(8,128)S(1)}, u32[]{:S(2)}, u32[]{:S(2)}) collective-permute-start(f32[592,128]{1,0:T(8,128)S(1)} %get-tuple-element.37), channel_id=1, source_target_pairs={{4,8},{8,4},{12,16},{16,12},{20,24},{24,20},{5,9},{9,5},{13,17},{1... | collective-permute-start | bytes 909320 | tf_op jit(solution)/shard_map/ppermute | solution.py:69
  8.8 5.1 %collective-permute-start.3 = (f32[336,128]{1,0:T(8,128)S(1)}, f32[336,128]{1,0:T(8,128)S(1)}, u32[]{:S(2)}, u32[]{:S(2)}) collective-permute-start(f32[336,128]{1,0:T(8,128)S(1)} %get-tuple-element.35), channel_id=1, source_target_pairs={{0,4},{4,8},{8,12},{12,16},{16,20},{20,24},{24,28},{1,5},{5,9},{9,... | collective-permute-start | bytes 516104 | tf_op jit(solution)/shard_map/ppermute | solution.py:520
  13.9 1.3 %collective-permute-start.2 = (f32[48,128]{1,0:T(8,128)S(1)}, f32[48,128]{1,0:T(8,128)S(1)}, u32[]{:S(2)}, u32[]{:S(2)}) collective-permute-start(f32[48,128]{1,0:T(8,128)S(1)} %get-tuple-element.25.padded), channel_id=1, source_target_pairs={{4,0},{8,4},{12,8},{16,12},{20,16},{24,20},{28,24},{5,1},{9,5},{13... | collective-permute-start | bytes 73736 | tf_op jit(solution)/shard_map/ppermute | solution.py:520
  15.2 1.8 %collective-permute-done.2.south = f32[48,128]{1,0:T(8,128)S(1)} collective-permute-done((f32[48,128]{1,0:T(8,128)S(1)}, f32[48,128]{1,0:T(8,128)S(1)}, u32[]{:S(2)}, u32[]{:S(2)}) %collective-permute-start.2) | collective-permute-done | bytes 24608 | tf_op jit(solution)/shard_map/ppermute | solution.py:520
  17.0 0.7 %shard_map.61 = (f32[12,200,128]{2,1,0:T(8,128)S(1)}, f32[4,200,128]{2,1,0:T(8,128)S(1)}, f32[12,200,128]{2,1,0:T(8,128)S(1)}, f32[12,200,128]{2,1,0:T(8,128)S(1)}, f32[32,1,128]{2,1,0:T(1,128)S(1)}) custom-call(f32[28,200,128]{2,1,0:T(8,128)S(1)} %get-tuple-element.28.points.refs_0_, f32[48,128]{1,0:T(8,128)S(1)} %get-tuple-element.29.text, ...), custom_call_target="tpu_custom_call" | custom-call | tf_op jit(solution)/shard_map/pallas_call | solution.py:25
  17.6 18.7 %all_to_all.10.refs_5_.got0 = f32[32,1,128]{2,1,0:T(1,128)S(1)} all-to-all(f32[32,1,128]{2,1,0:T(1,128)S(1)} %get-tuple-element.30), channel_id=1, replica_groups=mesh['row'=8,'col'=4] {'row','col'}, dimensions={0} | all-to-all | bytes 32768 | tf_op jit(solution)/shard_map/all_to_all | solution.py:524
  36.3 0.0 collective-permute-done.3.refs_6_
  36.3 0.0 collective-permute-done.4.refs_7_
  36.3 0.0 collective-permute-done.5.refs_8_
  36.3 2.5 %shard_map.62 = (f32[28,200,128]{2,1,0:T(8,128)S(1)}, f32[12,200,128]{2,1,0:T(8,128)S(1)}, f32[4,200,128]{2,1,0:T(8,128)S(1)}, f32[12,200,128]{2,1,0:T(8,128)S(1...) custom-call(f32[28,200,128]{2,1,0:T(8,128)S(1)} %get-tuple-element.2, ...), custom_call_target="tpu_custom_call", output_to_operand_aliasing={{0}: (0, {}), {1}: (1, {}), {2}: (2, {}), {3}: (3, {}), {4}... | custom-call | tf_op jit(solution)/shard_map/pallas_call | solution.py:25
  38.8 8.9 %all_to_all.11.got1 = f32[32,1,128]{2,1,0:T(1,128)S(1)} all-to-all(f32[32,1,128]{2,1,0:T(1,128)S(1)} %get-tuple-element.38), channel_id=1, replica_groups=mesh['row'=8,'col'=4] {'row','col'}, dimensions={0} | all-to-all | bytes 32768 | tf_op jit(solution)/shard_map/all_to_all | solution.py:524
  47.7 1.8 %shard_map.63 = (f32[12,4,16]{2,1,0:T(4,128)}, f32[2,2]{1,0:T(2,128)}) custom-call(f32[32,1,128]{2,1,0:T(1,128)S(1)} %all_to_all.10.refs_5_.got0, f32[32,1,128]{2,1,0:T(1,128)S(1)} %all_to_all.11.got1, f32[28,200,128]{2,1,0:T(8,128)S(1)} %get-tuple-element.39.points, f32[12,200,128]{2,1,0:T(8,128)S(1)} %get-tuple-element.40.rep, ...), custom_call_target="tpu_custom_call" | custom-call | tf_op jit(solution)/shard_map/pallas_call | solution.py:25
Async XLA Ops:
  2.1 5.7 %collective-permute-start = (f32[176,128]{1,0:T(8,128)S(1)}, f32[176,128]{1,0:T(8,128)S(1)}, u32[]{:S(2)}, u32[]{:S(2)}) collective-permute-start(f32[176,128]{1,0:T(8,128)S(1)} %get-tuple-element.26), channel_id=1, source_target_pairs={{0,1},{1,0},{2,3},{3,2},{4,5},{5,4},{6,7},{7,6},{8,9},{9,8},{10,11... | collective-permute-start | bytes 270344 | tf_op jit(solution)/shard_map/ppermute | solution.py:69
  5.2 2.6 %collective-permute-start.1 = (f32[176,128]{1,0:T(8,128)S(1)}, f32[176,128]{1,0:T(8,128)S(1)}, u32[]{:S(2)}, u32[]{:S(2)}) collective-permute-start(f32[176,128]{1,0:T(8,128)S(1)} %get-tuple-element.27), channel_id=1, source_target_pairs={{1,2},{2,1},{5,6},{6,5},{9,10},{10,9},{13,14},{14,13},{17,18},{18,... | collective-permute-start | bytes 270344 | tf_op jit(solution)/shard_map/ppermute | solution.py:69
  8.0 28.3 %collective-permute-start.4 = (f32[592,128]{1,0:T(8,128)S(1)}, f32[592,128]{1,0:T(8,128)S(1)}, u32[]{:S(2)}, u32[]{:S(2)}) collective-permute-start(f32[592,128]{1,0:T(8,128)S(1)} %get-tuple-element.36), channel_id=1, source_target_pairs={{0,4},{4,0},{8,12},{12,8},{16,20},{20,16},{24,28},{28,24},{1,5},{5... | collective-permute-start | bytes 909320 | tf_op jit(solution)/shard_map/ppermute | solution.py:69
  8.1 28.2 %collective-permute-start.5 = (f32[592,128]{1,0:T(8,128)S(1)}, f32[592,128]{1,0:T(8,128)S(1)}, u32[]{:S(2)}, u32[]{:S(2)}) collective-permute-start(f32[592,128]{1,0:T(8,128)S(1)} %get-tuple-element.37), channel_id=1, source_target_pairs={{4,8},{8,4},{12,16},{16,12},{20,24},{24,20},{5,9},{9,5},{13,17},{1... | collective-permute-start | bytes 909320 | tf_op jit(solution)/shard_map/ppermute | solution.py:69
  8.8 27.5 %collective-permute-start.3 = (f32[336,128]{1,0:T(8,128)S(1)}, f32[336,128]{1,0:T(8,128)S(1)}, u32[]{:S(2)}, u32[]{:S(2)}) collective-permute-start(f32[336,128]{1,0:T(8,128)S(1)} %get-tuple-element.35), channel_id=1, source_target_pairs={{0,4},{4,8},{8,12},{12,16},{16,20},{20,24},{24,28},{1,5},{5,9},{9,... | collective-permute-start | bytes 516104 | tf_op jit(solution)/shard_map/ppermute | solution.py:520
  13.9 3.1 %collective-permute-start.2 = (f32[48,128]{1,0:T(8,128)S(1)}, f32[48,128]{1,0:T(8,128)S(1)}, u32[]{:S(2)}, u32[]{:S(2)}) collective-permute-start(f32[48,128]{1,0:T(8,128)S(1)} %get-tuple-element.25.padded), channel_id=1, source_target_pairs={{4,0},{8,4},{12,8},{16,12},{20,16},{24,20},{28,24},{5,1},{9,5},{13... | collective-permute-start | bytes 73736 | tf_op jit(solution)/shard_map/ppermute | solution.py:520

commit v7 on v6

--- a/solution.py
+++ b/solution.py
@@ -234,18 +234,26 @@
     return delta[0] * delta[0] + delta[1] * delta[1] + delta[2] * delta[2]
 
 
-def send_stats(out, largest, total, count):
-    lane = iota(out.shape, len(out.shape) - 1)
-    out[...] = jnp.where(lane == 0, largest, jnp.where(lane == 1, total, jnp.where(lane == 2, count, 0.0)))
+def send_stats(out, top, total, count):
+    def one(reduce, value):
+        value = reduce(reduce(value, axis=0, keepdims=True), axis=1, keepdims=True)
+        return jnp.broadcast_to(value, (1, LANES))
+
+    lane = iota((1, LANES), 1)
+    value = jnp.where(lane == 1, one(jnp.sum, total), jnp.where(lane == 2, one(jnp.sum, count), 0.0))
+    value = jnp.where(lane == 0, one(jnp.max, top), value)
+    out[...] = jnp.broadcast_to(value[None], out.shape)
 
 
 def read_stats(got):
     values = got[...]
-    lane = iota(values.shape, 2)
-    largest = jnp.max(jnp.where(lane == 0, values, 0.0))
-    total = jnp.sum(jnp.where(lane == 1, values, 0.0))
-    count = jnp.sum(jnp.where(lane == 2, values, 0.0))
-    return largest, total / jnp.maximum(count, 1.0)
+    most = jnp.max(values, axis=0)
+    sums = jnp.sum(values, axis=0)
+
+    def spread_lane(value, n):
+        return jnp.broadcast_to(value[:, n : n + 1], (SUB, LANES))
+
+    return spread_lane(most, 0), spread_lane(sums, 1) / jnp.maximum(spread_lane(sums, 2), 1.0)
 
 
 class Flat:
@@ -309,7 +317,7 @@
             top = jnp.maximum(top, masked)
             total = total + masked
             count = count + weight
-    send_stats(out, jnp.max(top), jnp.sum(total), jnp.sum(count))
+    send_stats(out, top, total, count)
 
 
 def first_stats(flat, devices):
@@ -509,6 +517,7 @@
                 aligned[k, r : r + 1] = take_lanes(lines, at, cols)
         row = iota((2, 2), 0)
         col = iota((2, 2), 1)
+        first, largest, mean0, mean_error = [v[0:2, 0:2] for v in (first, largest, mean0, mean_error)]
         stats[...] = jnp.where(row == 0, jnp.where(col == 0, first, largest), jnp.where(col == 0, mean0, mean_error))
 
     t = flat.tiles

time: 49.8 us -> 49.5 us (level)
  no operation moved by 1% of the time
where the time goes in v7:
time: 49.5 us; the launch traced here: 49.2 us
  blocking collectives  27.6 us (56%)
  starting transfers between devices  10.9 us (22%)
  Pallas kernels  6.24 us (13%)
  waiting for transfers between devices  3.76 us (8%)
  between operations  0.71 us (1%)
    all_to_all x2, blocking collectives, everyone(): return lax.all_to_all(array, ('row', 'col'), 0, 0)  27.6 us
    ppermute x2, starting transfers between devices, onward(): lax.ppermute(array, axis, [(i, i + by) for i in range(peers) if 0 <= i +...  6.37 us
    pallas_call x5, Pallas kernels, run(): pl.pallas_call(body, out_shape=shapes, in_specs=[hbm if i in in_hbm else...  6.24 us
    ppermute x4, starting transfers between devices, swap(): lax.ppermute(array, axis, [pair for i in lower for pair in ((i, i + 1), (...  4.52 us
    ppermute x4, waiting for transfers between devices, swap(): lax.ppermute(array, axis, [pair for i in lower for pair in ((i, i + 1), (...  1.96 us
    ppermute x2, waiting for transfers between devices, onward(): lax.ppermute(array, axis, [(i, i + by) for i in range(peers) if 0 <= i +...  1.79 us
  transfers between devices with their start and end apart: 6, of which 2 were waited for; matrix products, arithmetic and copies ran while one was open for 0% of the time, Pallas kernels for 1%

profile of v7, /device:TPU:0, one launch (start us, length us, event | category | flops | bytes accessed | tf_op | source)
XLA Modules:
  0.0 49.2 jit_solution(12316758893153872755)
XLA Ops:
  0.6 1.4 %shard_map.59 = (f32[28,200,128]{2,1,0:T(8,128)S(1)}, f32[48,128]{1,0:T(8,128)S(1)}, f32[176,128]{1,0:T(8,128)S(1)}, f32[176,128]{1,0:T(8,128)S(1)}, f32[336,128]{1,0:T(8,128)S(1)}) custom-call(f32[4,3,4,16,128]{4,3,2,1,0:T(8,128)} %here_in.1, f32[4,3,4,16,128]{4,3,2,1,0:T(8,128)} %there_in.1, s32[4,4,16,128]{3,2,1,0:T(8,128)} %outlier_in.1, f32[48,16]{1,0:T(8,128)} %bitcast.2), custom_call_target="tpu_custom_call" | custom-call | tf_op jit(solution)/shard_map/pallas_call | solution.py:25
  2.1 3.1 %collective-permute-start = (f32[176,128]{1,0:T(8,128)S(1)}, f32[176,128]{1,0:T(8,128)S(1)}, u32[]{:S(2)}, u32[]{:S(2)}) collective-permute-start(f32[176,128]{1,0:T(8,128)S(1)} %get-tuple-element.26), channel_id=1, source_target_pairs={{0,1},{1,0},{2,3},{3,2},{4,5},{5,4},{6,7},{7,6},{8,9},{9,8},{10,11... | collective-permute-start | bytes 270344 | tf_op jit(solution)/shard_map/ppermute | solution.py:69
  5.2 0.7 %collective-permute-start.1 = (f32[176,128]{1,0:T(8,128)S(1)}, f32[176,128]{1,0:T(8,128)S(1)}, u32[]{:S(2)}, u32[]{:S(2)}) collective-permute-start(f32[176,128]{1,0:T(8,128)S(1)} %get-tuple-element.27), channel_id=1, source_target_pairs={{1,2},{2,1},{5,6},{6,5},{9,10},{10,9},{13,14},{14,13},{17,18},{18,... | collective-permute-start | bytes 270344 | tf_op jit(solution)/shard_map/ppermute | solution.py:69
  5.9 2.0 %collective-permute-done.first_swap = f32[176,128]{1,0:T(8,128)S(1)} collective-permute-done((f32[176,128]{1,0:T(8,128)S(1)}, f32[176,128]{1,0:T(8,128)S(1)}, u32[]{:S(2)}, u32[]{:S(2)}) %collective-permute-start) | collective-permute-done | bytes 90144 | tf_op jit(solution)/shard_map/ppermute | solution.py:69
  7.8 0.0 collective-permute-done.1.second_swap
  7.8 0.2 shard_map.60
  8.0 0.1 collective-permute-start.4
  8.1 0.7 %collective-permute-start.5 = (f32[592,128]{1,0:T(8,128)S(1)}, f32[592,128]{1,0:T(8,128)S(1)}, u32[]{:S(2)}, u32[]{:S(2)}) collective-permute-start(f32[592,128]{1,0:T(8,128)S(1)} %get-tuple-element.37), channel_id=1, source_target_pairs={{4,8},{8,4},{12,16},{16,12},{20,24},{24,20},{5,9},{9,5},{13,17},{1... | collective-permute-start | bytes 909320 | tf_op jit(solution)/shard_map/ppermute | solution.py:69
  8.8 5.1 %collective-permute-start.3 = (f32[336,128]{1,0:T(8,128)S(1)}, f32[336,128]{1,0:T(8,128)S(1)}, u32[]{:S(2)}, u32[]{:S(2)}) collective-permute-start(f32[336,128]{1,0:T(8,128)S(1)} %get-tuple-element.35), channel_id=1, source_target_pairs={{0,4},{4,8},{8,12},{12,16},{16,20},{20,24},{24,28},{1,5},{5,9},{9,... | collective-permute-start | bytes 516104 | tf_op jit(solution)/shard_map/ppermute | solution.py:529
  13.9 1.3 %collective-permute-start.2 = (f32[48,128]{1,0:T(8,128)S(1)}, f32[48,128]{1,0:T(8,128)S(1)}, u32[]{:S(2)}, u32[]{:S(2)}) collective-permute-start(f32[48,128]{1,0:T(8,128)S(1)} %get-tuple-element.25.padded), channel_id=1, source_target_pairs={{4,0},{8,4},{12,8},{16,12},{20,16},{24,20},{28,24},{5,1},{9,5},{13... | collective-permute-start | bytes 73736 | tf_op jit(solution)/shard_map/ppermute | solution.py:529
  15.2 1.8 %collective-permute-done.2.south = f32[48,128]{1,0:T(8,128)S(1)} collective-permute-done((f32[48,128]{1,0:T(8,128)S(1)}, f32[48,128]{1,0:T(8,128)S(1)}, u32[]{:S(2)}, u32[]{:S(2)}) %collective-permute-start.2) | collective-permute-done | bytes 24608 | tf_op jit(solution)/shard_map/ppermute | solution.py:529
  17.0 0.6 %shard_map.61 = (f32[12,200,128]{2,1,0:T(8,128)S(1)}, f32[4,200,128]{2,1,0:T(8,128)S(1)}, f32[12,200,128]{2,1,0:T(8,128)S(1)}, f32[12,200,128]{2,1,0:T(8,128)S(1)}, f32[32,1,128]{2,1,0:T(1,128)S(1)}) custom-call(f32[28,200,128]{2,1,0:T(8,128)S(1)} %get-tuple-element.28.points.refs_0_, f32[48,128]{1,0:T(8,128)S(1)} %get-tuple-element.29.text, ...), custom_call_target="tpu_custom_call" | custom-call | tf_op jit(solution)/shard_map/pallas_call | solution.py:25
  17.6 18.7 %all_to_all.10.refs_5_.got0 = f32[32,1,128]{2,1,0:T(1,128)S(1)} all-to-all(f32[32,1,128]{2,1,0:T(1,128)S(1)} %get-tuple-element.30), channel_id=1, replica_groups=mesh['row'=8,'col'=4] {'row','col'}, dimensions={0} | all-to-all | bytes 32768 | tf_op jit(solution)/shard_map/all_to_all | solution.py:533
  36.3 0.0 collective-permute-done.3.refs_6_
  36.3 0.0 collective-permute-done.4.refs_7_
  36.3 0.0 collective-permute-done.5.refs_8_
  36.3 2.4 %shard_map.62 = (f32[28,200,128]{2,1,0:T(8,128)S(1)}, f32[12,200,128]{2,1,0:T(8,128)S(1)}, f32[4,200,128]{2,1,0:T(8,128)S(1)}, f32[12,200,128]{2,1,0:T(8,128)S(1...) custom-call(f32[28,200,128]{2,1,0:T(8,128)S(1)} %get-tuple-element.2, ...), custom_call_target="tpu_custom_call", output_to_operand_aliasing={{0}: (0, {}), {1}: (1, {}), {2}: (2, {}), {3}: (3, {}), {4}... | custom-call | tf_op jit(solution)/shard_map/pallas_call | solution.py:25
  38.7 8.9 %all_to_all.11.got1 = f32[32,1,128]{2,1,0:T(1,128)S(1)} all-to-all(f32[32,1,128]{2,1,0:T(1,128)S(1)} %get-tuple-element.38), channel_id=1, replica_groups=mesh['row'=8,'col'=4] {'row','col'}, dimensions={0} | all-to-all | bytes 32768 | tf_op jit(solution)/shard_map/all_to_all | solution.py:533
  47.6 1.6 %shard_map.63 = (f32[12,4,16]{2,1,0:T(4,128)}, f32[2,2]{1,0:T(2,128)}) custom-call(f32[32,1,128]{2,1,0:T(1,128)S(1)} %all_to_all.10.refs_5_.got0, f32[32,1,128]{2,1,0:T(1,128)S(1)} %all_to_all.11.got1, f32[28,200,128]{2,1,0:T(8,128)S(1)} %get-tuple-element.39.points, f32[12,200,128]{2,1,0:T(8,128)S(1)} %get-tuple-element.40.rep, ...), custom_call_target="tpu_custom_call" | custom-call | tf_op jit(solution)/shard_map/pallas_call | solution.py:25
Async XLA Ops:
  2.1 5.7 %collective-permute-start = (f32[176,128]{1,0:T(8,128)S(1)}, f32[176,128]{1,0:T(8,128)S(1)}, u32[]{:S(2)}, u32[]{:S(2)}) collective-permute-start(f32[176,128]{1,0:T(8,128)S(1)} %get-tuple-element.26), channel_id=1, source_target_pairs={{0,1},{1,0},{2,3},{3,2},{4,5},{5,4},{6,7},{7,6},{8,9},{9,8},{10,11... | collective-permute-start | bytes 270344 | tf_op jit(solution)/shard_map/ppermute | solution.py:69
  5.2 2.6 %collective-permute-start.1 = (f32[176,128]{1,0:T(8,128)S(1)}, f32[176,128]{1,0:T(8,128)S(1)}, u32[]{:S(2)}, u32[]{:S(2)}) collective-permute-start(f32[176,128]{1,0:T(8,128)S(1)} %get-tuple-element.27), channel_id=1, source_target_pairs={{1,2},{2,1},{5,6},{6,5},{9,10},{10,9},{13,14},{14,13},{17,18},{18,... | collective-permute-start | bytes 270344 | tf_op jit(solution)/shard_map/ppermute | solution.py:69
  8.0 28.3 %collective-permute-start.4 = (f32[592,128]{1,0:T(8,128)S(1)}, f32[592,128]{1,0:T(8,128)S(1)}, u32[]{:S(2)}, u32[]{:S(2)}) collective-permute-start(f32[592,128]{1,0:T(8,128)S(1)} %get-tuple-element.36), channel_id=1, source_target_pairs={{0,4},{4,0},{8,12},{12,8},{16,20},{20,16},{24,28},{28,24},{1,5},{5... | collective-permute-start | bytes 909320 | tf_op jit(solution)/shard_map/ppermute | solution.py:69
  8.1 28.2 %collective-permute-start.5 = (f32[592,128]{1,0:T(8,128)S(1)}, f32[592,128]{1,0:T(8,128)S(1)}, u32[]{:S(2)}, u32[]{:S(2)}) collective-permute-start(f32[592,128]{1,0:T(8,128)S(1)} %get-tuple-element.37), channel_id=1, source_target_pairs={{4,8},{8,4},{12,16},{16,12},{20,24},{24,20},{5,9},{9,5},{13,17},{1... | collective-permute-start | bytes 909320 | tf_op jit(solution)/shard_map/ppermute | solution.py:69
  8.8 27.5 %collective-permute-start.3 = (f32[336,128]{1,0:T(8,128)S(1)}, f32[336,128]{1,0:T(8,128)S(1)}, u32[]{:S(2)}, u32[]{:S(2)}) collective-permute-start(f32[336,128]{1,0:T(8,128)S(1)} %get-tuple-element.35), channel_id=1, source_target_pairs={{0,4},{4,8},{8,12},{12,16},{16,20},{20,24},{24,28},{1,5},{5,9},{9,... | collective-permute-start | bytes 516104 | tf_op jit(solution)/shard_map/ppermute | solution.py:529
  13.9 3.1 %collective-permute-start.2 = (f32[48,128]{1,0:T(8,128)S(1)}, f32[48,128]{1,0:T(8,128)S(1)}, u32[]{:S(2)}, u32[]{:S(2)}) collective-permute-start(f32[48,128]{1,0:T(8,128)S(1)} %get-tuple-element.25.padded), channel_id=1, source_target_pairs={{4,0},{8,4},{12,8},{16,12},{20,16},{24,20},{28,24},{5,1},{9,5},{13... | collective-permute-start | bytes 73736 | tf_op jit(solution)/shard_map/ppermute | solution.py:529

commit v8 on v7

--- a/solution.py
+++ b/solution.py
@@ -355,10 +355,13 @@
                     spread(source[row : row + 1], rep, k, flat.at(first + j, -2), span)
 
     by_parity("row", unpack, first_row, second_row)
-    inner = set(f for f in flat.own_blocks() if f + SUB <= flat.at(rows - 1, -2))
+    own = set(flat.own_blocks())
+    inner = set(f for f in own if f + SUB <= flat.at(rows - 1, -2))
     for f in flat.blocks(-2, -2, rows, flat.cols + 1):
         if f not in inner:
-            for d in range(4):
+            outer = f + SUB <= flat.at(-1, -2)
+            known = f in own and f + SUB <= flat.at(rows, -2)
+            for d in range(1 if outer or known else 0, 4):
                 link_values(flat, f, d, points, rep, errors, mapped, target)
 
 

time: 49.5 us -> 49.4 us (level)
  no operation moved by 1% of the time
where the time goes in v8:
time: 49.4 us; the launch traced here: 49.2 us
  blocking collectives  27.6 us (56%)
  starting transfers between devices  10.9 us (22%)
  Pallas kernels  6.21 us (13%)
  waiting for transfers between devices  3.76 us (8%)
  between operations  0.71 us (1%)
    all_to_all x2, blocking collectives, everyone(): return lax.all_to_all(array, ('row', 'col'), 0, 0)  27.6 us
    ppermute x2, starting transfers between devices, onward(): lax.ppermute(array, axis, [(i, i + by) for i in range(peers) if 0 <= i +...  6.37 us
    pallas_call x5, Pallas kernels, run(): pl.pallas_call(body, out_shape=shapes, in_specs=[hbm if i in in_hbm else...  6.21 us
    ppermute x4, starting transfers between devices, swap(): lax.ppermute(array, axis, [pair for i in lower for pair in ((i, i + 1), (...  4.52 us
    ppermute x4, waiting for transfers between devices, swap(): lax.ppermute(array, axis, [pair for i in lower for pair in ((i, i + 1), (...  1.96 us
    ppermute x2, waiting for transfers between devices, onward(): lax.ppermute(array, axis, [(i, i + by) for i in range(peers) if 0 <= i +...  1.79 us
  transfers between devices with their start and end apart: 6, of which 2 were waited for; matrix products, arithmetic and copies ran while one was open for 0% of the time, Pallas kernels for 1%

profile of v8, /device:TPU:0, one launch (start us, length us, event | category | flops | bytes accessed | tf_op | source)
XLA Modules:
  0.0 49.2 jit_solution(16412289319152734614)
XLA Ops:
  0.6 1.4 %shard_map.59 = (f32[28,200,128]{2,1,0:T(8,128)S(1)}, f32[48,128]{1,0:T(8,128)S(1)}, f32[176,128]{1,0:T(8,128)S(1)}, f32[176,128]{1,0:T(8,128)S(1)}, f32[336,128]{1,0:T(8,128)S(1)}) custom-call(f32[4,3,4,16,128]{4,3,2,1,0:T(8,128)} %here_in.1, f32[4,3,4,16,128]{4,3,2,1,0:T(8,128)} %there_in.1, s32[4,4,16,128]{3,2,1,0:T(8,128)} %outlier_in.1, f32[48,16]{1,0:T(8,128)} %bitcast.2), custom_call_target="tpu_custom_call" | custom-call | tf_op jit(solution)/shard_map/pallas_call | solution.py:25
  2.1 3.1 %collective-permute-start = (f32[176,128]{1,0:T(8,128)S(1)}, f32[176,128]{1,0:T(8,128)S(1)}, u32[]{:S(2)}, u32[]{:S(2)}) collective-permute-start(f32[176,128]{1,0:T(8,128)S(1)} %get-tuple-element.26), channel_id=1, source_target_pairs={{0,1},{1,0},{2,3},{3,2},{4,5},{5,4},{6,7},{7,6},{8,9},{9,8},{10,11... | collective-permute-start | bytes 270344 | tf_op jit(solution)/shard_map/ppermute | solution.py:69
  5.2 0.7 %collective-permute-start.1 = (f32[176,128]{1,0:T(8,128)S(1)}, f32[176,128]{1,0:T(8,128)S(1)}, u32[]{:S(2)}, u32[]{:S(2)}) collective-permute-start(f32[176,128]{1,0:T(8,128)S(1)} %get-tuple-element.27), channel_id=1, source_target_pairs={{1,2},{2,1},{5,6},{6,5},{9,10},{10,9},{13,14},{14,13},{17,18},{18,... | collective-permute-start | bytes 270344 | tf_op jit(solution)/shard_map/ppermute | solution.py:69
  5.9 2.0 %collective-permute-done.first_swap = f32[176,128]{1,0:T(8,128)S(1)} collective-permute-done((f32[176,128]{1,0:T(8,128)S(1)}, f32[176,128]{1,0:T(8,128)S(1)}, u32[]{:S(2)}, u32[]{:S(2)}) %collective-permute-start) | collective-permute-done | bytes 90144 | tf_op jit(solution)/shard_map/ppermute | solution.py:69
  7.8 0.0 collective-permute-done.1.second_swap
  7.8 0.2 shard_map.60
  8.0 0.1 collective-permute-start.4
  8.1 0.7 %collective-permute-start.5 = (f32[592,128]{1,0:T(8,128)S(1)}, f32[592,128]{1,0:T(8,128)S(1)}, u32[]{:S(2)}, u32[]{:S(2)}) collective-permute-start(f32[592,128]{1,0:T(8,128)S(1)} %get-tuple-element.37), channel_id=1, source_target_pairs={{4,8},{8,4},{12,16},{16,12},{20,24},{24,20},{5,9},{9,5},{13,17},{1... | collective-permute-start | bytes 909320 | tf_op jit(solution)/shard_map/ppermute | solution.py:69
  8.8 5.1 %collective-permute-start.3 = (f32[336,128]{1,0:T(8,128)S(1)}, f32[336,128]{1,0:T(8,128)S(1)}, u32[]{:S(2)}, u32[]{:S(2)}) collective-permute-start(f32[336,128]{1,0:T(8,128)S(1)} %get-tuple-element.35), channel_id=1, source_target_pairs={{0,4},{4,8},{8,12},{12,16},{16,20},{20,24},{24,28},{1,5},{5,9},{9,... | collective-permute-start | bytes 516104 | tf_op jit(solution)/shard_map/ppermute | solution.py:532
  13.9 1.3 %collective-permute-start.2 = (f32[48,128]{1,0:T(8,128)S(1)}, f32[48,128]{1,0:T(8,128)S(1)}, u32[]{:S(2)}, u32[]{:S(2)}) collective-permute-start(f32[48,128]{1,0:T(8,128)S(1)} %get-tuple-element.25.padded), channel_id=1, source_target_pairs={{4,0},{8,4},{12,8},{16,12},{20,16},{24,20},{28,24},{5,1},{9,5},{13... | collective-permute-start | bytes 73736 | tf_op jit(solution)/shard_map/ppermute | solution.py:532
  15.2 1.8 %collective-permute-done.2.south = f32[48,128]{1,0:T(8,128)S(1)} collective-permute-done((f32[48,128]{1,0:T(8,128)S(1)}, f32[48,128]{1,0:T(8,128)S(1)}, u32[]{:S(2)}, u32[]{:S(2)}) %collective-permute-start.2) | collective-permute-done | bytes 24608 | tf_op jit(solution)/shard_map/ppermute | solution.py:532
  17.0 0.6 %shard_map.61 = (f32[12,200,128]{2,1,0:T(8,128)S(1)}, f32[4,200,128]{2,1,0:T(8,128)S(1)}, f32[12,200,128]{2,1,0:T(8,128)S(1)}, f32[12,200,128]{2,1,0:T(8,128)S(1)}, f32[32,1,128]{2,1,0:T(1,128)S(1)}) custom-call(f32[28,200,128]{2,1,0:T(8,128)S(1)} %get-tuple-element.28.points.refs_0_, f32[48,128]{1,0:T(8,128)S(1)} %get-tuple-element.29.text, ...), custom_call_target="tpu_custom_call" | custom-call | tf_op jit(solution)/shard_map/pallas_call | solution.py:25
  17.6 18.7 %all_to_all.10.refs_5_.got0 = f32[32,1,128]{2,1,0:T(1,128)S(1)} all-to-all(f32[32,1,128]{2,1,0:T(1,128)S(1)} %get-tuple-element.30), channel_id=1, replica_groups=mesh['row'=8,'col'=4] {'row','col'}, dimensions={0} | all-to-all | bytes 32768 | tf_op jit(solution)/shard_map/all_to_all | solution.py:536
  36.3 0.0 collective-permute-done.3.refs_6_
  36.3 0.0 collective-permute-done.4.refs_7_
  36.3 0.0 collective-permute-done.5.refs_8_
  36.3 2.4 %shard_map.62 = (f32[28,200,128]{2,1,0:T(8,128)S(1)}, f32[12,200,128]{2,1,0:T(8,128)S(1)}, f32[4,200,128]{2,1,0:T(8,128)S(1)}, f32[12,200,128]{2,1,0:T(8,128)S(1...) custom-call(f32[28,200,128]{2,1,0:T(8,128)S(1)} %get-tuple-element.2, ...), custom_call_target="tpu_custom_call", output_to_operand_aliasing={{0}: (0, {}), {1}: (1, {}), {2}: (2, {}), {3}: (3, {}), {4}... | custom-call | tf_op jit(solution)/shard_map/pallas_call | solution.py:25
  38.7 8.9 %all_to_all.11.got1 = f32[32,1,128]{2,1,0:T(1,128)S(1)} all-to-all(f32[32,1,128]{2,1,0:T(1,128)S(1)} %get-tuple-element.38), channel_id=1, replica_groups=mesh['row'=8,'col'=4] {'row','col'}, dimensions={0} | all-to-all | bytes 32768 | tf_op jit(solution)/shard_map/all_to_all | solution.py:536
  47.6 1.6 %shard_map.63 = (f32[12,4,16]{2,1,0:T(4,128)}, f32[2,2]{1,0:T(2,128)}) custom-call(f32[32,1,128]{2,1,0:T(1,128)S(1)} %all_to_all.10.refs_5_.got0, f32[32,1,128]{2,1,0:T(1,128)S(1)} %all_to_all.11.got1, f32[28,200,128]{2,1,0:T(8,128)S(1)} %get-tuple-element.39.points, f32[12,200,128]{2,1,0:T(8,128)S(1)} %get-tuple-element.40.rep, ...), custom_call_target="tpu_custom_call" | custom-call | tf_op jit(solution)/shard_map/pallas_call | solution.py:25
Async XLA Ops:
  2.1 5.7 %collective-permute-start = (f32[176,128]{1,0:T(8,128)S(1)}, f32[176,128]{1,0:T(8,128)S(1)}, u32[]{:S(2)}, u32[]{:S(2)}) collective-permute-start(f32[176,128]{1,0:T(8,128)S(1)} %get-tuple-element.26), channel_id=1, source_target_pairs={{0,1},{1,0},{2,3},{3,2},{4,5},{5,4},{6,7},{7,6},{8,9},{9,8},{10,11... | collective-permute-start | bytes 270344 | tf_op jit(solution)/shard_map/ppermute | solution.py:69
  5.2 2.6 %collective-permute-start.1 = (f32[176,128]{1,0:T(8,128)S(1)}, f32[176,128]{1,0:T(8,128)S(1)}, u32[]{:S(2)}, u32[]{:S(2)}) collective-permute-start(f32[176,128]{1,0:T(8,128)S(1)} %get-tuple-element.27), channel_id=1, source_target_pairs={{1,2},{2,1},{5,6},{6,5},{9,10},{10,9},{13,14},{14,13},{17,18},{18,... | collective-permute-start | bytes 270344 | tf_op jit(solution)/shard_map/ppermute | solution.py:69
  8.0 28.3 %collective-permute-start.4 = (f32[592,128]{1,0:T(8,128)S(1)}, f32[592,128]{1,0:T(8,128)S(1)}, u32[]{:S(2)}, u32[]{:S(2)}) collective-permute-start(f32[592,128]{1,0:T(8,128)S(1)} %get-tuple-element.36), channel_id=1, source_target_pairs={{0,4},{4,0},{8,12},{12,8},{16,20},{20,16},{24,28},{28,24},{1,5},{5... | collective-permute-start | bytes 909320 | tf_op jit(solution)/shard_map/ppermute | solution.py:69
  8.1 28.2 %collective-permute-start.5 = (f32[592,128]{1,0:T(8,128)S(1)}, f32[592,128]{1,0:T(8,128)S(1)}, u32[]{:S(2)}, u32[]{:S(2)}) collective-permute-start(f32[592,128]{1,0:T(8,128)S(1)} %get-tuple-element.37), channel_id=1, source_target_pairs={{4,8},{8,4},{12,16},{16,12},{20,24},{24,20},{5,9},{9,5},{13,17},{1... | collective-permute-start | bytes 909320 | tf_op jit(solution)/shard_map/ppermute | solution.py:69
  8.8 27.5 %collective-permute-start.3 = (f32[336,128]{1,0:T(8,128)S(1)}, f32[336,128]{1,0:T(8,128)S(1)}, u32[]{:S(2)}, u32[]{:S(2)}) collective-permute-start(f32[336,128]{1,0:T(8,128)S(1)} %get-tuple-element.35), channel_id=1, source_target_pairs={{0,4},{4,8},{8,12},{12,16},{16,20},{20,24},{24,28},{1,5},{5,9},{9,... | collective-permute-start | bytes 516104 | tf_op jit(solution)/shard_map/ppermute | solution.py:532
  13.9 3.1 %collective-permute-start.2 = (f32[48,128]{1,0:T(8,128)S(1)}, f32[48,128]{1,0:T(8,128)S(1)}, u32[]{:S(2)}, u32[]{:S(2)}) collective-permute-start(f32[48,128]{1,0:T(8,128)S(1)} %get-tuple-element.25.padded), channel_id=1, source_target_pairs={{4,0},{8,4},{12,8},{16,12},{20,16},{24,20},{28,24},{5,1},{9,5},{13... | collective-permute-start | bytes 73736 | tf_op jit(solution)/shard_map/ppermute | solution.py:532
